TPU v7x, 512 devices: a whole 4x8x8 slice. The times are simulated.
512 devices in a mesh: gx: 32 (over z, x), gy: 16 (over y, core).
Axes of the slice: x: 4, y: 8, z: 8, core: 2. Of those that a mesh axis runs over, the one named last changes fastest.
Arguments:
- gap_load: float32 [32, 16, 384, 128], P('gx', 'gy'), may hold values from -6 to 6
- flexibility: bfloat16 [32, 16, 768, 768], P('gx', 'gy'), as said below
- schur_blocks: bfloat16 [32, 16, 768, 768], P('gx', 'gy'), as said below
- body_modes: float32 [32, 16, 3, 768], P('gx', 'gy'), may hold values from -6 to 6
- coarse_inverse: float32 [1536, 1536], P(('gx', 'gy')), as said below
- saved_search: float32 [32, 16, 16, 384], P('gx', 'gy'), may hold values from -6 to 6
- saved_images: float32 [32, 16, 16, 384], P('gx', 'gy'), may hold values from -0.0017089844 to 0.0017089844
- face_slots: int32 [32, 16, 4, 192], P('gx', 'gy'), may hold values from 0 to 767, as said below
- face_count: int32 [32, 16, 4], P('gx', 'gy'), may hold values from 0 to 192, as said below
- multiplicity: int32 [32, 16, 768], P('gx', 'gy'), may hold values from 1 to 3, as said below
Outputs:
- multipliers: float32 [32, 16, 384, 128], P('gx', 'gy')
- residual: float32 [32, 16, 384, 128], P('gx', 'gy')
Inputs may be any that keep to these rules, and one draw needn't show every extreme that they name: For k < face_count[a, b, d] the entries face_slots[a, b, d, k] are distinct slots of subdomain (a, b), except that faces that follow each other in the order up, right, down, left share one slot when both are not empty. Link k of the face between two neighbouring subdomains is entry k of both their lists (down of the upper one and up of the lower one, right of the left one and left of the right one). Entries with k >= face_count carry no meaning. face_count[a, b, 0] = face_count[a - 1, b, 1] and face_count[a, b, 2] = face_count[a, b - 1, 3]; faces on the grid's border have 0 links, inner faces between 96 and 192, and in every draw some face along each grid direction has exactly 192. multiplicity[a, b, i] is 1 plus the number of faces of (a, b) whose first face_count entries name slot i. `flexibility`: each block is symmetric. `schur_blocks`: each block is symmetric. `coarse_inverse`: Symmetric.
All inputs are finite; a program needn't handle non-finite values.
Results may differ from a plain program's by a relative error of at most 0.0015.
The roundings to bfloat16 on the way count: a program that leaves them out, or rounds other values in their place, can miss the bound.
Values sent between devices are 32-bit elements.
No kernel may reach another device: no remote copies, remote signals or barrier semaphores. Data moves between devices by JAX's collectives and lax.ppermute only.
A program may use at most 64 MiB of HBM per device.

v0:
```python
import functools

import jax
import jax.numpy as jnp
from jax import lax
from jax.sharding import Mesh
from jax.sharding import PartitionSpec as P

GX = ("gx_0", "gx_1")
GY = ("gy_0", "gy_1")
GX_GY = ("gx_0", "gx_1", "gy_0", "gy_1")


HIGHEST_MODE = lax.Precision.HIGHEST


def shifted(value, axis, steps):
    count = lax.axis_size(axis)
    initial, last = (max(0, -steps), min(count, count - steps))
    return lax.ppermute(value, axis, [(source, source + steps) for source in range(initial, last)])


def over_axes(x, axes):
    return functools.reduce(lax.psum, axes, x)


def place_parts(
    down_values, right_values, from_above, from_left, slot_table, face_valid, slot_total
):
    load_cases = down_values.shape[1]
    signed_parts = (
        jnp.stack([-from_above, down_values, -from_left, right_values], axis=0)
        * face_valid[:, :, None]
    )
    empty = jnp.zeros((slot_total, load_cases), jnp.float32)
    return empty.at[slot_table.reshape(-1)].add(signed_parts.reshape(-1, load_cases))


def place_full(full_links, slot_table, face_valid, slot_total):
    return place_parts(
        full_links[1],
        full_links[3],
        full_links[0],
        full_links[2],
        slot_table,
        face_valid,
        slot_total,
    )


def gain_copies(link_values, face_width):
    down_values = link_values[:face_width]
    right_values = link_values[face_width:]
    upper_copy = shifted(down_values, GX, 1)
    left_copy = shifted(right_values, GY, 1)
    return jnp.stack([upper_copy, down_values, left_copy, right_values], axis=0)


def own_links(full_links):
    return jnp.concatenate([full_links[1], full_links[3]], axis=0)


def jumps_full(slot_values, slot_table, face_valid):
    face_width = slot_table.shape[1]
    picked = jnp.take(slot_values, slot_table.reshape(-1), axis=0).reshape(
        4, face_width, slot_values.shape[1]
    )
    below_values = shifted(picked[0], GX, -1)
    right_values = shifted(picked[2], GY, -1)
    above_values = shifted(picked[1], GX, 1)
    left_values = shifted(picked[3], GY, 1)
    down_part = (picked[1] - below_values) * face_valid[1][:, None]
    right_part = (picked[3] - right_values) * face_valid[3][:, None]
    upper_part = (above_values - picked[0]) * face_valid[0][:, None]
    left_part = (left_values - picked[2]) * face_valid[2][:, None]
    return jnp.stack([upper_part, down_part, left_part, right_part], axis=0)


def late_dots(energy_part, intersect_part):
    return (over_axes(energy_part, GX_GY), over_axes(intersect_part, GX_GY))


def curvature_sum(curvature_part):
    return over_axes(curvature_part, GX_GY)


def per_device(
    gap_load,
    flexibility,
    schur_blocks,
    body_modes,
    coarse_inverse,
    saved_search,
    saved_images,
    face_slots,
    face_count,
    multiplicity,
):
    local_flex = flexibility[0, 0]
    local_schur = schur_blocks[0, 0]
    rigid_modes = body_modes[0, 0]
    slot_table = face_slots[0, 0]
    face_width = slot_table.shape[1]
    slot_total = rigid_modes.shape[1]
    face_valid = (jnp.arange(face_width)[None, :] < face_count[0, 0][:, None]).astype(jnp.float32)
    link_valid = jnp.concatenate([face_valid[1], face_valid[3]], axis=0)
    weights = 1.0 / multiplicity[0, 0].astype(jnp.float32)
    residual = gap_load[0, 0] * link_valid[:, None]
    kept_search = saved_search[0, 0] * link_valid[None, :]
    kept_images = saved_images[0, 0] * link_valid[None, :]
    residual_full = gain_copies(residual, face_width)
    search_full_kept = gain_copies(kept_search.T, face_width)
    weighted = (
        weights[:, None] * place_full(residual_full, slot_table, face_valid, slot_total)
    ).astype(jnp.bfloat16)
    smoothed = jnp.dot(local_schur, weighted, preferred_element_type=jnp.float32)
    precond_full = jumps_full(weights[:, None] * smoothed, slot_table, face_valid)
    precond = own_links(precond_full)
    energy_part = jnp.sum(own_links(residual_full) * precond, axis=0)
    coarse_in = jnp.dot(
        rigid_modes,
        place_full(precond_full, slot_table, face_valid, slot_total),
        precision=HIGHEST_MODE,
    )
    coarse_out = jnp.dot(
        coarse_inverse, lax.all_gather(coarse_in, GX_GY, axis=0, tiled=True), precision=HIGHEST_MODE
    )
    projected_full = precond_full - jumps_full(
        jnp.dot(rigid_modes.T, coarse_out, precision=HIGHEST_MODE), slot_table, face_valid
    )
    intersect_part = jnp.dot(kept_images, own_links(projected_full), precision=HIGHEST_MODE)
    energy, intersect = late_dots(energy_part, intersect_part)
    search_full = projected_full - jnp.einsum(
        "dfj,jc->dfc", search_full_kept, intersect, precision=HIGHEST_MODE
    )
    lifted = place_full(search_full, slot_table, face_valid, slot_total).astype(jnp.bfloat16)
    applied_full = jumps_full(
        jnp.dot(local_flex, lifted, preferred_element_type=jnp.float32), slot_table, face_valid
    )
    search = own_links(search_full)
    curvature = curvature_sum(jnp.sum(search * own_links(applied_full), axis=0))
    step_size = energy / curvature
    multipliers = step_size * search
    residual_full = residual_full - step_size * applied_full
    residual = own_links(residual_full)
    return (multipliers[None, None], residual[None, None])


def solution(mesh):
    split = Mesh(mesh.devices.reshape(8, 4, 8, 2), ("gx_0", "gx_1", "gy_0", "gy_1"))
    placed = (
        P(GX, GY, None, None),
        P(GX, GY, None, None),
        P(GX, GY, None, None),
        P(GX, GY, None, None),
        P(GX_GY, None),
        P(GX, GY, None, None),
        P(GX, GY, None, None),
        P(GX, GY, None, None),
        P(GX, GY, None),
        P(GX, GY, None),
    )
    return jax.shard_map(
        per_device,
        mesh=split,
        in_specs=placed,
        out_specs=(P(GX, GY, None, None), P(GX, GY, None, None)),
        check_vma=False,
    )
```

profile of v0, /device:TPU:1, one launch (start us, length us, event | category | flops | bytes accessed | tf_op | source)
XLA Modules:
  0.0 272.0 jit_solution(19171111291158714)
XLA Ops:
  0.6 0.8 fusion.39
  1.6 1.0 bitcast_multiply_fusion.3
  2.7 4.6 %collective-permute-start.1 = (f32[192,128]{1,0:T(8,128)S(1)}, f32[192,128]{1,0:T(8,128)S(1)}, u32[]{:S(2)}, u32[]{:S(2)}) collective-permute-start(f32[192,128]{1,0:T(8,128)S(1)} %get-tuple-element.54), channel_id=1, source_target_pairs={{0,1},{1,2},{2,3},{3,4},{4,5},{5,6},{6,7},{7,8},{8,9},{9,10},{10,1... | collective-permute-start | bytes 294920 | tf_op jit(solution)/shard_map/ppermute | solution.py:20
  7.3 3.1 %collective-permute-start = (f32[192,128]{1,0:T(8,128)S(1)}, f32[192,128]{1,0:T(8,128)S(1)}, u32[]{:S(2)}, u32[]{:S(2)}) collective-permute-start(f32[192,128]{1,0:T(8,128)S(1)} %get-tuple-element.51), channel_id=1, source_target_pairs={{0,16},{16,32},{32,48},{48,64},{64,80},{80,96},{96,112},{112,128},... | collective-permute-start | bytes 294920 | tf_op jit(solution)/shard_map/ppermute | solution.py:20
  10.5 0.8 reshape_squeeze.4
  11.2 0.8 reshape_squeeze.5
  12.1 0.7 divide_reduce_fusion
  12.9 0.5 copy-done.3
  13.5 0.2 bitcast_multiply_fusion.2
  13.6 6.6 %scatter_custom_fusion = f32[768,128]{1,0:T(8,128)S(1)} fusion(s32[768]{0:T(1024)S(1)} %fusion.40, f32[768,128]{1,0:T(8,128)S(1)} %bitcast_multiply_fusion.2, f32[]{:T(128)} %constant.2.clone.1), kind=kCustom, calls=%fused_computation.53 | custom fusion | flops 98304 | bytes 393220 | tf_op jit(solution)/shard_map/scatter-add | solution.py:36
  20.3 0.6 fusion
  20.9 0.2 copy.18
  21.1 1.6 gather_fusion
  22.7 0.2 broadcast_select_fusion.2
  22.9 2.8 %collective-permute-start.4 = (f32[192,128]{1,0:T(8,128)S(1)}, f32[192,128]{1,0:T(8,128)S(1)}, u32[]{:S(2)}, u32[]{:S(2)}) collective-permute-start(f32[192,128]{1,0:T(8,128)S(1)} %get-tuple-element.47), channel_id=1, source_target_pairs={{0,16},{16,32},{32,48},{48,64},{64,80},{80,96},{96,112},{112,128},... | collective-permute-start | bytes 294920 | tf_op jit(solution)/shard_map/ppermute | solution.py:20
  25.7 3.4 %collective-permute-start.5 = (f32[192,128]{1,0:T(8,128)S(1)}, f32[192,128]{1,0:T(8,128)S(1)}, u32[]{:S(2)}, u32[]{:S(2)}) collective-permute-start(f32[192,128]{1,0:T(8,128)S(1)} %get-tuple-element.49), channel_id=1, source_target_pairs={{0,1},{1,2},{2,3},{3,4},{4,5},{5,6},{6,7},{7,8},{8,9},{9,10},{10,1... | collective-permute-start | bytes 294920 | tf_op jit(solution)/shard_map/ppermute | solution.py:20
  29.2 1.3 collective-permute-start.2
  30.5 2.7 collective-permute-start.3
  33.2 1.3 collective-permute-done.2
  34.5 1.9 collective-permute-done.3
  36.4 0.8 negate_bitcast_fusion.1
  37.3 0.2 bitcast_multiply_fusion.1
  37.4 6.6 %scatter_custom_fusion.1 = f32[768,128]{1,0:T(8,128)S(1)} fusion(s32[768]{0:T(1024)S(1)} %fusion.40, f32[768,128]{1,0:T(8,128)S(1)} %bitcast_multiply_fusion.1, f32[]{:T(128)} %constant.2.clone.1), kind=kCustom, calls=%fused_computation.51 | custom fusion | flops 98304 | bytes 393220 | tf_op jit(solution)/shard_map/scatter-add | solution.py:36
  44.1 0.3 convolution_bitcast_fusion.2
  44.4 85.8 %all-gather = f32[512,3,128]{2,1,0:T(4,128)S(1)} all-gather(f32[1,3,128]{2,1,0:T(4,128)S(1)} %convolution_bitcast_fusion.2), channel_id=1, replica_groups=mesh['gx_0'=8,'gx_1'=4,'gy_0'=8,'gy_1'=2] {'gx_0','gx_1','gy_0','gy_1'}, dimensions={0}, use_global_device_ids=true | all-gather | bytes 787968 | tf_op jit(solution)/shard_map/all_gather | solution.py:126
  130.2 0.4 reshape.221
  130.5 1.3 fusion.49
  131.8 0.5 convolution_bitcast_fusion.1
  132.3 0.2 copy.19
  132.5 1.6 gather_fusion.1
  134.2 0.2 broadcast_select_fusion.1
  134.4 2.8 %collective-permute-start.6 = (f32[192,128]{1,0:T(8,128)S(1)}, f32[192,128]{1,0:T(8,128)S(1)}, u32[]{:S(2)}, u32[]{:S(2)}) collective-permute-start(f32[192,128]{1,0:T(8,128)S(1)} %get-tuple-element.39), channel_id=1, source_target_pairs={{0,16},{16,32},{32,48},{48,64},{64,80},{80,96},{96,112},{112,128},... | collective-permute-start | bytes 294920 | tf_op jit(solution)/shard_map/ppermute | solution.py:20
  137.2 1.3 collective-permute-start.7
  138.5 2.3 collective-permute-start.9
  140.9 3.2 %collective-permute-start.8 = (f32[192,128]{1,0:T(8,128)S(1)}, f32[192,128]{1,0:T(8,128)S(1)}, u32[]{:S(2)}, u32[]{:S(2)}) collective-permute-start(f32[192,128]{1,0:T(8,128)S(1)} %get-tuple-element.41), channel_id=1, source_target_pairs={{0,1},{1,2},{2,3},{3,4},{4,5},{5,6},{6,7},{7,8},{8,9},{9,10},{10,1... | collective-permute-start | bytes 294920 | tf_op jit(solution)/shard_map/ppermute | solution.py:20
  144.2 1.9 collective-permute-start.11
  146.1 4.0 %collective-permute-start.10 = (f32[192,16]{0,1:T(8,128)S(1)}, f32[192,16]{0,1:T(8,128)S(1)}, u32[]{:S(2)}, u32[]{:S(2)}) collective-permute-start(f32[192,16]{0,1:T(8,128)S(1)} %get-tuple-element.55), channel_id=1, source_target_pairs={{0,16},{16,32},{32,48},{48,64},{64,80},{80,96},{96,112},{112,128},... | collective-permute-start | bytes 36872 | tf_op jit(solution)/shard_map/ppermute | solution.py:20
  150.2 0.2 multiply_bitcast_fusion.5
  150.5 0.2 fusion.10
  150.7 14.6 %psum.88 = f32[16,128]{1,0:T(8,128)S(1)} all-reduce(f32[16,128]{1,0:T(8,128)S(1)} %fusion.10), channel_id=1, replica_groups=mesh['gx_0'=8,'gx_1'=4,'gy_0'=8,'gy_1'=2] {'gx_0'}, use_global_device_ids=true, to_apply=%region_7.9 | all-reduce | flops 2048 | bytes 16384 | tf_op jit(solution)/shard_map/psum | solution.py:24
  165.3 9.9 %psum.89 = f32[16,128]{1,0:T(8,128)S(1)} all-reduce(f32[16,128]{1,0:T(8,128)S(1)} %psum.88), channel_id=1, replica_groups=mesh['gx_0'=8,'gx_1'=4,'gy_0'=8,'gy_1'=2] {'gx_1'}, use_global_device_ids=true, to_apply=%region_8.10 | all-reduce | flops 2048 | bytes 16384 | tf_op jit(solution)/shard_map/psum | solution.py:24
  175.2 13.5 %psum.90 = f32[16,128]{1,0:T(8,128)S(1)} all-reduce(f32[16,128]{1,0:T(8,128)S(1)} %psum.89), channel_id=1, replica_groups=mesh['gx_0'=8,'gx_1'=4,'gy_0'=8,'gy_1'=2] {'gy_0'}, use_global_device_ids=true, to_apply=%region_9.11 | all-reduce | flops 2048 | bytes 16384 | tf_op jit(solution)/shard_map/psum | solution.py:24
  188.8 11.6 %psum.91 = f32[16,128]{1,0:T(8,128)S(1)} all-reduce(f32[16,128]{1,0:T(8,128)S(1)} %psum.90), channel_id=1, replica_groups=mesh['gx_0'=8,'gx_1'=4,'gy_0'=8,'gy_1'=2] {'gy_1'}, use_global_device_ids=true, to_apply=%region_10.12 | all-reduce | flops 2048 | bytes 16384 | tf_op jit(solution)/shard_map/psum | solution.py:24
  200.3 0.8 convolution_subtract_fusion
  201.2 0.8 slice_negate_fusion.1
  202.0 0.2 bitcast_multiply_fusion
  202.1 6.9 %scatter_custom_fusion.2 = f32[768,128]{1,0:T(8,128)S(1)} fusion(s32[768]{0:T(1024)} %copy-done.31, f32[768,128]{1,0:T(8,128)S(1)} %bitcast_multiply_fusion, f32[]{:T(128)} %constant.2.clone.1), kind=kCustom, calls=%fused_computation.49 | custom fusion | flops 98304 | bytes 393728 | tf_op jit(solution)/shard_map/scatter-add | solution.py:36
  209.0 0.5 convolution_bitcast_fusion
  209.6 0.2 copy.20
  209.7 1.6 gather_fusion.2
  211.4 0.2 broadcast_select_fusion
  211.6 1.4 collective-permute-start.14
  213.1 1.3 collective-permute-start.12
  214.4 2.5 collective-permute-start.13
  216.8 3.1 %collective-permute-start.15 = (f32[192,128]{1,0:T(8,128)S(1)}, f32[192,128]{1,0:T(8,128)S(1)}, u32[]{:S(2)}, u32[]{:S(2)}) collective-permute-start(f32[192,128]{1,0:T(8,128)S(1)} %get-tuple-element.23), channel_id=1, source_target_pairs={{0,1},{1,2},{2,3},{3,4},{4,5},{5,6},{6,7},{7,8},{8,9},{9,10},{10,1... | collective-permute-start | bytes 294920 | tf_op jit(solution)/shard_map/ppermute | solution.py:20
  220.1 0.2 collective-permute-done.13
  220.3 1.3 collective-permute-done.15
  221.6 0.2 multiply_bitcast_fusion.1
  221.9 16.9 %all-reduce.1 = (f32[128]{0:T(128)S(1)}, f32[128]{0:T(128)S(1)}) all-reduce(f32[128]{0:T(128)S(1)} %fusion.9, f32[128]{0:T(128)S(1)} %fusion.14), channel_id=1, replica_groups=mesh['gx_0'=8,'gx_1'=4,'gy_0'=8,'gy_1'=2] {'gx_0'}, use_global_device_ids=true, to_apply=%region_2.4 | all-reduce | flops 256 | bytes 2048 | tf_op jit(solution)/shard_map/psum | solution.py:24
  238.8 6.1 %all-reduce.2 = (f32[128]{0:T(128)S(1)}, f32[128]{0:T(128)S(1)}) all-reduce(f32[128]{0:T(128)S(1)} %get-tuple-element.5, f32[128]{0:T(128)S(1)} %get-tuple-element.6), channel_id=1, replica_groups=mesh['gx_0'=8,'gx_1'=4,'gy_0'=8,'gy_1'=2] {'gx_1'}, use_global_device_ids=true, to_apply=%region_3.5 | all-reduce | flops 256 | bytes 2048 | tf_op jit(solution)/shard_map/psum | solution.py:24
  244.9 12.2 %all-reduce = (f32[128]{0:T(128)S(1)}, f32[128]{0:T(128)S(1)}) all-reduce(f32[128]{0:T(128)S(1)} %get-tuple-element.7, f32[128]{0:T(128)S(1)} %get-tuple-element.8), channel_id=1, replica_groups=mesh['gx_0'=8,'gx_1'=4,'gy_0'=8,'gy_1'=2] {'gy_0'}, use_global_device_ids=true, to_apply=%region_4.6 | all-reduce | flops 256 | bytes 2048 | tf_op jit(solution)/shard_map/psum | solution.py:24
  257.1 13.4 %all-reduce.3 = (f32[128]{0:T(128)S(1)}, f32[128]{0:T(128)S(1)}) all-reduce(f32[128]{0:T(128)S(1)} %get-tuple-element.3, f32[128]{0:T(128)S(1)} %get-tuple-element.4), channel_id=1, replica_groups=mesh['gx_0'=8,'gx_1'=4,'gy_0'=8,'gy_1'=2] {'gy_1'}, use_global_device_ids=true, to_apply=%region_5.7 | all-reduce | flops 256 | bytes 2048 | tf_op jit(solution)/shard_map/psum | solution.py:24
  270.6 0.7 maximum_multiply_fusion.3
  271.3 0.7 maximum_bitcast_fusion
  (100 shorter events, 1.0 us)
Async XLA Ops:
  0.6 19.6 %copy-start = (bf16[1,1,768,768]{3,2,1,0:T(8,128)(2,1)S(1)}, bf16[1,1,768,768]{3,2,1,0:T(8,128)(2,1)}, u32[]{:S(2)}) copy-start(bf16[1,1,768,768]{3,2,1,0:T(8,128)(2,1)} %param.14) | copy-start | bytes 3538948
  1.5 34.9 %copy-start.17 = (f32[1,192]{1,0:T(1,128)}, f32[1,192]{1,0:T(1,128)S(1)}, u32[]{:S(2)}) copy-start(f32[1,192]{1,0:T(1,128)S(1)} %get-tuple-element.61) | copy-start | bytes 2308
  1.5 34.9 %copy-start.19 = (f32[1,192]{1,0:T(1,128)}, f32[1,192]{1,0:T(1,128)S(1)}, u32[]{:S(2)}) copy-start(f32[1,192]{1,0:T(1,128)S(1)} %get-tuple-element.62) | copy-start | bytes 2308
  1.5 34.9 %copy-start.25 = (f32[1,192]{1,0:T(1,128)}, f32[1,192]{1,0:T(1,128)S(1)}, u32[]{:S(2)}) copy-start(f32[1,192]{1,0:T(1,128)S(1)} %get-tuple-element.59) | copy-start | bytes 2308
  1.5 34.9 %copy-start.28 = (f32[1,192]{1,0:T(1,128)}, f32[1,192]{1,0:T(1,128)S(1)}, u32[]{:S(2)}) copy-start(f32[1,192]{1,0:T(1,128)S(1)} %get-tuple-element.60) | copy-start | bytes 2308
  1.6 148.9 %copy-start.15 = (f32[384]{0:T(512)}, f32[384]{0:T(512)S(1)}, u32[]{:S(2)}) copy-start(f32[384]{0:T(512)S(1)} %pad_maximum_fusion.9) | copy-start | bytes 4612
  2.7 10.1 %collective-permute-start.1 = (f32[192,128]{1,0:T(8,128)S(1)}, f32[192,128]{1,0:T(8,128)S(1)}, u32[]{:S(2)}, u32[]{:S(2)}) collective-permute-start(f32[192,128]{1,0:T(8,128)S(1)} %get-tuple-element.54), channel_id=1, source_target_pairs={{0,1},{1,2},{2,3},{3,4},{4,5},{5,6},{6,7},{7,8},{8,9},{9,10},{10,1... | collective-permute-start | bytes 294920 | tf_op jit(solution)/shard_map/ppermute | solution.py:20
  7.3 5.6 %collective-permute-start = (f32[192,128]{1,0:T(8,128)S(1)}, f32[192,128]{1,0:T(8,128)S(1)}, u32[]{:S(2)}, u32[]{:S(2)}) collective-permute-start(f32[192,128]{1,0:T(8,128)S(1)} %get-tuple-element.51), channel_id=1, source_target_pairs={{0,16},{16,32},{32,48},{48,64},{64,80},{80,96},{96,112},{112,128},... | collective-permute-start | bytes 294920 | tf_op jit(solution)/shard_map/ppermute | solution.py:20
  12.0 10.7 %copy-start.23 = (pred[768]{0:T(1024)(128)(4,1)}, pred[768]{0:T(1024)(128)(4,1)S(1)}, u32[]{:S(2)}) copy-start(pred[768]{0:T(1024)(128)(4,1)S(1)} %compare_and_fusion) | copy-start | bytes 2308
  12.0 25.4 %copy-start.31 = (s32[768]{0:T(1024)}, s32[768]{0:T(1024)S(1)}, u32[]{:S(2)}) copy-start(s32[768]{0:T(1024)S(1)} %fusion.40) | copy-start | bytes 9220
  12.8 119.7 %copy-start.13 = (s32[1024]{0:T(1024)}, s32[1024]{0:T(1024)S(1)}, u32[]{:S(2)}) copy-start(s32[1024]{0:T(1024)S(1)} %pad_clamp_fusion) | copy-start | bytes 12292
  12.8 0.6 copy-start.3
  12.8 0.6 copy-start.5
  22.7 10.5 %copy-start.22 = (f32[1,1,16,384]{3,2,1,0:T(8,128)S(1)}, f32[1,1,16,384]{3,2,1,0:T(8,128)}, u32[]{:S(2)}) copy-start(f32[1,1,16,384]{3,2,1,0:T(8,128)} %param.17) | copy-start | bytes 73732
  22.9 10.3 %collective-permute-start.4 = (f32[192,128]{1,0:T(8,128)S(1)}, f32[192,128]{1,0:T(8,128)S(1)}, u32[]{:S(2)}, u32[]{:S(2)}) collective-permute-start(f32[192,128]{1,0:T(8,128)S(1)} %get-tuple-element.47), channel_id=1, source_target_pairs={{0,16},{16,32},{32,48},{48,64},{64,80},{80,96},{96,112},{112,128},... | collective-permute-start | bytes 294920 | tf_op jit(solution)/shard_map/ppermute | solution.py:20
  25.7 7.5 %collective-permute-start.5 = (f32[192,128]{1,0:T(8,128)S(1)}, f32[192,128]{1,0:T(8,128)S(1)}, u32[]{:S(2)}, u32[]{:S(2)}) collective-permute-start(f32[192,128]{1,0:T(8,128)S(1)} %get-tuple-element.49), channel_id=1, source_target_pairs={{0,1},{1,2},{2,3},{3,4},{4,5},{5,6},{6,7},{7,8},{8,9},{9,10},{10,1... | collective-permute-start | bytes 294920 | tf_op jit(solution)/shard_map/ppermute | solution.py:20
  29.2 5.4 %collective-permute-start.2 = (f32[192,128]{1,0:T(8,128)S(1)}, f32[192,128]{1,0:T(8,128)S(1)}, u32[]{:S(2)}, u32[]{:S(2)}) collective-permute-start(f32[192,128]{1,0:T(8,128)S(1)} %get-tuple-element.50), channel_id=1, source_target_pairs={{16,0},{32,16},{48,32},{64,48},{80,64},{96,80},{112,96},{128,112},... | collective-permute-start | bytes 294920 | tf_op jit(solution)/shard_map/ppermute | solution.py:20
  30.5 5.9 %collective-permute-start.3 = (f32[192,128]{1,0:T(8,128)S(1)}, f32[192,128]{1,0:T(8,128)S(1)}, u32[]{:S(2)}, u32[]{:S(2)}) collective-permute-start(f32[192,128]{1,0:T(8,128)S(1)} %get-tuple-element.48), channel_id=1, source_target_pairs={{1,0},{2,1},{3,2},{4,3},{5,4},{6,5},{7,6},{8,7},{9,8},{10,9},{11,1... | collective-permute-start | bytes 294920 | tf_op jit(solution)/shard_map/ppermute | solution.py:20
  37.2 6.8 %copy-start.12 = (f32[1,1,3,768]{3,1,2,0:T(1,128)S(1)}, f32[1,1,3,768]{3,1,2,0:T(1,128)}, u32[]{:S(2)}) copy-start(f32[1,1,3,768]{3,1,2,0:T(1,128)} %param.15) | copy-start | bytes 27652
  132.5 1.6 copy-start.24
  134.1 16.0 %copy-start.18 = (f32[1,192]{1,0:T(1,128)S(1)}, f32[1,192]{1,0:T(1,128)}, u32[]{:S(2)}) copy-start(f32[1,192]{1,0:T(1,128)} %copy-done.17) | copy-start | bytes 2308
  134.1 16.0 %copy-start.20 = (f32[1,192]{1,0:T(1,128)S(1)}, f32[1,192]{1,0:T(1,128)}, u32[]{:S(2)}) copy-start(f32[1,192]{1,0:T(1,128)} %copy-done.19) | copy-start | bytes 2308
  134.1 16.0 %copy-start.26 = (f32[1,192]{1,0:T(1,128)S(1)}, f32[1,192]{1,0:T(1,128)}, u32[]{:S(2)}) copy-start(f32[1,192]{1,0:T(1,128)} %copy-done.25) | copy-start | bytes 2308
  134.1 16.0 %copy-start.29 = (f32[1,192]{1,0:T(1,128)S(1)}, f32[1,192]{1,0:T(1,128)}, u32[]{:S(2)}) copy-start(f32[1,192]{1,0:T(1,128)} %copy-done.28) | copy-start | bytes 2308
  134.3 16.0 %copy-start.11 = (f32[1,192,128]{2,1,0:T(8,128)S(1)}, f32[1,192,128]{2,1,0:T(8,128)}, u32[]{:S(2)}) copy-start(f32[1,192,128]{2,1,0:T(8,128)} %get-tuple-element.43) | copy-start | bytes 294916
  134.4 11.7 %collective-permute-start.6 = (f32[192,128]{1,0:T(8,128)S(1)}, f32[192,128]{1,0:T(8,128)S(1)}, u32[]{:S(2)}, u32[]{:S(2)}) collective-permute-start(f32[192,128]{1,0:T(8,128)S(1)} %get-tuple-element.39), channel_id=1, source_target_pairs={{0,16},{16,32},{32,48},{48,64},{64,80},{80,96},{96,112},{112,128},... | collective-permute-start | bytes 294920 | tf_op jit(solution)/shard_map/ppermute | solution.py:20
  137.2 12.9 %collective-permute-start.7 = (f32[192,128]{1,0:T(8,128)S(1)}, f32[192,128]{1,0:T(8,128)S(1)}, u32[]{:S(2)}, u32[]{:S(2)}) collective-permute-start(f32[192,128]{1,0:T(8,128)S(1)} %get-tuple-element.42), channel_id=1, source_target_pairs={{16,0},{32,16},{48,32},{64,48},{80,64},{96,80},{112,96},{128,112},... | collective-permute-start | bytes 294920 | tf_op jit(solution)/shard_map/ppermute | solution.py:20
  138.5 11.6 %collective-permute-start.9 = (f32[192,128]{1,0:T(8,128)S(1)}, f32[192,128]{1,0:T(8,128)S(1)}, u32[]{:S(2)}, u32[]{:S(2)}) collective-permute-start(f32[192,128]{1,0:T(8,128)S(1)} %get-tuple-element.40), channel_id=1, source_target_pairs={{1,0},{2,1},{3,2},{4,3},{5,4},{6,5},{7,6},{8,7},{9,8},{10,9},{11,1... | collective-permute-start | bytes 294920 | tf_op jit(solution)/shard_map/ppermute | solution.py:20
  140.9 9.3 %collective-permute-start.8 = (f32[192,128]{1,0:T(8,128)S(1)}, f32[192,128]{1,0:T(8,128)S(1)}, u32[]{:S(2)}, u32[]{:S(2)}) collective-permute-start(f32[192,128]{1,0:T(8,128)S(1)} %get-tuple-element.41), channel_id=1, source_target_pairs={{0,1},{1,2},{2,3},{3,4},{4,5},{5,6},{6,7},{7,8},{8,9},{9,10},{10,1... | collective-permute-start | bytes 294920 | tf_op jit(solution)/shard_map/ppermute | solution.py:20
  144.2 56.1 %collective-permute-start.11 = (f32[192,16]{0,1:T(8,128)S(1)}, f32[192,16]{0,1:T(8,128)S(1)}, u32[]{:S(2)}, u32[]{:S(2)}) collective-permute-start(f32[192,16]{0,1:T(8,128)S(1)} %get-tuple-element.58), channel_id=1, source_target_pairs={{0,1},{1,2},{2,3},{3,4},{4,5},{5,6},{6,7},{7,8},{8,9},{9,10},{10,1... | collective-permute-start | bytes 36872 | tf_op jit(solution)/shard_map/ppermute | solution.py:20
  146.1 4.4 %copy-start.21 = (f32[1,1,16,384]{3,2,1,0:T(8,128)S(1)}, f32[1,1,16,384]{3,2,1,0:T(8,128)}, u32[]{:S(2)}) copy-start(f32[1,1,16,384]{3,2,1,0:T(8,128)} %param.18) | copy-start | bytes 73732
  146.1 54.2 %collective-permute-start.10 = (f32[192,16]{0,1:T(8,128)S(1)}, f32[192,16]{0,1:T(8,128)S(1)}, u32[]{:S(2)}, u32[]{:S(2)}) collective-permute-start(f32[192,16]{0,1:T(8,128)S(1)} %get-tuple-element.55), channel_id=1, source_target_pairs={{0,16},{16,32},{32,48},{48,64},{64,80},{80,96},{96,112},{112,128},... | collective-permute-start | bytes 36872 | tf_op jit(solution)/shard_map/ppermute | solution.py:20
  201.9 7.1 %copy-start.1 = (bf16[1,1,768,768]{3,2,1,0:T(8,128)(2,1)S(1)}, bf16[1,1,768,768]{3,2,1,0:T(8,128)(2,1)}, u32[]{:S(2)}) copy-start(bf16[1,1,768,768]{3,2,1,0:T(8,128)(2,1)} %param.13) | copy-start | bytes 3538948
  209.0 0.7 copy-start.14
  211.3 8.6 %copy-start.2 = (f32[1,1,384,128]{3,2,1,0:T(8,128)S(1)}, f32[1,1,384,128]{3,2,1,0:T(8,128)}, u32[]{:S(2)}) copy-start(f32[1,1,384,128]{3,2,1,0:T(8,128)} %param.12) | copy-start | bytes 589828
  211.3 8.6 %copy-start.16 = (f32[384]{0:T(512)S(1)}, f32[384]{0:T(512)}, u32[]{:S(2)}) copy-start(f32[384]{0:T(512)} %copy-done.15) | copy-start | bytes 4612
  211.4 10.2 %copy-start.27 = (f32[1,192]{1,0:T(1,128)S(1)}, f32[1,192]{1,0:T(1,128)}, u32[]{:S(2)}) copy-start(f32[1,192]{1,0:T(1,128)} %copy-done.25) | copy-start | bytes 2308
  211.4 10.2 %copy-start.30 = (f32[1,192]{1,0:T(1,128)S(1)}, f32[1,192]{1,0:T(1,128)}, u32[]{:S(2)}) copy-start(f32[1,192]{1,0:T(1,128)} %copy-done.28) | copy-start | bytes 2308
  211.5 10.2 %copy-start.9 = (f32[192,128]{1,0:T(8,128)S(1)}, f32[192,128]{1,0:T(8,128)}, u32[]{:S(2)}) copy-start(f32[192,128]{1,0:T(8,128)} %get-tuple-element.26) | copy-start | bytes 294916
  211.6 10.2 %copy-start.10 = (f32[192,128]{1,0:T(8,128)S(1)}, f32[192,128]{1,0:T(8,128)}, u32[]{:S(2)}) copy-start(f32[192,128]{1,0:T(8,128)} %get-tuple-element.28) | copy-start | bytes 294916
  211.6 58.9 %copy-start.4 = (f32[192,128]{1,0:T(8,128)S(1)}, f32[192,128]{1,0:T(8,128)}, u32[]{:S(2)}) copy-start(f32[192,128]{1,0:T(8,128)} %copy-done.3) | copy-start | bytes 294916
  211.6 58.9 %copy-start.6 = (f32[192,128]{1,0:T(8,128)S(1)}, f32[192,128]{1,0:T(8,128)}, u32[]{:S(2)}) copy-start(f32[192,128]{1,0:T(8,128)} %copy-done.5) | copy-start | bytes 294916
  211.6 8.5 %collective-permute-start.14 = (f32[192,128]{1,0:T(8,128)S(1)}, f32[192,128]{1,0:T(8,128)S(1)}, u32[]{:S(2)}, u32[]{:S(2)}) collective-permute-start(f32[192,128]{1,0:T(8,128)S(1)} %get-tuple-element.21), channel_id=1, source_target_pairs={{0,16},{16,32},{32,48},{48,64},{64,80},{80,96},{96,112},{112,128},... | collective-permute-start | bytes 294920 | tf_op jit(solution)/shard_map/ppermute | solution.py:20
  213.1 7.0 %collective-permute-start.12 = (f32[192,128]{1,0:T(8,128)S(1)}, f32[192,128]{1,0:T(8,128)S(1)}, u32[]{:S(2)}, u32[]{:S(2)}) collective-permute-start(f32[192,128]{1,0:T(8,128)S(1)} %get-tuple-element.24), channel_id=1, source_target_pairs={{16,0},{32,16},{48,32},{64,48},{80,64},{96,80},{112,96},{128,112},... | collective-permute-start | bytes 294920 | tf_op jit(solution)/shard_map/ppermute | solution.py:20
  214.4 5.9 %collective-permute-start.13 = (f32[192,128]{1,0:T(8,128)S(1)}, f32[192,128]{1,0:T(8,128)S(1)}, u32[]{:S(2)}, u32[]{:S(2)}) collective-permute-start(f32[192,128]{1,0:T(8,128)S(1)} %get-tuple-element.22), channel_id=1, source_target_pairs={{1,0},{2,1},{3,2},{4,3},{5,4},{6,5},{7,6},{8,7},{9,8},{10,9},{11,1... | collective-permute-start | bytes 294920 | tf_op jit(solution)/shard_map/ppermute | solution.py:20
  216.8 4.7 %collective-permute-start.15 = (f32[192,128]{1,0:T(8,128)S(1)}, f32[192,128]{1,0:T(8,128)S(1)}, u32[]{:S(2)}, u32[]{:S(2)}) collective-permute-start(f32[192,128]{1,0:T(8,128)S(1)} %get-tuple-element.23), channel_id=1, source_target_pairs={{0,1},{1,2},{2,3},{3,4},{4,5},{5,6},{6,7},{7,8},{8,9},{9,10},{10,1... | collective-permute-start | bytes 294920 | tf_op jit(solution)/shard_map/ppermute | solution.py:20
  221.7 48.9 %copy-start.7 = (f32[1,1,192,128]{3,2,1,0:T(8,128)S(1)}, f32[1,1,192,128]{3,2,1,0:T(8,128)}, u32[]{:S(2)}) copy-start(f32[1,1,192,128]{3,2,1,0:T(8,128)} %get-tuple-element.27) | copy-start | bytes 294916
  221.8 48.9 %copy-start.8 = (f32[1,1,192,128]{3,2,1,0:T(8,128)S(1)}, f32[1,1,192,128]{3,2,1,0:T(8,128)}, u32[]{:S(2)}) copy-start(f32[1,1,192,128]{3,2,1,0:T(8,128)} %get-tuple-element.29) | copy-start | bytes 294916
where the time goes:
time: 273 us; the launch traced here: 272 us
  blocking collectives  184 us (67%)
  starting transfers between devices  41.8 us (15%)
  other arithmetic  27.5 us (10%)
  local copies, waits for them, and re-layouts  8.11 us (3%)
  waiting for transfers between devices  4.66 us (2%)
  matrix products  4.32 us (2%)
    psum x8, blocking collectives, over_axes(): return functools.reduce(lax.psum, axes, x)  98.3 us
    all_gather x1, blocking collectives, per_device(): lax.all_gather(coarse_in, GX_GY, axis=0, tiled=True)  85.8 us
    ppermute x16, starting transfers between devices, shifted(): lax.ppermute(value, axis, [(source, source + steps) for source in range(i...  41.8 us
    scatter-add x3, other arithmetic, place_parts(): empty.at[slot_table.reshape(-1)].add(signed_parts.reshape(-1, load_cases))  20.1 us
  transfers between devices with their start and end apart: 16, of which 4 were waited for; matrix products, arithmetic and copies ran while one was open for 1% of the time, Pallas kernels for 0%

commit v1 on v0

v1 whole, which is shorter than its diff:
```python
import functools

import jax
import jax.numpy as jnp
import numpy as np
from jax import lax
from jax.experimental import pallas as pl
from jax.experimental.pallas import tpu as pltpu
from jax.sharding import Mesh
from jax.sharding import PartitionSpec as P

GX = ("gx_0", "gx_1")
GY = ("gy_0", "gy_1")
GX_GY = ("gx_0", "gx_1", "gy_0", "gy_1")

F32 = jnp.float32
BF16 = jnp.bfloat16
HIGHEST = lax.Precision.HIGHEST
SIGNS = (-1.0, 1.0, -1.0, 1.0)


def shifted(value, axis, steps):
    count = lax.axis_size(axis)
    initial, last = (max(0, -steps), min(count, count - steps))
    return lax.ppermute(value, axis, [(source, source + steps) for source in range(initial, last)])


def split3(x):
    high = x.astype(BF16)
    rest = x - high.astype(F32)
    mid = rest.astype(BF16)
    low = (rest - mid.astype(F32)).astype(BF16)
    return high, mid, low


def dot(a, b):
    return lax.dot_general(a, b, (((1,), (0,)), ((), ())), preferred_element_type=F32)


def dot_nt(a, b):
    return lax.dot_general(a, b, (((1,), (1,)), ((), ())), preferred_element_type=F32)


def dot_exact(a, b):
    return lax.dot_general(
        a, b, (((1,), (0,)), ((), ())), precision=HIGHEST, preferred_element_type=F32
    )


def select_rows(selection, x):
    width = x.shape[1]
    out = dot(selection, jnp.concatenate(split3(x), axis=1))
    return out[:, :width] + (out[:, width : 2 * width] + out[:, 2 * width :])


def select_lanes(x, selection):
    rows = x.shape[0]
    out = dot(jnp.concatenate(split3(x), axis=0), selection)
    return out[:rows] + (out[rows : 2 * rows] + out[2 * rows :])


def six_left(tiled):
    high, mid, low = split3(tiled)
    group = lax.broadcasted_iota(jnp.int32, tiled.shape, 1) // 16
    zero = jnp.zeros_like(tiled)
    is_high = (group == 0) | (group == 1) | (group == 3)
    is_mid = (group == 2) | (group == 4)
    out = jnp.where(
        is_high,
        high.astype(F32),
        jnp.where(is_mid, mid.astype(F32), jnp.where(group == 5, low.astype(F32), zero)),
    )
    return out.astype(BF16)


def six_right(x):
    high, mid, low = split3(x)
    zero = jnp.zeros_like(high)
    return jnp.concatenate([high, mid, high, low, mid, high, zero, zero], axis=0)


def tile_matrix():
    row = lax.broadcasted_iota(jnp.int32, (16, 128), 0)
    lane = lax.broadcasted_iota(jnp.int32, (16, 128), 1)
    return jnp.where(lane % 16 == row, 1.0, 0.0).astype(F32)


def widened(x, lanes):
    return jnp.concatenate([x, jnp.zeros((x.shape[0], lanes - x.shape[1]), x.dtype)], axis=1)


def lane_window(x, start, width):
    total = x.shape[1]
    if start:
        x = pltpu.roll(x, total - start, 1)
    return x[:, :width]


def at_lanes(x, start):
    return pltpu.roll(x, start, 1) if start else x


def prepare_kernel(
    windows, count, slots, mult, modes, schur, coarse,
    place, pick, pick_schur, mode_rows, mode_cols, columns, blocks, buffer, wide,
):
    width = slots.shape[1]
    total = 4 * width
    buffer[...] = jnp.zeros_like(buffer)
    buffer[0:4, 0:width] = slots[...].astype(F32)
    raw = buffer[...]
    lane = lax.broadcasted_iota(jnp.int32, (1, total), 1)
    slot_row = jnp.zeros((1, total), F32)
    sign_row = jnp.zeros((1, total), F32)
    for f in range(4):
        inside = (lane >= width * f) & (lane < width * f + count[f])
        slot_row = jnp.where(inside, at_lanes(raw, width * f)[f : f + 1], slot_row)
        sign_row = jnp.where(inside, SIGNS[f], sign_row)
    weights = 1.0 / mult[...].astype(F32)
    buffer[...] = jnp.zeros_like(buffer)
    buffer[0:1, :] = slot_row
    buffer[1:2, :] = sign_row
    buffer[2:3, :] = weights
    cols = jnp.transpose(buffer[...])
    columns[...] = cols
    down = lax.broadcasted_iota(jnp.int32, (total, total), 0).astype(F32)
    place_value = jnp.where(down == slot_row, sign_row, 0.0).astype(BF16)
    place[...] = place_value
    across = lax.broadcasted_iota(jnp.int32, (total, total), 1).astype(F32)
    pick_value = jnp.where(across == cols[:, 0:1], cols[:, 1:2], 0.0).astype(BF16)
    pick[...] = pick_value
    buffer[...] = jnp.zeros_like(buffer)
    buffer[0:3, :] = modes[...]
    buffer[3:4, :] = weights
    rows = select_lanes(buffer[...], place_value)
    mode_rows[...] = rows
    mode_cols[...] = jnp.transpose(rows)
    pick_schur[...] = dot(pick_value, schur[...]).astype(BF16)
    wide[...] = jnp.zeros_like(wide)
    wide[0:3, :] = coarse[...]
    for i, start in enumerate(windows):
        blocks[8 * i : 8 * i + 8, :] = wide[:, start : start + blocks.shape[1]]


def precond_kernel(
    gap, above, left, place, pick_schur, columns, mode_rows, mode_cols, saved,
    up_msg, down_msg, left_msg, right_msg, own,
):
    width = above.shape[0]
    links = jnp.concatenate([above[...], gap[0:width], left[...], gap[width:]], axis=0)
    spread = select_rows(place[...], links)
    weighted = (columns[:, 2:3] * spread).astype(BF16)
    picked = jnp.abs(mode_cols[:, 3:4]) * dot(pick_schur[...], weighted)
    own[...] = picked
    for f, msg in enumerate((up_msg, down_msg, left_msg, right_msg)):
        msg[0:width, :] = picked[width * f : width * f + width]
        rows = lane_window(mode_rows[...], width * f, 256)
        msg[width : width + 8, :] = rows[:, 0:128]
        msg[width + 8 : width + 16, :] = rows[:, 128:256]
    for start, msg in ((0, down_msg), (width, right_msg)):
        rows = lane_window(saved[...], start, 256)
        msg[width + 16 : width + 32, :] = rows[:, 0:128]
        msg[width + 32 : width + 48, :] = rows[:, 128:256]


def flex_kernel(pick, place, flex, pick_flex, link_flex):
    rows = dot(pick[...], flex[...]).astype(BF16)
    pick_flex[...] = rows
    link_flex[...] = dot(rows, place[...]).astype(BF16)


def coarse_in_kernel(own, above, below, left, right, mode_rows, precond, coarse):
    width = own.shape[0] // 4
    full = own[...] + jnp.concatenate(
        [above[0:width], below[0:width], left[0:width], right[0:width]], axis=0
    )
    precond[...] = full
    rows = dot_exact(mode_rows[...], full)
    rows = jnp.where(lax.broadcasted_iota(jnp.int32, rows.shape, 0) < 3, rows, 0.0)
    for i in range(coarse.shape[0] // 8):
        coarse[8 * i : 8 * i + 8, :] = rows


def tables_kernel(
    count, offset, above, below, left, right, mode_rows, saved, images, link_flex, gap, precond,
    blocks, wanted,
    mode_six, search_six, forms, sums, coarse_rows,
):
    total = mode_rows.shape[1]
    width = total // 4
    tiles = tile_matrix()
    lane = lax.broadcasted_iota(jnp.int32, (1, 256), 1)
    row = lax.broadcasted_iota(jnp.int32, (16, total), 0)
    mine = jnp.concatenate([mode_rows[...], jnp.zeros((8, total), F32)], axis=0)
    modes = jnp.where(row < 3, mine, 0.0)
    for f, msg in enumerate((above, below, left, right)):
        theirs = jnp.concatenate([msg[width : width + 8], msg[width + 8 : width + 16]], axis=1)
        theirs = jnp.where(lane < count[f], theirs, 0.0)
        theirs = at_lanes(widened(theirs, total), width * f)
        theirs = jnp.concatenate([theirs, jnp.zeros((8, total), F32)], axis=0)
        theirs = jnp.where(row < 3, theirs, 0.0)
        modes = modes + pltpu.roll(theirs, 3 * (1 + f), 0)
    mode_six[...] = six_left(
        lax.dot_general(modes, tiles, (((0,), (0,)), ((), ())), precision=HIGHEST, preferred_element_type=F32)
    )
    search = jnp.zeros((16, total), F32)
    for f in range(4):
        if f % 2 == 0:
            msg = above if f == 0 else left
            piece = jnp.concatenate(
                [msg[width + 16 : width + 32], msg[width + 32 : width + 48]], axis=1
            )
        else:
            piece = lane_window(saved[...], 0 if f == 1 else width, 256)
        piece = jnp.where(lane < count[f], piece, 0.0)
        search = search + at_lanes(widened(piece, total), width * f)
    search_tiled = lax.dot_general(
        search, tiles, (((0,), (0,)), ((), ())), precision=HIGHEST, preferred_element_type=F32
    )
    search_six[...] = six_left(search_tiled)
    flex_search = select_lanes(search, link_flex[...])
    lanes = lax.broadcasted_iota(jnp.int32, (16, total), 1)
    image = widened(images[...], total)
    image_down = at_lanes(image, width)
    image_right = at_lanes(image, 2 * width)
    forms[0:16, :] = jnp.where(
        (lanes >= width) & (lanes < 2 * width),
        image_down,
        jnp.where(lanes >= 3 * width, image_right, 0.0),
    )
    forms[16:32, :] = flex_search
    products = dot_exact(flex_search, search_tiled)
    group = lax.broadcasted_iota(jnp.int32, (16, 128), 1) // 16
    part = lax.broadcasted_iota(jnp.int32, (16, 128), 0)
    products = jnp.where(group == part % 8, products, 0.0)
    energy = jnp.sum(gap[0:width] * precond[width : 2 * width], axis=0, keepdims=True) + jnp.sum(
        gap[width:] * precond[3 * width :], axis=0, keepdims=True
    )
    sums[...] = jnp.concatenate(
        [
            energy,
            jnp.zeros((1, 128), F32),
            jnp.sum(products[0:8], axis=0, keepdims=True),
            jnp.sum(products[8:16], axis=0, keepdims=True),
            jnp.zeros((4, 128), F32),
        ],
        axis=0,
    )
    at = lax.broadcasted_iota(jnp.int32, (wanted.shape[0], blocks.shape[1]), 1)
    chosen = jnp.where(at == wanted[:, 0:1] + offset[0], 1.0, 0.0).astype(BF16)
    high, mid, low = split3(blocks[...])
    coarse_rows[...] = dot_nt(chosen, high) + (dot_nt(chosen, mid) + dot_nt(chosen, low))


def coarse_kernel(coarse_rows, gathered, parts):
    parts[...] = dot_exact(coarse_rows[...], gathered[...])


def project_kernel(arrived, precond, mode_six, forms, sums, link_flex, projected, partial):
    amplitudes = arrived[0:16]
    for j in range(1, arrived.shape[0] // 16):
        amplitudes = amplitudes + arrived[16 * j : 16 * j + 16]
    links = precond[...] - dot(mode_six[...], six_right(amplitudes))
    projected[...] = links
    linear = dot_exact(forms[...], links)
    high, mid, _ = split3(links)
    image = dot(link_flex[...], jnp.concatenate([high, mid], axis=1))
    square = jnp.sum(links * (image[:, :128] + image[:, 128:]), axis=0, keepdims=True)
    row = lax.broadcasted_iota(jnp.int32, (8, 128), 0)
    last = jnp.where(row == 1, square, sums[...])
    for j in range(partial.shape[0] // 40):
        partial[40 * j : 40 * j + 32, :] = linear
        partial[40 * j + 32 : 40 * j + 40, :] = last


def block_sum(ref, height):
    out = ref[0:height]
    for j in range(1, ref.shape[0] // height):
        out = out + ref[height * j : height * j + height]
    return out


def spread_sum_kernel(arrived, partial):
    out = block_sum(arrived, 40)
    for i in range(partial.shape[0] // 40):
        partial[40 * i : 40 * i + 40, :] = out


def search_kernel(
    arrived, projected, search_six, place, pick_flex,
    up_msg, left_msg, own, multipliers, step,
):
    width = up_msg.shape[0]
    sums = block_sum(arrived, 40)
    intersect = sums[0:16]
    cross = sums[16:32]
    energy = sums[32:33]
    square = sums[33:34]
    group = lax.broadcasted_iota(jnp.int32, (16, 128), 1) // 16
    part = lax.broadcasted_iota(jnp.int32, (16, 128), 0)
    packed = jnp.where(part < 8, sums[34:35], sums[35:36])
    packed = jnp.where(group == part % 8, packed, 0.0)
    products = dot_exact(packed, jnp.concatenate([intersect] * 8, axis=0))
    curvature = square + jnp.sum(intersect * (products - 2.0 * cross), axis=0, keepdims=True)
    size = energy / curvature
    step[...] = jnp.broadcast_to(size, step.shape)
    search = projected[...] - dot(search_six[...], six_right(intersect))
    multipliers[0:width, :] = size * search[width : 2 * width]
    multipliers[width:, :] = size * search[3 * width :]
    lifted = select_rows(place[...], search).astype(BF16)
    image = dot(pick_flex[...], lifted)
    up_msg[...] = image[0:width]
    own[0:width, :] = image[width : 2 * width]
    left_msg[...] = image[2 * width : 3 * width]
    own[width:, :] = image[3 * width :]


def residual_kernel(count, gap, own, below, right, step, residual):
    width = below.shape[0]
    row = lax.broadcasted_iota(jnp.int32, below.shape, 0)
    size = step[0:1]
    residual[0:width, :] = jnp.where(
        row < count[1], gap[0:width] - size * (own[0:width] + below[...]), 0.0
    )
    residual[width:, :] = jnp.where(
        row < count[3], gap[width:] - size * (own[width:] + right[...]), 0.0
    )


VMEM_LIMIT = 24 * 1024 * 1024
VMEM = pl.BlockSpec(memory_space=pltpu.VMEM)
SMEM = pl.BlockSpec(memory_space=pltpu.SMEM)


def call(kernel, inputs, outputs, scalars=0, scratch=(), flops=0, name=None):
    outputs = tuple(jax.ShapeDtypeStruct(shape, dtype) for shape, dtype in outputs)
    return pl.pallas_call(
        kernel,
        out_shape=outputs,
        in_specs=[SMEM] * scalars + [VMEM] * (len(inputs) - scalars),
        out_specs=tuple(VMEM for _ in outputs),
        scratch_shapes=[pltpu.VMEM(shape, dtype) for shape, dtype in scratch],
        cost_estimate=pl.CostEstimate(flops=flops, transcendentals=0, bytes_accessed=0),
        compiler_params=pltpu.CompilerParams(vmem_limit_bytes=VMEM_LIMIT),
        name=name,
    )(*inputs)


def wanted_rows(columns, modes):
    table = np.full((columns * 16, 128), -(1 << 20), np.int32)
    for j in range(columns):
        for s, (down, right) in enumerate(((0, 0), (-1, 0), (1, 0), (0, -1), (0, 1))):
            if 0 <= j + right < columns:
                for k in range(modes):
                    table[16 * j + modes * s + k] = ((down + 1) * columns + j + right) * modes + k
    return table


def per_device(
    gap_load, flexibility, schur_blocks, body_modes, coarse_inverse,
    saved_search, saved_images, face_slots, face_count, multiplicity,
):
    rows = lax.axis_size(GX)
    columns = lax.axis_size(GY)
    gap = gap_load[0, 0]
    flex = flexibility[0, 0]
    modes = body_modes[0, 0]
    saved = saved_search[0, 0]
    images = saved_images[0, 0]
    slots = face_slots[0, 0]
    count = face_count[0, 0]
    width = slots.shape[1]
    total = 4 * width
    cases = gap.shape[1]
    unknowns = coarse_inverse.shape[1]
    row_unknowns = columns * modes.shape[0]
    window = min(unknowns, 384)
    windows = [
        min(max((row_unknowns * (i - 1)) // 128, 0), (unknowns - window) // 128) * 128
        for i in range(rows)
    ]
    here = lax.axis_index(GX)
    offsets = jnp.asarray([row_unknowns * (i - 1) - windows[i] for i in range(rows)], jnp.int32)
    offset = lax.dynamic_slice(offsets, (here,), (1,))

    above = shifted(gap[:width], GX, 1)
    left = shifted(gap[width:], GY, 1)
    big = (total, total)
    cube = 2 * total**3
    place, pick, pick_schur, mode_rows, mode_cols, slot_cols, blocks = call(
        functools.partial(prepare_kernel, windows),
        (count, slots, multiplicity[0], modes, schur_blocks[0, 0], coarse_inverse),
        (
            (big, BF16), (big, BF16), (big, BF16), ((8, total), F32), ((total, 8), F32),
            ((total, 8), F32), ((8 * rows, window), F32),
        ),
        scalars=1,
        scratch=(((8, total), F32), ((8, unknowns), F32)),
        flops=cube,
        name="prepare",
    )
    blocks = lax.all_to_all(blocks, GX, 0, 0, tiled=True)
    up_msg, down_msg, left_msg, right_msg, own = call(
        precond_kernel,
        (gap, above, left, place, pick_schur, slot_cols, mode_rows, mode_cols, saved),
        tuple(((width + extra, cases), F32) for extra in (16, 48, 16, 48)) + (((total, cases), F32),),
        flops=cube // 2,
        name="precond",
    )
    from_above = shifted(down_msg, GX, 1)
    from_below = shifted(up_msg, GX, -1)
    from_left = shifted(right_msg, GY, 1)
    from_right = shifted(left_msg, GY, -1)
    pick_flex, link_flex = call(
        flex_kernel, (pick, place, flex), ((big, BF16), (big, BF16)), flops=2 * cube, name="flex"
    )
    precond, coarse_in = call(
        coarse_in_kernel,
        (own, from_above, from_below, from_left, from_right, mode_rows),
        (((total, cases), F32), ((8 * rows, cases), F32)),
        flops=cube // 16,
        name="coarse_in",
    )
    gathered = lax.all_to_all(coarse_in, GX, 0, 0, tiled=True)
    mode_six, search_six, forms, sums, coarse_rows = call(
        tables_kernel,
        (
            count, offset, from_above, from_below, from_left, from_right, mode_rows, saved, images,
            link_flex, gap, precond, blocks, jnp.asarray(wanted_rows(columns, modes.shape[0])),
        ),
        (
            ((total, 128), BF16), ((total, 128), BF16), ((32, total), F32), ((8, cases), F32),
            ((16 * columns, 8 * rows), F32),
        ),
        scalars=2,
        flops=cube,
        name="tables",
    )
    (parts,) = call(
        coarse_kernel, (coarse_rows, gathered), (((16 * columns, cases), F32),), flops=cube // 8,
        name="coarse",
    )
    parts = lax.all_to_all(parts, GY, 0, 0, tiled=True)
    projected, partial = call(
        project_kernel,
        (parts, precond, mode_six, forms, sums, link_flex),
        (((total, cases), F32), ((40 * columns, cases), F32)),
        flops=cube // 2,
        name="project",
    )
    partial = lax.all_to_all(partial, GY, 0, 0, tiled=True)
    (partial,) = call(
        spread_sum_kernel, (partial,), (((40 * rows, cases), F32),), flops=cube // 16, name="spread_sum"
    )
    partial = lax.all_to_all(partial, GX, 0, 0, tiled=True)
    up_msg, left_msg, own, multipliers, step = call(
        search_kernel,
        (partial, projected, search_six, place, pick_flex),
        (
            ((width, cases), F32), ((width, cases), F32), ((2 * width, cases), F32),
            ((2 * width, cases), F32), ((8, cases), F32),
        ),
        flops=cube // 2,
        name="search",
    )
    from_below = shifted(up_msg, GX, -1)
    from_right = shifted(left_msg, GY, -1)
    (residual,) = call(
        residual_kernel,
        (count, gap, own, from_below, from_right, step),
        (((2 * width, cases), F32),),
        scalars=1,
        flops=cube // 64,
        name="residual",
    )
    return (multipliers[None, None], residual[None, None])


def split_shape(mesh):
    rows, columns = (mesh.devices.shape[0], mesh.devices.shape[1])
    inner = 4 if rows % 4 == 0 and rows > 4 else 2
    return (rows // inner, inner, columns // 2, 2)


def solution(mesh):
    split = Mesh(mesh.devices.reshape(split_shape(mesh)), GX_GY)
    placed = (
        P(GX, GY, None, None),
        P(GX, GY, None, None),
        P(GX, GY, None, None),
        P(GX, GY, None, None),
        P(GX_GY, None),
        P(GX, GY, None, None),
        P(GX, GY, None, None),
        P(GX, GY, None, None),
        P(GX, GY, None),
        P(GX, GY, None),
    )
    return jax.shard_map(
        per_device,
        mesh=split,
        in_specs=placed,
        out_specs=(P(GX, GY, None, None), P(GX, GY, None, None)),
        check_vma=False,
    )
```

time: 273 us -> 158 us (0.58)
  blocking collectives: 184 us -> 60.9 us
  other arithmetic: 27.5 us -> 0 us
  Pallas kernels: 0 us -> 16.2 us
  starting transfers between devices: 41.8 us -> 51.7 us
  local copies, waits for them, and re-layouts: 8.11 us -> 17.1 us
  matrix products: 4.32 us -> 0 us
  waiting for transfers between devices: 4.66 us -> 8.37 us
    psum x8 -> x0, blocking collectives: 98.3 us -> none  [over_axes(): return functools.reduce(lax.psum, axes, x)]
    all_gather x1 -> x0, blocking collectives: 85.8 us -> none  [per_device(): lax.all_gather(coarse_in, GX_GY, axis=0, tiled=True)]
    all_to_all x0 -> x3, blocking collectives: none -> 60.9 us  [the longest x1 29.1 us: per_device(): partial = lax.all_to_all(partial, GX, 0, 0, tiled=True)]
    all_to_all x0 -> x2, starting transfers between devices: none -> 29 us  [the longest x1 15 us: per_device(): gathered = lax.all_to_all(coarse_in, GX, 0, 0, tiled=True)]
    scatter-add x3 -> x0, other arithmetic: 20.1 us -> none  [place_parts(): empty.at[slot_table.reshape(-1)].add(signed_parts.reshape(-1, load_cases))]
    ppermute x16 -> x8, starting transfers between devices: 41.8 us -> 22.7 us  [shifted(): lax.ppermute(value, axis, [(source, source + steps) for source in range(i...]
    pallas_call x0 -> x10, Pallas kernels: none -> 16.2 us  [call(): pl.pallas_call(kernel, out_shape=outputs, in_specs=[SMEM] * scalars + [VM...]
    unnamed x65 -> x69, local copies, waits for them, and re-layouts: 1.08 us -> 16.5 us
  transfers between devices with their start and end apart: 16 -> 10, of which waited for: 4 -> 5; matrix products, arithmetic and copies ran while one was open for 1% -> 0% of each run, Pallas kernels for 0% -> 6%
where the time goes in v1:
time: 158 us; the launch traced here: 155 us
  blocking collectives  60.9 us (39%)
  starting transfers between devices  51.7 us (33%)
  local copies, waits for them, and re-layouts  17.1 us (11%)
  Pallas kernels  16.2 us (10%)
  waiting for transfers between devices  8.37 us (5%)
    all_to_all x1, blocking collectives, per_device(): partial = lax.all_to_all(partial, GX, 0, 0, tiled=True)  29.1 us
    ppermute x8, starting transfers between devices, shifted(): lax.ppermute(value, axis, [(source, source + steps) for source in range(i...  22.7 us
    unnamed x69, local copies, waits for them, and re-layouts  16.5 us
    pallas_call x10, Pallas kernels, call(): pl.pallas_call(kernel, out_shape=outputs, in_specs=[SMEM] * scalars + [VM...  16.2 us
    all_to_all x1, blocking collectives, per_device(): parts = lax.all_to_all(parts, GY, 0, 0, tiled=True)  16.1 us
    all_to_all x1, blocking collectives, per_device(): partial = lax.all_to_all(partial, GY, 0, 0, tiled=True)  15.6 us
    all_to_all x1, starting transfers between devices, per_device(): gathered = lax.all_to_all(coarse_in, GX, 0, 0, tiled=True)  15 us
    all_to_all x1, starting transfers between devices, per_device(): blocks = lax.all_to_all(blocks, GX, 0, 0, tiled=True)  13.9 us
  transfers between devices with their start and end apart: 10, of which 5 were waited for; matrix products, arithmetic and copies ran while one was open for 0% of the time, Pallas kernels for 6%

profile of v1, /device:TPU:1, one launch (start us, length us, event | category | flops | bytes accessed | tf_op | source)
XLA Modules:
  0.0 155.3 jit_solution(17029415979028642876)
XLA Ops:
  0.6 0.7 copy.16
  1.3 0.7 copy-done.22
  2.0 1.3 copy-done.24
  3.3 0.7 copy-done.26
  4.0 0.7 copy-done.28
  4.7 0.7 copy-done.29
  5.4 2.2 %prepare.1 = (bf16[768,768]{1,0:T(8,128)(2,1)S(1)}, bf16[768,768]{1,0:T(8,128)(2,1)S(1)}, bf16[768,768]{1,0:T(8,128)(2,1)S(1)}, f32[8,768]{1,0:T(8,128)S(1)}, f3...) custom-call(s32[4]{0:T(128)S(1)} %bitcast.41, s32[4,192]{1,0:T(4,128)S(1)} %bitcast.47, ...), custom_call_target="tpu_custom_call" | custom-call | flops 905969664 | tf_op jit(solution)/shard_map/prepare/pallas_call | solution.py:337
  7.5 0.0 copy-start.3
  7.5 0.7 copy-done.3
  8.3 1.1 copy-done.31
  9.4 13.9 %all-to-all-start = ((f32[32,8,384]{2,1,0:T(8,128)}), f32[32,8,384]{2,1,0:T(8,128)}, u32[]{:S(2)}, u32[]{:S(2)}) async-start(f32[32,8,384]{2,1,0:T(8,128)} %bitcast.36), calls=%async_computation | async-start | bytes 786432 | tf_op jit(solution)/shard_map/all_to_all | solution.py:402
  23.3 0.0 copy-done
  23.4 3.1 %collective-permute-start = (f32[192,128]{1,0:T(8,128)S(1)}, f32[192,128]{1,0:T(8,128)S(1)}, u32[]{:S(2)}, u32[]{:S(2)}) collective-permute-start(f32[192,128]{1,0:T(8,128)S(1)} %get-tuple-element.59), channel_id=1, source_target_pairs={{0,16},{16,32},{32,48},{48,64},{64,80},{80,96},{96,112},{112,128},... | collective-permute-start | bytes 294920 | tf_op jit(solution)/shard_map/ppermute | solution.py:25
  26.4 4.6 %collective-permute-start.1 = (f32[192,128]{1,0:T(8,128)S(1)}, f32[192,128]{1,0:T(8,128)S(1)}, u32[]{:S(2)}, u32[]{:S(2)}) collective-permute-start(f32[192,128]{1,0:T(8,128)S(1)} %get-tuple-element.58), channel_id=1, source_target_pairs={{0,1},{1,2},{2,3},{3,4},{4,5},{5,6},{6,7},{7,8},{8,9},{9,10},{10,1... | collective-permute-start | bytes 294920 | tf_op jit(solution)/shard_map/ppermute | solution.py:25
  31.0 0.0 collective-permute-done.above
  31.1 1.6 %collective-permute-done.1.left = f32[192,128]{1,0:T(8,128)S(1)} collective-permute-done((f32[192,128]{1,0:T(8,128)S(1)}, f32[192,128]{1,0:T(8,128)S(1)}, u32[]{:S(2)}, u32[]{:S(2)}) %collective-permute-start.1) | collective-permute-done | bytes 98336 | tf_op jit(solution)/shard_map/ppermute | solution.py:25
  32.7 0.0 copy-done.20
  32.7 2.3 %precond.1 = (f32[208,128]{1,0:T(8,128)}, f32[240,128]{1,0:T(8,128)}, f32[208,128]{1,0:T(8,128)}, f32[240,128]{1,0:T(8,128)S(1)}, f32[768,128]{1,0:T(8,128)S(1)}) custom-call(f32[384,128]{1,0:T(8,128)S(1)} %bitcast.29, f32[192,128]{1,0:T(8,128)S(1)} %collective-permute-done.above, f32[192,128]{1,0:T(8,128)S(1)} %collective-permute-done.1.left, ...), custom_call_target="tpu_custom_call" | custom-call | flops 452984832 | tf_op jit(solution)/shard_map/precond/pallas_call | solution.py:337
  34.9 0.8 copy-done.4
  35.7 3.1 %collective-permute-start.2 = (f32[240,128]{1,0:T(8,128)}, f32[240,128]{1,0:T(8,128)S(1)}, u32[]{:S(2)}, u32[]{:S(2)}) collective-permute-start(f32[240,128]{1,0:T(8,128)} %get-tuple-element.35), channel_id=1, source_target_pairs={{0,16},{16,32},{32,48},{48,64},{64,80},{80,96},{96,112},{112,128},... | collective-permute-start | bytes 368648 | tf_op jit(solution)/shard_map/ppermute | solution.py:25
  38.8 4.6 %collective-permute-start.4 = (f32[240,128]{1,0:T(8,128)S(1)}, f32[240,128]{1,0:T(8,128)S(1)}, u32[]{:S(2)}, u32[]{:S(2)}) collective-permute-start(f32[240,128]{1,0:T(8,128)S(1)} %get-tuple-element.37), channel_id=1, source_target_pairs={{0,1},{1,2},{2,3},{3,4},{4,5},{5,6},{6,7},{7,8},{8,9},{9,10},{10,1... | collective-permute-start | bytes 368648 | tf_op jit(solution)/shard_map/ppermute | solution.py:25
  43.4 1.3 collective-permute-start.3
  44.7 1.9 %collective-permute-start.5 = (f32[208,128]{1,0:T(8,128)}, f32[208,128]{1,0:T(8,128)S(1)}, u32[]{:S(2)}, u32[]{:S(2)}) collective-permute-start(f32[208,128]{1,0:T(8,128)} %get-tuple-element.38), channel_id=1, source_target_pairs={{1,0},{2,1},{3,2},{4,3},{5,4},{6,5},{7,6},{8,7},{9,8},{10,9},{11,1... | collective-permute-start | bytes 319496 | tf_op jit(solution)/shard_map/ppermute | solution.py:25
  46.6 0.6 dynamic_slice.3.offset
  47.2 1.8 %collective-permute-done.3.below = f32[208,128]{1,0:T(8,128)S(1)} collective-permute-done((f32[208,128]{1,0:T(8,128)}, f32[208,128]{1,0:T(8,128)S(1)}, u32[]{:S(2)}, u32[]{:S(2)}) %collective-permute-start.3) | collective-permute-done | bytes 106528 | tf_op jit(solution)/shard_map/ppermute | solution.py:25
  49.0 1.9 %collective-permute-done.5.right = f32[208,128]{1,0:T(8,128)S(1)} collective-permute-done((f32[208,128]{1,0:T(8,128)}, f32[208,128]{1,0:T(8,128)S(1)}, u32[]{:S(2)}, u32[]{:S(2)}) %collective-permute-start.5) | collective-permute-done | bytes 106528 | tf_op jit(solution)/shard_map/ppermute | solution.py:25
  50.9 0.0 collective-permute-done.2.above
  50.9 0.0 collective-permute-done.4.left
  51.0 1.1 copy-done.5
  52.1 1.0 coarse_in.1
  53.0 0.0 all-to-all-done
  53.0 15.0 %all-to-all-start.1 = ((f32[32,8,128]{2,1,0:T(8,128)}), f32[32,8,128]{2,1,0:T(8,128)S(1)}, u32[]{:S(2)}, u32[]{:S(2)}) async-start(f32[32,8,128]{2,1,0:T(8,128)} %bitcast.12), calls=%async_computation.1 | async-start | bytes 262144 | tf_op jit(solution)/shard_map/all_to_all | solution.py:424
  68.1 0.0 copy-done.12
  68.1 0.0 copy-done.14
  68.1 0.0 copy-done.8
  68.1 0.0 copy-done.10
  68.1 0.0 copy-start.25
  68.1 1.3 copy-done.25
  69.4 1.3 copy-done.32
  70.7 0.0 copy-start.21
  70.7 0.0 copy-start.23
  70.7 0.0 copy-start.27
  70.7 0.0 copy-start.30
  70.7 2.1 %flex.1 = (bf16[768,768]{1,0:T(8,128)(2,1)S(1)}, bf16[768,768]{1,0:T(8,128)(2,1)S(1)}) custom-call(bf16[768,768]{1,0:T(8,128)(2,1)S(1)} %copy-done.32, bf16[768,768]{1,0:T(8,128)(2,1)S(1)} %get-tuple-element.30.place, bf16[768,768]{1,0:T(8,128)(2,1)S(1)} %bitcast.45), custom_call_target="tpu_custom_call" | custom-call | flops 1811939328 | tf_op jit(solution)/shard_map/flex/pallas_call | solution.py:337
  72.9 3.8 %tables.1 = (bf16[768,128]{1,0:T(8,128)(2,1)S(1)}, bf16[768,128]{1,0:T(8,128)(2,1)S(1)}, f32[32,768]{1,0:T(8,128)S(1)}, f32[8,128]{1,0:T(8,128)S(1)}, f32[256,256]{1,0:T(8,128)S(1)}) custom-call(s32[4]{0:T(128)S(1)} %bitcast.42, s32[1]{0:T(128)} %dynamic_slice.3.offset, f32[240,128]{1,0:T(8,128)S(1)} %copy-done.9, f32[208,128]{1,0:T(8,128)S(1)} %copy-done.13, ...), custom_call_target="tpu_custom_call" | custom-call | flops 905969664 | tf_op jit(solution)/shard_map/tables/pallas_call | solution.py:337
  76.7 1.1 copy-done.1
  77.8 0.7 copy-done.6
  78.5 0.6 copy-done.18
  79.1 0.0 all-to-all-done.1
  79.1 0.4 coarse.3
  79.5 16.1 %all_to_all.55 = f32[16,16,128]{2,1,0:T(8,128)S(1)} all-to-all(f32[16,16,128]{2,1,0:T(8,128)S(1)} %bitcast.34), channel_id=1, replica_groups=mesh['gx_0'=8,'gx_1'=4,'gy_0'=8,'gy_1'=2] {'gy_0','gy_1'}, dimensions={0} | all-to-all | bytes 262144 | tf_op jit(solution)/shard_map/all_to_all | solution.py:443
  95.6 1.3 copy-done.2
  96.9 0.9 copy-done.7
  97.8 0.9 copy-done.19
  98.7 0.9 project.1
  99.6 15.6 %all_to_all.56 = f32[16,40,128]{2,1,0:T(8,128)S(1)} all-to-all(f32[16,40,128]{2,1,0:T(8,128)S(1)} %bitcast.37), channel_id=1, replica_groups=mesh['gx_0'=8,'gx_1'=4,'gy_0'=8,'gy_1'=2] {'gy_0','gy_1'}, dimensions={0} | all-to-all | bytes 655360 | tf_op jit(solution)/shard_map/all_to_all | solution.py:451
  115.2 0.1 spread_sum.1
  115.3 29.1 %all_to_all.57 = f32[32,40,128]{2,1,0:T(8,128)S(1)} all-to-all(f32[32,40,128]{2,1,0:T(8,128)S(1)} %bitcast.28), channel_id=1, replica_groups=mesh['gx_0'=8,'gx_1'=4,'gy_0'=8,'gy_1'=2] {'gx_0','gx_1'}, dimensions={0} | all-to-all | bytes 1310720 | tf_op jit(solution)/shard_map/all_to_all | solution.py:455
  144.4 2.4 %search.1 = (f32[192,128]{1,0:T(8,128)S(1)}, f32[192,128]{1,0:T(8,128)S(1)}, f32[384,128]{1,0:T(8,128)S(1)}, f32[384,128]{1,0:T(8,128)}, f32[8,128]{1,0:T(8,128)S(1)}) custom-call(f32[1280,128]{1,0:T(8,128)S(1)} %bitcast.27, f32[768,128]{1,0:T(8,128)S(1)} %get-tuple-element.50.projected, bf16[768,128]{1,0:T(8,128)(2,1)S(1)} %get-tuple-element.51.search_six, ...), custom_call_target="tpu_custom_call" | custom-call | flops 452984832 | tf_op jit(solution)/shard_map/search/pallas_call | solution.py:337
  146.8 1.3 collective-permute-start.6
  148.1 2.9 %collective-permute-start.7 = (f32[192,128]{1,0:T(8,128)S(1)}, f32[192,128]{1,0:T(8,128)S(1)}, u32[]{:S(2)}, u32[]{:S(2)}) collective-permute-start(f32[192,128]{1,0:T(8,128)S(1)} %get-tuple-element.56), channel_id=1, source_target_pairs={{1,0},{2,1},{3,2},{4,3},{5,4},{6,5},{7,6},{8,7},{9,8},{10,9},{11,1... | collective-permute-start | bytes 294920 | tf_op jit(solution)/shard_map/ppermute | solution.py:25
  151.0 1.2 collective-permute-done.6.below
  152.1 1.9 %collective-permute-done.7.right = f32[192,128]{1,0:T(8,128)S(1)} collective-permute-done((f32[192,128]{1,0:T(8,128)S(1)}, f32[192,128]{1,0:T(8,128)S(1)}, u32[]{:S(2)}, u32[]{:S(2)}) %collective-permute-start.7) | collective-permute-done | bytes 98336 | tf_op jit(solution)/shard_map/ppermute | solution.py:25
  154.0 1.3 residual.1
  (40 shorter events, 0.1 us)
Async XLA Ops:
  1.3 0.7 copy-start.22
  2.0 1.3 copy-start.24
  3.3 0.7 copy-start.26
  4.0 0.7 copy-start.28
  4.7 0.7 copy-start.29
  5.4 17.9 %copy-start = (f32[1,1,384,128]{3,2,1,0:T(8,128)S(1)}, f32[1,1,384,128]{3,2,1,0:T(8,128)}, u32[]{:S(2)}) copy-start(f32[1,1,384,128]{3,2,1,0:T(8,128)} %param.12) | copy-start | bytes 589828
  7.5 0.7 copy-start.3
  8.3 1.1 copy-start.31
  9.4 41.6 %copy-start.16 = (f32[8,768]{1,0:T(8,128)}, f32[8,768]{1,0:T(8,128)S(1)}, u32[]{:S(2)}) copy-start(f32[8,768]{1,0:T(8,128)S(1)} %get-tuple-element.33.mode_rows) | copy-start | bytes 73732
  9.4 23.3 %copy-start.20 = (f32[1,1,16,384]{3,2,1,0:T(8,128)S(1)}, f32[1,1,16,384]{3,2,1,0:T(8,128)}, u32[]{:S(2)}) copy-start(f32[1,1,16,384]{3,2,1,0:T(8,128)} %param.17) | copy-start | bytes 73732
  9.4 43.7 %all-to-all-start = ((f32[32,8,384]{2,1,0:T(8,128)}), f32[32,8,384]{2,1,0:T(8,128)}, u32[]{:S(2)}, u32[]{:S(2)}) async-start(f32[32,8,384]{2,1,0:T(8,128)} %bitcast.36), calls=%async_computation | async-start | bytes 786432 | tf_op jit(solution)/shard_map/all_to_all | solution.py:402
  23.4 7.7 %collective-permute-start = (f32[192,128]{1,0:T(8,128)S(1)}, f32[192,128]{1,0:T(8,128)S(1)}, u32[]{:S(2)}, u32[]{:S(2)}) collective-permute-start(f32[192,128]{1,0:T(8,128)S(1)} %get-tuple-element.59), channel_id=1, source_target_pairs={{0,16},{16,32},{32,48},{48,64},{64,80},{80,96},{96,112},{112,128},... | collective-permute-start | bytes 294920 | tf_op jit(solution)/shard_map/ppermute | solution.py:25
  26.4 6.2 %collective-permute-start.1 = (f32[192,128]{1,0:T(8,128)S(1)}, f32[192,128]{1,0:T(8,128)S(1)}, u32[]{:S(2)}, u32[]{:S(2)}) collective-permute-start(f32[192,128]{1,0:T(8,128)S(1)} %get-tuple-element.58), channel_id=1, source_target_pairs={{0,1},{1,2},{2,3},{3,4},{4,5},{5,6},{6,7},{7,8},{8,9},{9,10},{10,1... | collective-permute-start | bytes 294920 | tf_op jit(solution)/shard_map/ppermute | solution.py:25
  32.7 14.0 %copy-start.33 = (s32[32]{0:T(128)S(1)}, s32[32]{0:T(128)}, u32[]{:S(2)}) copy-start(s32[32]{0:T(128)} %constant.22.clone) | copy-start | bytes 388
  34.9 0.8 copy-start.4
  35.7 15.2 %collective-permute-start.2 = (f32[240,128]{1,0:T(8,128)}, f32[240,128]{1,0:T(8,128)S(1)}, u32[]{:S(2)}, u32[]{:S(2)}) collective-permute-start(f32[240,128]{1,0:T(8,128)} %get-tuple-element.35), channel_id=1, source_target_pairs={{0,16},{16,32},{32,48},{48,64},{64,80},{80,96},{96,112},{112,128},... | collective-permute-start | bytes 368648 | tf_op jit(solution)/shard_map/ppermute | solution.py:25
  38.8 12.1 %collective-permute-start.4 = (f32[240,128]{1,0:T(8,128)S(1)}, f32[240,128]{1,0:T(8,128)S(1)}, u32[]{:S(2)}, u32[]{:S(2)}) collective-permute-start(f32[240,128]{1,0:T(8,128)S(1)} %get-tuple-element.37), channel_id=1, source_target_pairs={{0,1},{1,2},{2,3},{3,4},{4,5},{5,6},{6,7},{7,8},{8,9},{9,10},{10,1... | collective-permute-start | bytes 368648 | tf_op jit(solution)/shard_map/ppermute | solution.py:25
  43.4 5.7 %collective-permute-start.3 = (f32[208,128]{1,0:T(8,128)}, f32[208,128]{1,0:T(8,128)S(1)}, u32[]{:S(2)}, u32[]{:S(2)}) collective-permute-start(f32[208,128]{1,0:T(8,128)} %get-tuple-element.36), channel_id=1, source_target_pairs={{16,0},{32,16},{48,32},{64,48},{80,64},{96,80},{112,96},{128,112},... | collective-permute-start | bytes 319496 | tf_op jit(solution)/shard_map/ppermute | solution.py:25
  44.7 6.2 %collective-permute-start.5 = (f32[208,128]{1,0:T(8,128)}, f32[208,128]{1,0:T(8,128)S(1)}, u32[]{:S(2)}, u32[]{:S(2)}) collective-permute-start(f32[208,128]{1,0:T(8,128)} %get-tuple-element.38), channel_id=1, source_target_pairs={{1,0},{2,1},{3,2},{4,3},{5,4},{6,5},{7,6},{8,7},{9,8},{10,9},{11,1... | collective-permute-start | bytes 319496 | tf_op jit(solution)/shard_map/ppermute | solution.py:25
  49.0 19.0 %copy-start.12 = (f32[208,128]{1,0:T(8,128)}, f32[208,128]{1,0:T(8,128)S(1)}, u32[]{:S(2)}) copy-start(f32[208,128]{1,0:T(8,128)S(1)} %collective-permute-done.3.below) | copy-start | bytes 319492
  50.9 17.2 %copy-start.14 = (f32[208,128]{1,0:T(8,128)}, f32[208,128]{1,0:T(8,128)S(1)}, u32[]{:S(2)}) copy-start(f32[208,128]{1,0:T(8,128)S(1)} %collective-permute-done.5.right) | copy-start | bytes 319492
  50.9 17.2 %copy-start.8 = (f32[240,128]{1,0:T(8,128)}, f32[240,128]{1,0:T(8,128)S(1)}, u32[]{:S(2)}) copy-start(f32[240,128]{1,0:T(8,128)S(1)} %collective-permute-done.2.above) | copy-start | bytes 368644
  50.9 17.2 %copy-start.10 = (f32[240,128]{1,0:T(8,128)}, f32[240,128]{1,0:T(8,128)S(1)}, u32[]{:S(2)}) copy-start(f32[240,128]{1,0:T(8,128)S(1)} %collective-permute-done.4.left) | copy-start | bytes 368644
  51.0 1.1 copy-start.5
  53.0 26.1 %all-to-all-start.1 = ((f32[32,8,128]{2,1,0:T(8,128)}), f32[32,8,128]{2,1,0:T(8,128)S(1)}, u32[]{:S(2)}, u32[]{:S(2)}) async-start(f32[32,8,128]{2,1,0:T(8,128)} %bitcast.12), calls=%async_computation.1 | async-start | bytes 262144 | tf_op jit(solution)/shard_map/all_to_all | solution.py:424
  68.1 1.3 copy-start.25
  69.4 1.3 copy-start.32
  70.6 2.2 %copy-start.9 = (f32[240,128]{1,0:T(8,128)S(1)}, f32[240,128]{1,0:T(8,128)}, u32[]{:S(2)}) copy-start(f32[240,128]{1,0:T(8,128)} %copy-done.8) | copy-start | bytes 368644
  70.6 2.2 %copy-start.11 = (f32[240,128]{1,0:T(8,128)S(1)}, f32[240,128]{1,0:T(8,128)}, u32[]{:S(2)}) copy-start(f32[240,128]{1,0:T(8,128)} %copy-done.10) | copy-start | bytes 368644
  70.6 2.2 %copy-start.13 = (f32[208,128]{1,0:T(8,128)S(1)}, f32[208,128]{1,0:T(8,128)}, u32[]{:S(2)}) copy-start(f32[208,128]{1,0:T(8,128)} %copy-done.12) | copy-start | bytes 319492
  70.7 2.2 %copy-start.15 = (f32[208,128]{1,0:T(8,128)S(1)}, f32[208,128]{1,0:T(8,128)}, u32[]{:S(2)}) copy-start(f32[208,128]{1,0:T(8,128)} %copy-done.14) | copy-start | bytes 319492
  70.7 2.2 %copy-start.17 = (f32[8,768]{1,0:T(8,128)S(1)}, f32[8,768]{1,0:T(8,128)}, u32[]{:S(2)}) copy-start(f32[8,768]{1,0:T(8,128)} %copy-done.16) | copy-start | bytes 73732
  70.7 2.2 %copy-start.21 = (f32[1,1,16,384]{3,2,1,0:T(8,128)S(1)}, f32[1,1,16,384]{3,2,1,0:T(8,128)}, u32[]{:S(2)}) copy-start(f32[1,1,16,384]{3,2,1,0:T(8,128)} %param.17) | copy-start | bytes 73732
  70.7 2.2 %copy-start.23 = (s32[1,1,4]{2,1,0:T(1,128)S(1)}, s32[1,1,4]{2,1,0:T(1,128)}, u32[]{:S(2)}) copy-start(s32[1,1,4]{2,1,0:T(1,128)} %param.20) | copy-start | bytes 52
  70.7 2.2 %copy-start.27 = (f32[1,1,16,384]{3,2,1,0:T(8,128)S(1)}, f32[1,1,16,384]{3,2,1,0:T(8,128)}, u32[]{:S(2)}) copy-start(f32[1,1,16,384]{3,2,1,0:T(8,128)} %param.18) | copy-start | bytes 73732
  70.7 2.2 %copy-start.30 = (s32[256,128]{1,0:T(8,128)S(1)}, s32[256,128]{1,0:T(8,128)}, u32[]{:S(2)}) copy-start(s32[256,128]{1,0:T(8,128)} %constant.23.clone.wanted) | copy-start | bytes 393220
  76.7 1.1 copy-start.1
  77.8 0.7 copy-start.6
  78.5 0.6 copy-start.18
  95.6 1.3 copy-start.2
  96.9 0.9 copy-start.7
  97.8 0.9 copy-start.19
  146.8 5.3 %collective-permute-start.6 = (f32[192,128]{1,0:T(8,128)S(1)}, f32[192,128]{1,0:T(8,128)S(1)}, u32[]{:S(2)}, u32[]{:S(2)}) collective-permute-start(f32[192,128]{1,0:T(8,128)S(1)} %get-tuple-element.55), channel_id=1, source_target_pairs={{16,0},{32,16},{48,32},{64,48},{80,64},{96,80},{112,96},{128,112},... | collective-permute-start | bytes 294920 | tf_op jit(solution)/shard_map/ppermute | solution.py:25
  148.1 5.9 %collective-permute-start.7 = (f32[192,128]{1,0:T(8,128)S(1)}, f32[192,128]{1,0:T(8,128)S(1)}, u32[]{:S(2)}, u32[]{:S(2)}) collective-permute-start(f32[192,128]{1,0:T(8,128)S(1)} %get-tuple-element.56), channel_id=1, source_target_pairs={{1,0},{2,1},{3,2},{4,3},{5,4},{6,5},{7,6},{8,7},{9,8},{10,9},{11,1... | collective-permute-start | bytes 294920 | tf_op jit(solution)/shard_map/ppermute | solution.py:25

commit v2 on v1

v2 whole, which is shorter than its diff:
```python
import functools

import jax
import jax.numpy as jnp
from jax import lax
from jax.experimental import pallas as pl
from jax.experimental.pallas import tpu as pltpu
from jax.sharding import Mesh
from jax.sharding import PartitionSpec as P


GX = ("gx_0", "gx_1")
GY = ("gy_0", "gy_1")
GX_GY = ("gx_0", "gx_1", "gy_0", "gy_1")

F32 = jnp.float32
BF16 = jnp.bfloat16
HIGHEST = lax.Precision.HIGHEST
SIGNS = (-1.0, 1.0, -1.0, 1.0)


def shifted(value, axis, steps):
    count = lax.axis_size(axis)
    initial, last = (max(0, -steps), min(count, count - steps))
    return lax.ppermute(value, axis, [(source, source + steps) for source in range(initial, last)])


def split3(x):
    high = x.astype(BF16)
    rest = x - high.astype(F32)
    mid = rest.astype(BF16)
    low = (rest - mid.astype(F32)).astype(BF16)
    return high, mid, low


def dot(a, b):
    return lax.dot_general(a, b, (((1,), (0,)), ((), ())), preferred_element_type=F32)


def dot_nt(a, b):
    return lax.dot_general(a, b, (((1,), (1,)), ((), ())), preferred_element_type=F32)


def dot_exact(a, b):
    return lax.dot_general(
        a, b, (((1,), (0,)), ((), ())), precision=HIGHEST, preferred_element_type=F32
    )


def select_rows(selection, x):
    width = x.shape[1]
    out = dot(selection, jnp.concatenate(split3(x), axis=1))
    return out[:, :width] + (out[:, width : 2 * width] + out[:, 2 * width :])


def select_lanes(x, selection):
    rows = x.shape[0]
    out = dot(jnp.concatenate(split3(x), axis=0), selection)
    return out[:rows] + (out[rows : 2 * rows] + out[2 * rows :])


def six_left(tiled):
    high, mid, low = split3(tiled)
    group = lax.broadcasted_iota(jnp.int32, tiled.shape, 1) // 16
    zero = jnp.zeros_like(tiled)
    is_high = (group == 0) | (group == 1) | (group == 3)
    is_mid = (group == 2) | (group == 4)
    out = jnp.where(
        is_high,
        high.astype(F32),
        jnp.where(is_mid, mid.astype(F32), jnp.where(group == 5, low.astype(F32), zero)),
    )
    return out.astype(BF16)


def six_right(x):
    high, mid, low = split3(x)
    zero = jnp.zeros_like(high)
    return jnp.concatenate([high, mid, high, low, mid, high, zero, zero], axis=0)


def tile_matrix():
    row = lax.broadcasted_iota(jnp.int32, (16, 128), 0)
    lane = lax.broadcasted_iota(jnp.int32, (16, 128), 1)
    return jnp.where(lane % 16 == row, 1.0, 0.0).astype(F32)


def widened(x, lanes):
    return jnp.concatenate([x, jnp.zeros((x.shape[0], lanes - x.shape[1]), x.dtype)], axis=1)


def lane_window(x, start, width):
    total = x.shape[1]
    if start:
        x = pltpu.roll(x, total - start, 1)
    return x[:, :width]


def at_lanes(x, start):
    return pltpu.roll(x, start, 1) if start else x


def first_kernel(windows, gap_hbm, coarse_hbm, down, right, blocks, coarse, wide, arrived):
    width = down.shape[0]
    copies = [
        pltpu.make_async_copy(source, target, arrived.at[n])
        for n, (source, target) in enumerate(
            (
                (coarse_hbm, coarse),
                (gap_hbm.at[pl.ds(0, width)], down),
                (gap_hbm.at[pl.ds(width, width)], right),
            )
        )
    ]
    for copy in copies:
        copy.start()
    wide[...] = jnp.zeros_like(wide)
    copies[0].wait()
    wide[0:3, :] = coarse[...]
    for i, start in enumerate(windows):
        blocks[8 * i : 8 * i + 8, :] = wide[:, start : start + blocks.shape[1]]
    copies[1].wait()
    copies[2].wait()


def prepare_kernel(
    count_hbm, slots_hbm, mult_hbm, modes_hbm, schur_hbm,
    place, pick_schur, mode_rows, link_rows, columns,
    buffer, slots, mult, modes, schur, count, arrived,
):
    copies = [
        pltpu.make_async_copy(source, target, arrived.at[n])
        for n, (source, target) in enumerate(
            (
                (count_hbm, count), (slots_hbm, slots), (mult_hbm, mult), (modes_hbm, modes),
                (schur_hbm, schur),
            )
        )
    ]
    for copy in copies:
        copy.start()
    width = slots.shape[1]
    total = 4 * width
    buffer[...] = jnp.zeros_like(buffer)
    lane = lax.broadcasted_iota(jnp.int32, (1, total), 1)
    copies[0].wait()
    copies[1].wait()
    buffer[0:4, 0:width] = slots[...].astype(F32)
    raw = buffer[...]
    slot_row = jnp.zeros((1, total), F32)
    sign_row = jnp.zeros((1, total), F32)
    for f in range(4):
        inside = (lane >= width * f) & (lane < width * f + count[0, f])
        slot_row = jnp.where(inside, at_lanes(raw, width * f)[f : f + 1], slot_row)
        sign_row = jnp.where(inside, SIGNS[f], sign_row)
    copies[2].wait()
    weights = 1.0 / mult[...].astype(F32)
    down = lax.broadcasted_iota(jnp.int32, (total, total), 0).astype(F32)
    place_value = jnp.where(down == slot_row, sign_row, 0.0).astype(BF16)
    place[...] = place_value
    copies[3].wait()
    buffer[...] = jnp.zeros_like(buffer)
    for k in range(modes.shape[0]):
        buffer[k : k + 1, :] = modes[k]
    buffer[3:4, :] = weights
    rows = select_lanes(buffer[...], place_value)
    mode_rows[...] = rows
    buffer[...] = jnp.zeros_like(buffer)
    buffer[0:1, :] = slot_row
    buffer[1:2, :] = sign_row
    buffer[2:3, :] = weights
    buffer[3:4, :] = jnp.abs(rows[3:4])
    link_rows[...] = buffer[...]
    cols = jnp.transpose(buffer[...])
    columns[...] = cols
    pick_value = picking(cols)
    copies[4].wait()
    pick_schur[...] = dot(pick_value, schur[...]).astype(BF16)


def picking(cols):
    total = cols.shape[0]
    across = lax.broadcasted_iota(jnp.int32, (total, total), 1).astype(F32)
    return jnp.where(across == cols[:, 0:1], cols[:, 1:2], 0.0).astype(BF16)


def precond_kernel(
    gap_down, gap_right, above, left, place, pick_schur, columns, mode_rows, saved,
    up_msg, down_msg, left_msg, right_msg, own, residual,
):
    width = above.shape[0]
    links = jnp.concatenate([above[...], gap_down[...], left[...], gap_right[...]], axis=0)
    spread = select_rows(place[...], links)
    weighted = (columns[:, 2:3] * spread).astype(BF16)
    picked = columns[:, 3:4] * dot(pick_schur[...], weighted)
    own[...] = picked
    for f, msg in enumerate((up_msg, down_msg, left_msg, right_msg)):
        msg[0:width, :] = picked[width * f : width * f + width]
        rows = lane_window(mode_rows[...], width * f, 256)
        msg[width : width + 8, :] = rows[:, 0:128]
        msg[width + 8 : width + 16, :] = rows[:, 128:256]
    for start, msg in ((0, down_msg), (width, right_msg)):
        rows = lane_window(saved[...], start, 256)
        msg[width + 16 : width + 32, :] = rows[:, 0:128]
        msg[width + 32 : width + 48, :] = rows[:, 128:256]
    residual[0:width, :] = jnp.where(columns[width : 2 * width, 1:2] != 0.0, gap_down[...], 0.0)
    residual[width:, :] = jnp.where(columns[3 * width :, 1:2] != 0.0, gap_right[...], 0.0)


def flex_kernel(
    grid, here, link_rows, place, blocks, flex_hbm, pick_flex_hbm, link_flex_hbm, coarse_rows,
    flex, pick_flex, link_flex, arrived,
):
    load = pltpu.make_async_copy(flex_hbm, flex, arrived.at[0])
    load.start()
    row_unknowns, last_window = grid
    count = row_unknowns // 3
    first = row_unknowns * (here[0] - 1)
    offset = first - jnp.clip(first >> 7, 0, last_window) * 128
    row = lax.broadcasted_iota(jnp.int32, (coarse_rows.shape[0], 1), 0)
    j = row >> 4
    part = ((row & 15) * 11) >> 5
    mode = (row & 15) - 3 * part
    down = jnp.where(part == 1, -1, jnp.where(part == 2, 1, 0))
    j = j + jnp.where(part == 3, -1, jnp.where(part == 4, 1, 0))
    valid = (part < 5) & (j >= 0) & (j < count)
    wanted = jnp.where(valid, ((down + 1) * count + j) * 3 + mode + offset, -1)
    at = lax.broadcasted_iota(jnp.int32, (coarse_rows.shape[0], blocks.shape[1]), 1)
    chosen = jnp.where(at == wanted, 1.0, 0.0).astype(BF16)
    high, mid, low = split3(blocks[...])
    coarse_rows[...] = dot_nt(chosen, high) + (dot_nt(chosen, mid) + dot_nt(chosen, low))
    pick_value = picking(jnp.transpose(link_rows[...]))
    load.wait()
    rows = dot(pick_value, flex[...]).astype(BF16)
    pick_flex[...] = rows
    store = pltpu.make_async_copy(pick_flex, pick_flex_hbm, arrived.at[1])
    store.start()
    link_flex[...] = dot(rows, place[...]).astype(BF16)
    store_link = pltpu.make_async_copy(link_flex, link_flex_hbm, arrived.at[2])
    store_link.start()
    store.wait()
    store_link.wait()


def coarse_in_kernel(own, above, below, left, right, mode_rows, precond, coarse):
    width = own.shape[0] // 4
    full = own[...] + jnp.concatenate(
        [above[0:width], below[0:width], left[0:width], right[0:width]], axis=0
    )
    precond[...] = full
    rows = dot_exact(mode_rows[...], full)
    rows = jnp.where(lax.broadcasted_iota(jnp.int32, rows.shape, 0) < 3, rows, 0.0)
    for i in range(coarse.shape[0] // 8):
        coarse[8 * i : 8 * i + 8, :] = rows


def tables_kernel(
    above, below, left, right, mode_rows, link_rows, saved, images, residual, precond, link_flex_hbm,
    mode_six, search_six, forms, sums,
    link_flex, arrived,
):
    load = pltpu.make_async_copy(link_flex_hbm, link_flex, arrived.at[0])
    load.start()
    total = mode_rows.shape[1]
    width = total // 4
    tiles = tile_matrix()
    near = lax.broadcasted_iota(jnp.int32, (1, 256), 1) < width
    used = link_rows[1:2, :] != 0.0
    row = lax.broadcasted_iota(jnp.int32, (16, total), 0)
    mine = jnp.concatenate([mode_rows[...], jnp.zeros((8, total), F32)], axis=0)
    modes = jnp.where(row < 3, mine, 0.0)
    for f, msg in enumerate((above, below, left, right)):
        theirs = jnp.concatenate([msg[width : width + 8], msg[width + 8 : width + 16]], axis=1)
        theirs = at_lanes(widened(jnp.where(near, theirs, 0.0), total), width * f)
        theirs = jnp.concatenate([theirs, jnp.zeros((8, total), F32)], axis=0)
        theirs = jnp.where(row < 3, theirs, 0.0)
        modes = modes + pltpu.roll(theirs, 3 * (1 + f), 0)
    modes = jnp.where(used, modes, 0.0)
    mode_six[...] = six_left(
        lax.dot_general(modes, tiles, (((0,), (0,)), ((), ())), precision=HIGHEST, preferred_element_type=F32)
    )
    search = jnp.zeros((16, total), F32)
    for f in range(4):
        if f % 2 == 0:
            msg = above if f == 0 else left
            piece = jnp.concatenate(
                [msg[width + 16 : width + 32], msg[width + 32 : width + 48]], axis=1
            )
        else:
            piece = lane_window(saved[...], 0 if f == 1 else width, 256)
        search = search + at_lanes(widened(jnp.where(near, piece, 0.0), total), width * f)
    search = jnp.where(used, search, 0.0)
    search_tiled = lax.dot_general(
        search, tiles, (((0,), (0,)), ((), ())), precision=HIGHEST, preferred_element_type=F32
    )
    search_six[...] = six_left(search_tiled)
    lanes = lax.broadcasted_iota(jnp.int32, (16, total), 1)
    image = widened(images[...], total)
    image_down = at_lanes(image, width)
    image_right = at_lanes(image, 2 * width)
    forms[0:16, :] = jnp.where(
        (lanes >= width) & (lanes < 2 * width),
        image_down,
        jnp.where(lanes >= 3 * width, image_right, 0.0),
    )
    energy = jnp.sum(residual[0:width] * precond[width : 2 * width], axis=0, keepdims=True) + jnp.sum(
        residual[width:] * precond[3 * width :], axis=0, keepdims=True
    )
    load.wait()
    flex_search = select_lanes(search, link_flex[...])
    forms[16:32, :] = flex_search
    products = dot_exact(flex_search, search_tiled)
    group = lax.broadcasted_iota(jnp.int32, (16, 128), 1) // 16
    part = lax.broadcasted_iota(jnp.int32, (16, 128), 0)
    products = jnp.where(group == part % 8, products, 0.0)
    sums[...] = jnp.concatenate(
        [
            energy,
            jnp.zeros((1, 128), F32),
            jnp.sum(products[0:8], axis=0, keepdims=True),
            jnp.sum(products[8:16], axis=0, keepdims=True),
            jnp.zeros((4, 128), F32),
        ],
        axis=0,
    )


def coarse_kernel(coarse_rows, gathered, parts):
    parts[...] = dot_exact(coarse_rows[...], gathered[...])


def block_sum(ref, height):
    out = ref[0:height]
    for j in range(1, ref.shape[0] // height):
        out = out + ref[height * j : height * j + height]
    return out


def project_kernel(
    chunk, arrived, precond, mode_six, forms, sums, link_flex_hbm, projected, partial,
    link_flex, copied,
):
    load = pltpu.make_async_copy(link_flex_hbm, link_flex, copied.at[0])
    load.start()
    links = precond[...] - dot(mode_six[...], six_right(block_sum(arrived, 16)))
    projected[...] = links
    linear = dot_exact(forms[...], links)
    high, mid, _ = split3(links)
    parts = jnp.concatenate([high, mid], axis=1)
    load.wait()
    image = dot(link_flex[...], parts)
    square = jnp.sum(links * (image[:, :128] + image[:, 128:]), axis=0, keepdims=True)
    row = lax.broadcasted_iota(jnp.int32, (8, 128), 0)
    last = jnp.where(row == 1, square, sums[...])
    padding = jnp.zeros((partial.shape[0] // 2 - 40, 128), F32)
    full = jnp.concatenate([linear, last, padding], axis=0)
    for j in range(partial.shape[0] // chunk):
        at = chunk * (j // 2)
        partial[chunk * j : chunk * j + chunk, :] = full[at : at + chunk]


def spread_sum_kernel(height, arrived, partial):
    out = block_sum(arrived, height)
    for i in range(partial.shape[0] // height):
        partial[height * i : height * i + height, :] = out


def search_kernel(
    sums, projected, search_six, place, pick_flex_hbm,
    up_msg, left_msg, own, search_own, step,
    pick_flex, arrived,
):
    load = pltpu.make_async_copy(pick_flex_hbm, pick_flex, arrived.at[0])
    load.start()
    width = up_msg.shape[0]
    intersect = sums[0:16]
    cross = sums[16:32]
    energy = sums[32:33]
    square = sums[33:34]
    search = projected[...] - dot(search_six[...], six_right(intersect))
    lifted = select_rows(place[...], search).astype(BF16)
    load.wait()
    image = dot(pick_flex[...], lifted)
    up_msg[...] = image[0:width]
    own[0:width, :] = image[width : 2 * width]
    left_msg[...] = image[2 * width : 3 * width]
    own[width:, :] = image[3 * width :]
    search_own[0:width, :] = search[width : 2 * width]
    search_own[width:, :] = search[3 * width :]
    group = lax.broadcasted_iota(jnp.int32, (16, 128), 1) // 16
    part = lax.broadcasted_iota(jnp.int32, (16, 128), 0)
    packed = jnp.where(part < 8, sums[34:35], sums[35:36])
    packed = jnp.where(group == part % 8, packed, 0.0)
    products = dot_exact(packed, jnp.concatenate([intersect] * 8, axis=0))
    curvature = square + jnp.sum(intersect * (products - 2.0 * cross), axis=0, keepdims=True)
    step[...] = jnp.broadcast_to(energy / curvature, step.shape)


def multiply_kernel(search_own, step, multipliers):
    multipliers[...] = step[0:1] * search_own[...]


def residual_kernel(before, own, below, right, step, residual):
    width = below.shape[0]
    size = step[0:1]
    residual[0:width, :] = before[0:width] - size * (own[0:width] + below[...])
    residual[width:, :] = before[width:] - size * (own[width:] + right[...])


VMEM_LIMIT = 24 * 1024 * 1024
VMEM = pl.BlockSpec(memory_space=pltpu.VMEM)
SMEM = pl.BlockSpec(memory_space=pltpu.SMEM)
HBM = pl.BlockSpec(memory_space=pltpu.HBM)


def call(kernel, inputs, outputs, scalars=0, remote=0, scratch=(), copies=0, hbm_out=(), flops=0):
    out_specs = tuple(HBM if n in hbm_out else VMEM for n in range(len(outputs)))
    outputs = tuple(
        pltpu.HBM(shape, dtype) if n in hbm_out else jax.ShapeDtypeStruct(shape, dtype)
        for n, (shape, dtype) in enumerate(outputs)
    )
    local = len(inputs) - remote
    inputs = tuple(
        x if n < local else pltpu.with_memory_space_constraint(x, pltpu.HBM)
        for n, x in enumerate(inputs)
    )
    scratch = [
        entry if not isinstance(entry, tuple) else pltpu.VMEM(*entry) for entry in scratch
    ]
    if copies:
        scratch.append(pltpu.SemaphoreType.DMA((copies,)))
    return pl.pallas_call(
        kernel,
        out_shape=outputs,
        in_specs=[SMEM] * scalars + [VMEM] * (len(inputs) - scalars - remote) + [HBM] * remote,
        out_specs=out_specs,
        scratch_shapes=scratch,
        cost_estimate=pl.CostEstimate(flops=flops, transcendentals=0, bytes_accessed=0),
        compiler_params=pltpu.CompilerParams(vmem_limit_bytes=VMEM_LIMIT),
    )(*inputs)


def step(
    gap_load, flexibility, schur_blocks, body_modes, coarse_inverse,
    saved_search, saved_images, face_slots, face_count, multiplicity,
):
    rows = lax.axis_size(GX)
    columns = lax.axis_size(GY)
    gap = gap_load[0, 0]
    flex = flexibility[0, 0]
    modes = jnp.transpose(body_modes, (0, 2, 1, 3))[0]
    saved = saved_search[0, 0]
    images = saved_images[0, 0]
    slots = face_slots[0, 0]
    count = face_count[0]
    width = slots.shape[1]
    total = 4 * width
    cases = gap.shape[1]
    unknowns = coarse_inverse.shape[1]
    row_unknowns = columns * modes.shape[0]
    window = min(unknowns, 384)
    windows = [
        min(max((row_unknowns * (i - 1)) // 128, 0), (unknowns - window) // 128) * 128
        for i in range(rows)
    ]
    here = lax.axis_index(GX).reshape(1)
    big = (total, total)
    cube = 2 * total**3
    gap_down, gap_right, blocks = call(
        functools.partial(first_kernel, windows),
        (gap, coarse_inverse),
        (((width, cases), F32), ((width, cases), F32), ((8 * rows, window), F32)),
        remote=2,
        scratch=((coarse_inverse.shape, F32), ((8, unknowns), F32)),
        copies=3,
        flops=cube // 64,
    )
    above = shifted(gap_down, GX, 1)
    left = shifted(gap_right, GY, 1)
    blocks = lax.all_to_all(blocks, GX, 0, 0, tiled=True)
    place, pick_schur, mode_rows, link_rows, slot_cols = call(
        prepare_kernel,
        (count, slots, multiplicity[0], modes, schur_blocks[0, 0]),
        (
            (big, BF16), (big, BF16), ((8, total), F32), ((8, total), F32), ((total, 8), F32),
        ),
        remote=5,
        scratch=(
            ((8, total), F32), (slots.shape, jnp.int32), ((1, total), jnp.int32), (modes.shape, F32),
            (big, BF16), pltpu.SMEM((1, 4), jnp.int32),
        ),
        copies=5,
        flops=cube,
    )
    up_msg, down_msg, left_msg, right_msg, own, residual = call(
        precond_kernel,
        (gap_down, gap_right, above, left, place, pick_schur, slot_cols, mode_rows, saved),
        tuple(((width + extra, cases), F32) for extra in (16, 48, 16, 48))
        + (((total, cases), F32), ((2 * width, cases), F32)),
        flops=cube // 2,
    )
    from_above = shifted(down_msg, GX, 1)
    from_below = shifted(up_msg, GX, -1)
    from_left = shifted(right_msg, GY, 1)
    from_right = shifted(left_msg, GY, -1)
    pick_flex, link_flex, coarse_rows = call(
        functools.partial(flex_kernel, (row_unknowns, (unknowns - window) // 128)),
        (here, link_rows, place, blocks, flex),
        ((big, BF16), (big, BF16), ((16 * columns, 8 * rows), F32)),
        scalars=1,
        remote=1,
        scratch=((big, BF16), (big, BF16), (big, BF16)),
        copies=3,
        hbm_out=(0, 1),
        flops=2 * cube,
    )
    precond, coarse_in = call(
        coarse_in_kernel,
        (own, from_above, from_below, from_left, from_right, mode_rows),
        (((total, cases), F32), ((8 * rows, cases), F32)),
        flops=cube // 16,
    )
    gathered = lax.all_to_all(coarse_in, GX, 0, 0, tiled=True)
    mode_six, search_six, forms, sums = call(
        tables_kernel,
        (
            from_above, from_below, from_left, from_right, mode_rows, link_rows, saved, images,
            residual, precond, link_flex,
        ),
        (((total, 128), BF16), ((total, 128), BF16), ((32, total), F32), ((8, cases), F32)),
        remote=1,
        scratch=((big, BF16),),
        copies=1,
        flops=cube,
    )
    (parts,) = call(
        coarse_kernel, (coarse_rows, gathered), (((16 * columns, cases), F32),), flops=cube // 8,
    )
    parts = lax.all_to_all(parts, GY, 0, 0, tiled=True)
    pairs = columns // 2
    chunk = -(-(-(-40 // pairs)) // 8) * 8
    projected, partial = call(
        functools.partial(project_kernel, chunk),
        (parts, precond, mode_six, forms, sums, link_flex),
        (((total, cases), F32), ((chunk * columns, cases), F32)),
        remote=1,
        scratch=((big, BF16),),
        copies=1,
        flops=cube // 2,
    )
    for axis, following in ((GY, rows), (GX, pairs)):
        partial = lax.all_to_all(partial, axis, 0, 0, tiled=True)
        (partial,) = call(
            functools.partial(spread_sum_kernel, chunk),
            (partial,),
            (((chunk * following, cases), F32),),
            flops=cube // 64,
        )
    sums = lax.all_to_all(partial, GY[0], 0, 0, tiled=True)
    up_msg, left_msg, own, search_own, step = call(
        search_kernel,
        (sums, projected, search_six, place, pick_flex),
        (
            ((width, cases), F32), ((width, cases), F32), ((2 * width, cases), F32),
            ((2 * width, cases), F32), ((8, cases), F32),
        ),
        remote=1,
        scratch=((big, BF16),),
        copies=1,
        flops=cube // 2,
    )
    from_below = shifted(up_msg, GX, -1)
    from_right = shifted(left_msg, GY, -1)
    (multipliers,) = call(
        multiply_kernel, (search_own, step), (((2 * width, cases), F32),), flops=cube // 64,
    )
    (residual,) = call(
        residual_kernel,
        (residual, own, from_below, from_right, step),
        (((2 * width, cases), F32),),
        flops=cube // 64,
    )
    return (multipliers[None, None], residual[None, None])


def split_shape(mesh):
    rows, columns = (mesh.devices.shape[0], mesh.devices.shape[1])
    inner = 4 if rows % 4 == 0 and rows > 4 else 2
    return (rows // inner, inner, columns // 2, 2)


def solution(mesh):
    split = Mesh(mesh.devices.reshape(split_shape(mesh)), GX_GY)
    placed = (
        P(GX, GY, None, None),
        P(GX, GY, None, None),
        P(GX, GY, None, None),
        P(GX, GY, None, None),
        P(GX_GY, None),
        P(GX, GY, None, None),
        P(GX, GY, None, None),
        P(GX, GY, None, None),
        P(GX, GY, None),
        P(GX, GY, None),
    )
    return jax.shard_map(
        step,
        mesh=split,
        in_specs=placed,
        out_specs=(P(GX, GY, None, None), P(GX, GY, None, None)),
        check_vma=False,
    )
```

time: 158 us -> 135 us (0.85)
  blocking collectives: 60.9 us -> 33.2 us
  local copies, waits for them, and re-layouts: 17.1 us -> 0.01 us
  waiting for transfers between devices: 8.37 us -> 17.7 us
  starting transfers between devices: 51.7 us -> 60.3 us
  Pallas kernels: 16.2 us -> 21.8 us
    all_to_all x3, blocking collectives: 60.9 us -> 33.2 us  [the longest x2 23.9 us: step(): partial = lax.all_to_all(partial, axis, 0, 0, tiled=True)]
    unnamed x69 -> x4, local copies, waits for them, and re-layouts: 16.5 us -> 0.01 us
    all_to_all x2 -> x3, waiting for transfers between devices: 0.01 us -> 11.5 us  [the longest x1 7.02 us: step(): parts = lax.all_to_all(parts, GY, 0, 0, tiled=True)]
    all_to_all x2 -> x3, starting transfers between devices: 29 us -> 37.3 us  [the longest x1 15.1 us: step(): gathered = lax.all_to_all(coarse_in, GX, 0, 0, tiled=True)]
    pallas_call x10 -> x13, Pallas kernels: 16.2 us -> 21.8 us  [call(): pl.pallas_call(kernel, out_shape=outputs, in_specs=[SMEM] * scalars + [VM...]
    ppermute x8, waiting for transfers between devices: 8.37 us -> 6.16 us  [shifted(): lax.ppermute(value, axis, [(source, source + steps) for source in range(i...]
  transfers between devices with their start and end apart: 10 -> 11, of which waited for: 5 -> 5; matrix products, arithmetic and copies ran while one was open for 0% -> 0% of each run, Pallas kernels for 6% -> 10%
where the time goes in v2:
time: 135 us; the launch traced here: 134 us
  starting transfers between devices  60.3 us (45%)
  blocking collectives  33.2 us (25%)
  Pallas kernels  21.8 us (16%)
  waiting for transfers between devices  17.7 us (13%)
    all_to_all x2, blocking collectives, step(): partial = lax.all_to_all(partial, axis, 0, 0, tiled=True)  23.9 us
    ppermute x8, starting transfers between devices, shifted(): lax.ppermute(value, axis, [(source, source + steps) for source in range(i...  23 us
    pallas_call x13, Pallas kernels, call(): pl.pallas_call(kernel, out_shape=outputs, in_specs=[SMEM] * scalars + [VM...  21.8 us
    all_to_all x1, starting transfers between devices, step(): gathered = lax.all_to_all(coarse_in, GX, 0, 0, tiled=True)  15.1 us
    all_to_all x1, starting transfers between devices, step(): blocks = lax.all_to_all(blocks, GX, 0, 0, tiled=True)  13.7 us
    all_to_all x1, blocking collectives, step(): sums = lax.all_to_all(partial, GY[0], 0, 0, tiled=True)  9.31 us
    all_to_all x1, starting transfers between devices, step(): parts = lax.all_to_all(parts, GY, 0, 0, tiled=True)  8.52 us
    all_to_all x1, waiting for transfers between devices, step(): parts = lax.all_to_all(parts, GY, 0, 0, tiled=True)  7.02 us
  transfers between devices with their start and end apart: 11, of which 5 were waited for; matrix products, arithmetic and copies ran while one was open for 0% of the time, Pallas kernels for 10%

profile of v2, /device:TPU:1, one launch (start us, length us, event | category | flops | bytes accessed | tf_op | source)
XLA Modules:
  0.0 133.8 jit_solution(12027242218646419726)
XLA Ops:
  0.6 1.7 %shard_map.114 = (f32[192,128]{1,0:T(8,128)S(1)}, f32[192,128]{1,0:T(8,128)S(1)}, f32[256,384]{1,0:T(8,128)}) custom-call(f32[384,128]{1,0:T(8,128)} %bitcast.36, f32[3,1536]{1,0:T(4,128)} %coarse_hbm.1), custom_call_target="tpu_custom_call" | custom-call | flops 14155776 | tf_op jit(solution)/shard_map/pallas_call | solution.py:432
  2.4 13.7 %all-to-all-start = ((f32[32,8,384]{2,1,0:T(8,128)}), f32[32,8,384]{2,1,0:T(8,128)S(1)}, u32[]{:S(2)}, u32[]{:S(2)}) async-start(f32[32,8,384]{2,1,0:T(8,128)} %bitcast.7), calls=%async_computation | async-start | bytes 786432 | tf_op jit(solution)/shard_map/all_to_all | solution.py:480
  16.1 3.1 %collective-permute-start = (f32[192,128]{1,0:T(8,128)S(1)}, f32[192,128]{1,0:T(8,128)S(1)}, u32[]{:S(2)}, u32[]{:S(2)}) collective-permute-start(f32[192,128]{1,0:T(8,128)S(1)} %get-tuple-element.36.gap_down), channel_id=1, source_target_pairs={{0,16},{16,32},{32,48},{48,64},{64,80},{80,96},{96,112},{112,128},... | collective-permute-start | bytes 294920 | tf_op jit(solution)/shard_map/ppermute | solution.py:25
  19.2 4.6 %collective-permute-start.1 = (f32[192,128]{1,0:T(8,128)S(1)}, f32[192,128]{1,0:T(8,128)S(1)}, u32[]{:S(2)}, u32[]{:S(2)}) collective-permute-start(f32[192,128]{1,0:T(8,128)S(1)} %get-tuple-element.37.gap_right), channel_id=1, source_target_pairs={{0,1},{1,2},{2,3},{3,4},{4,5},{5,6},{6,7},{7,8},{8,9},{9,10},{10,1... | collective-permute-start | bytes 294920 | tf_op jit(solution)/shard_map/ppermute | solution.py:25
  23.9 0.0 copy-start
  23.9 3.1 %shard_map.113 = (bf16[768,768]{1,0:T(8,128)(2,1)S(1)}, bf16[768,768]{1,0:T(8,128)(2,1)S(1)}, f32[8,768]{1,0:T(8,128)S(1)}, f32[8,768]{1,0:T(8,128)S(1)}, f32[768,8]{1,0:T(8,128)S(1)}) custom-call(s32[1,4]{1,0:T(1,128)} %bitcast.44, s32[4,192]{1,0:T(4,128)} %bitcast.42, s32[1,768]{1,0:T(1,128)} %bitcast.43, f32[3,1,768]{2,1,0:T(1,128)} %bitcast.41, ...), custom_call_target="tpu_custom_call" | custom-call | flops 905969664 | tf_op jit(solution)/shard_map/pallas_call | solution.py:432
  26.9 0.0 collective-permute-done.above
  26.9 0.0 collective-permute-done.1.left
  27.0 0.0 copy-done
  27.0 1.7 %shard_map.116 = (f32[208,128]{1,0:T(8,128)S(1)}, f32[240,128]{1,0:T(8,128)S(1)}, f32[208,128]{1,0:T(8,128)S(1)}, f32[240,128]{1,0:T(8,128)S(1)}, f32[768,128]{1,0:T(8,128)S(1)}, /*index=5*/f32[384,128]{1,0:T(8,128)S(1)}) custom-call(f32[192,128]{1,0:T(8,128)S(1)} %get-tuple-element.36.gap_down, f32[192,128]{1,0:T(8,128)S(1)} %get-tuple-element.37.gap_right, ...), custom_call_target="tpu_custom_call" | custom-call | flops 452984832 | tf_op jit(solution)/shard_map/pallas_call | solution.py:432
  28.7 3.1 %collective-permute-start.2 = (f32[240,128]{1,0:T(8,128)S(1)}, f32[240,128]{1,0:T(8,128)S(1)}, u32[]{:S(2)}, u32[]{:S(2)}) collective-permute-start(f32[240,128]{1,0:T(8,128)S(1)} %get-tuple-element.42), channel_id=1, source_target_pairs={{0,16},{16,32},{32,48},{48,64},{64,80},{80,96},{96,112},{112,128},... | collective-permute-start | bytes 368648 | tf_op jit(solution)/shard_map/ppermute | solution.py:25
  31.8 3.1 %collective-permute-start.4 = (f32[240,128]{1,0:T(8,128)S(1)}, f32[240,128]{1,0:T(8,128)S(1)}, u32[]{:S(2)}, u32[]{:S(2)}) collective-permute-start(f32[240,128]{1,0:T(8,128)S(1)} %get-tuple-element.44), channel_id=1, source_target_pairs={{0,1},{1,2},{2,3},{3,4},{4,5},{5,6},{6,7},{7,8},{8,9},{9,10},{10,1... | collective-permute-start | bytes 368648 | tf_op jit(solution)/shard_map/ppermute | solution.py:25
  34.9 1.3 collective-permute-start.3
  36.2 1.9 %collective-permute-start.5 = (f32[208,128]{1,0:T(8,128)S(1)}, f32[208,128]{1,0:T(8,128)S(1)}, u32[]{:S(2)}, u32[]{:S(2)}) collective-permute-start(f32[208,128]{1,0:T(8,128)S(1)} %get-tuple-element.45), channel_id=1, source_target_pairs={{1,0},{2,1},{3,2},{4,3},{5,4},{6,5},{7,6},{8,7},{9,8},{10,9},{11,1... | collective-permute-start | bytes 319496 | tf_op jit(solution)/shard_map/ppermute | solution.py:25
  38.1 3.2 %collective-permute-done.3.below = f32[208,128]{1,0:T(8,128)S(1)} collective-permute-done((f32[208,128]{1,0:T(8,128)S(1)}, f32[208,128]{1,0:T(8,128)S(1)}, u32[]{:S(2)}, u32[]{:S(2)}) %collective-permute-start.3) | collective-permute-done | bytes 106528 | tf_op jit(solution)/shard_map/ppermute | solution.py:25
  41.3 0.9 collective-permute-done.5.right
  42.2 0.0 collective-permute-done.2.above
  42.2 0.0 collective-permute-done.4.left
  42.2 1.0 shard_map.117
  43.2 0.0 all-to-all-done
  43.2 15.1 %all-to-all-start.1 = ((f32[32,8,128]{2,1,0:T(8,128)}), f32[32,8,128]{2,1,0:T(8,128)S(1)}, u32[]{:S(2)}, u32[]{:S(2)}) async-start(f32[32,8,128]{2,1,0:T(8,128)} %bitcast.11), calls=%async_computation.1 | async-start | bytes 262144 | tf_op jit(solution)/shard_map/all_to_all | solution.py:523
  58.3 0.0 copy-start.1
  58.3 4.8 %shard_map.115 = (bf16[768,768]{1,0:T(8,128)(2,1)}, bf16[768,768]{1,0:T(8,128)(2,1)}, f32[256,256]{1,0:T(8,128)S(1)}) custom-call(s32[1]{0:T(128)} %bitcast.here, f32[8,768]{1,0:T(8,128)S(1)} %get-tuple-element.32.link_rows, bf16[768,768]{1,0:T(8,128)(2,1)S(1)} %get-tuple-element.33.place, f32[256,384]{1,0:T(8,128)S(1)} %bitcast.28, bf16[768,768]{1,0:T(8,128)(2,1)} %bitcast.40), custom_call_target="tpu_custom_call" | custom-call | flops 1811939328 | tf_op jit(solution)/shard_map/pallas_call | solution.py:432
  63.1 4.5 %all-to-all-done.1 = f32[32,8,128]{2,1,0:T(8,128)S(1)} async-done(((f32[32,8,128]{2,1,0:T(8,128)}), f32[32,8,128]{2,1,0:T(8,128)S(1)}, u32[]{:S(2)}, u32[]{:S(2)}) %all-to-all-start.1) | async-done | bytes 131104 | tf_op jit(solution)/shard_map/all_to_all | solution.py:523
  67.6 1.0 shard_map.118
  68.7 8.5 %all-to-all-start.2 = ((f32[16,16,128]{2,1,0:T(8,128)}), f32[16,16,128]{2,1,0:T(8,128)S(1)}, u32[]{:S(2)}, u32[]{:S(2)}) async-start(f32[16,16,128]{2,1,0:T(8,128)} %bitcast.13), calls=%async_computation.2 | async-start | bytes 262144 | tf_op jit(solution)/shard_map/all_to_all | solution.py:539
  77.2 0.0 copy-done.1
  77.2 1.8 %shard_map.119 = (bf16[768,128]{1,0:T(8,128)(2,1)S(1)}, bf16[768,128]{1,0:T(8,128)(2,1)S(1)}, f32[32,768]{1,0:T(8,128)S(1)}, f32[8,128]{1,0:T(8,128)S(1)}) custom-call(f32[240,128]{1,0:T(8,128)S(1)} %collective-permute-done.2.above, f32[208,128]{1,0:T(8,128)S(1)} %collective-permute-done.3.below, f32[240,128]{1,0:T(8,128)S(1)} %collective-permute-done.4.left, ...), custom_call_target="tpu_custom_call" | custom-call | flops 905969664 | tf_op jit(solution)/shard_map/pallas_call | solution.py:432
  79.0 7.0 %all-to-all-done.2 = f32[16,16,128]{2,1,0:T(8,128)S(1)} async-done(((f32[16,16,128]{2,1,0:T(8,128)}), f32[16,16,128]{2,1,0:T(8,128)S(1)}, u32[]{:S(2)}, u32[]{:S(2)}) %all-to-all-start.2) | async-done | bytes 131104 | tf_op jit(solution)/shard_map/all_to_all | solution.py:539
  86.1 2.2 %shard_map.120 = (f32[768,128]{1,0:T(8,128)S(1)}, f32[128,128]{1,0:T(8,128)S(1)}) custom-call(f32[256,128]{1,0:T(8,128)S(1)} %bitcast.27, f32[768,128]{1,0:T(8,128)S(1)} %get-tuple-element.47.precond, bf16[768,128]{1,0:T(8,128)(2,1)S(1)} %get-tuple-element.50.mode_six, f32[32,768]{1,0:T(8,128)S(1)} %get-tuple-element.51.forms, ...), custom_call_target="tpu_custom_call" | custom-call | flops 452984832 | tf_op jit(solution)/shard_map/pallas_call | solution.py:432
  88.2 10.4 %all_to_all.66 = f32[16,8,128]{2,1,0:T(8,128)S(1)} all-to-all(f32[16,8,128]{2,1,0:T(8,128)S(1)} %bitcast.32), channel_id=1, replica_groups=mesh['gx_0'=8,'gx_1'=4,'gy_0'=8,'gy_1'=2] {'gy_0','gy_1'}, dimensions={0} | all-to-all | bytes 131072 | tf_op jit(solution)/shard_map/all_to_all | solution.py:552
  98.7 13.5 %all_to_all.67 = f32[32,8,128]{2,1,0:T(8,128)S(1)} all-to-all(f32[32,8,128]{2,1,0:T(8,128)S(1)} %bitcast.25), channel_id=1, replica_groups=mesh['gx_0'=8,'gx_1'=4,'gy_0'=8,'gy_1'=2] {'gx_0','gx_1'}, dimensions={0} | all-to-all | bytes 262144 | tf_op jit(solution)/shard_map/all_to_all | solution.py:552
  112.2 9.3 %all_to_all.68 = f32[8,8,128]{2,1,0:T(8,128)S(1)} all-to-all(f32[8,8,128]{2,1,0:T(8,128)S(1)} %bitcast.31), channel_id=1, replica_groups=mesh['gx_0'=8,'gx_1'=4,'gy_0'=8,'gy_1'=2] {'gy_0'}, dimensions={0} | all-to-all | bytes 65536 | tf_op jit(solution)/shard_map/all_to_all | solution.py:559
  121.5 3.0 %shard_map.123 = (f32[192,128]{1,0:T(8,128)S(1)}, f32[192,128]{1,0:T(8,128)S(1)}, f32[384,128]{1,0:T(8,128)S(1)}, f32[384,128]{1,0:T(8,128)S(1)}, f32[8,128]{1,0:T(8,128)S(1)}) custom-call(f32[64,128]{1,0:T(8,128)S(1)} %bitcast.30, f32[768,128]{1,0:T(8,128)S(1)} %get-tuple-element.54.projected, bf16[768,128]{1,0:T(8,128)(2,1)S(1)} %get-tuple-element.55.search_six, ...), custom_call_target="tpu_custom_call" | custom-call | flops 452984832 | tf_op jit(solution)/shard_map/pallas_call | solution.py:432
  124.5 1.3 collective-permute-start.6
  125.8 4.5 %collective-permute-start.7 = (f32[192,128]{1,0:T(8,128)S(1)}, f32[192,128]{1,0:T(8,128)S(1)}, u32[]{:S(2)}, u32[]{:S(2)}) collective-permute-start(f32[192,128]{1,0:T(8,128)S(1)} %get-tuple-element.61), channel_id=1, source_target_pairs={{1,0},{2,1},{3,2},{4,3},{5,4},{6,5},{7,6},{8,7},{9,8},{10,9},{11,1... | collective-permute-start | bytes 294920 | tf_op jit(solution)/shard_map/ppermute | solution.py:25
  130.4 0.7 shard_map.124
  131.1 0.0 collective-permute-done.6.below
  131.1 2.1 %collective-permute-done.7.right = f32[192,128]{1,0:T(8,128)S(1)} collective-permute-done((f32[192,128]{1,0:T(8,128)S(1)}, f32[192,128]{1,0:T(8,128)S(1)}, u32[]{:S(2)}, u32[]{:S(2)}) %collective-permute-start.7) | collective-permute-done | bytes 98336 | tf_op jit(solution)/shard_map/ppermute | solution.py:25
  133.1 0.7 shard_map.125
  (2 shorter events, 0.1 us)
Async XLA Ops:
  2.4 40.8 %all-to-all-start = ((f32[32,8,384]{2,1,0:T(8,128)}), f32[32,8,384]{2,1,0:T(8,128)S(1)}, u32[]{:S(2)}, u32[]{:S(2)}) async-start(f32[32,8,384]{2,1,0:T(8,128)} %bitcast.7), calls=%async_computation | async-start | bytes 786432 | tf_op jit(solution)/shard_map/all_to_all | solution.py:480
  16.1 10.8 %collective-permute-start = (f32[192,128]{1,0:T(8,128)S(1)}, f32[192,128]{1,0:T(8,128)S(1)}, u32[]{:S(2)}, u32[]{:S(2)}) collective-permute-start(f32[192,128]{1,0:T(8,128)S(1)} %get-tuple-element.36.gap_down), channel_id=1, source_target_pairs={{0,16},{16,32},{32,48},{48,64},{64,80},{80,96},{96,112},{112,128},... | collective-permute-start | bytes 294920 | tf_op jit(solution)/shard_map/ppermute | solution.py:25
  19.2 7.7 %collective-permute-start.1 = (f32[192,128]{1,0:T(8,128)S(1)}, f32[192,128]{1,0:T(8,128)S(1)}, u32[]{:S(2)}, u32[]{:S(2)}) collective-permute-start(f32[192,128]{1,0:T(8,128)S(1)} %get-tuple-element.37.gap_right), channel_id=1, source_target_pairs={{0,1},{1,2},{2,3},{3,4},{4,5},{5,6},{6,7},{7,8},{8,9},{9,10},{10,1... | collective-permute-start | bytes 294920 | tf_op jit(solution)/shard_map/ppermute | solution.py:25
  23.9 3.1 %copy-start = (f32[1,1,16,384]{3,2,1,0:T(8,128)S(1)}, f32[1,1,16,384]{3,2,1,0:T(8,128)}, u32[]{:S(2)}) copy-start(f32[1,1,16,384]{3,2,1,0:T(8,128)} %param.15) | copy-start | bytes 73732
  28.7 13.5 %collective-permute-start.2 = (f32[240,128]{1,0:T(8,128)S(1)}, f32[240,128]{1,0:T(8,128)S(1)}, u32[]{:S(2)}, u32[]{:S(2)}) collective-permute-start(f32[240,128]{1,0:T(8,128)S(1)} %get-tuple-element.42), channel_id=1, source_target_pairs={{0,16},{16,32},{32,48},{48,64},{64,80},{80,96},{96,112},{112,128},... | collective-permute-start | bytes 368648 | tf_op jit(solution)/shard_map/ppermute | solution.py:25
  31.8 10.4 %collective-permute-start.4 = (f32[240,128]{1,0:T(8,128)S(1)}, f32[240,128]{1,0:T(8,128)S(1)}, u32[]{:S(2)}, u32[]{:S(2)}) collective-permute-start(f32[240,128]{1,0:T(8,128)S(1)} %get-tuple-element.44), channel_id=1, source_target_pairs={{0,1},{1,2},{2,3},{3,4},{4,5},{5,6},{6,7},{7,8},{8,9},{9,10},{10,1... | collective-permute-start | bytes 368648 | tf_op jit(solution)/shard_map/ppermute | solution.py:25
  34.9 6.4 %collective-permute-start.3 = (f32[208,128]{1,0:T(8,128)S(1)}, f32[208,128]{1,0:T(8,128)S(1)}, u32[]{:S(2)}, u32[]{:S(2)}) collective-permute-start(f32[208,128]{1,0:T(8,128)S(1)} %get-tuple-element.43), channel_id=1, source_target_pairs={{16,0},{32,16},{48,32},{64,48},{80,64},{96,80},{112,96},{128,112},... | collective-permute-start | bytes 319496 | tf_op jit(solution)/shard_map/ppermute | solution.py:25
  36.2 6.0 %collective-permute-start.5 = (f32[208,128]{1,0:T(8,128)S(1)}, f32[208,128]{1,0:T(8,128)S(1)}, u32[]{:S(2)}, u32[]{:S(2)}) collective-permute-start(f32[208,128]{1,0:T(8,128)S(1)} %get-tuple-element.45), channel_id=1, source_target_pairs={{1,0},{2,1},{3,2},{4,3},{5,4},{6,5},{7,6},{8,7},{9,8},{10,9},{11,1... | collective-permute-start | bytes 319496 | tf_op jit(solution)/shard_map/ppermute | solution.py:25
  43.2 24.5 %all-to-all-start.1 = ((f32[32,8,128]{2,1,0:T(8,128)}), f32[32,8,128]{2,1,0:T(8,128)S(1)}, u32[]{:S(2)}, u32[]{:S(2)}) async-start(f32[32,8,128]{2,1,0:T(8,128)} %bitcast.11), calls=%async_computation.1 | async-start | bytes 262144 | tf_op jit(solution)/shard_map/all_to_all | solution.py:523
  58.3 18.9 %copy-start.1 = (f32[1,1,16,384]{3,2,1,0:T(8,128)S(1)}, f32[1,1,16,384]{3,2,1,0:T(8,128)}, u32[]{:S(2)}) copy-start(f32[1,1,16,384]{3,2,1,0:T(8,128)} %param.16) | copy-start | bytes 73732
  68.7 17.4 %all-to-all-start.2 = ((f32[16,16,128]{2,1,0:T(8,128)}), f32[16,16,128]{2,1,0:T(8,128)S(1)}, u32[]{:S(2)}, u32[]{:S(2)}) async-start(f32[16,16,128]{2,1,0:T(8,128)} %bitcast.13), calls=%async_computation.2 | async-start | bytes 262144 | tf_op jit(solution)/shard_map/all_to_all | solution.py:539
  124.5 6.5 %collective-permute-start.6 = (f32[192,128]{1,0:T(8,128)S(1)}, f32[192,128]{1,0:T(8,128)S(1)}, u32[]{:S(2)}, u32[]{:S(2)}) collective-permute-start(f32[192,128]{1,0:T(8,128)S(1)} %get-tuple-element.60), channel_id=1, source_target_pairs={{16,0},{32,16},{48,32},{64,48},{80,64},{96,80},{112,96},{128,112},... | collective-permute-start | bytes 294920 | tf_op jit(solution)/shard_map/ppermute | solution.py:25
  125.8 7.3 %collective-permute-start.7 = (f32[192,128]{1,0:T(8,128)S(1)}, f32[192,128]{1,0:T(8,128)S(1)}, u32[]{:S(2)}, u32[]{:S(2)}) collective-permute-start(f32[192,128]{1,0:T(8,128)S(1)} %get-tuple-element.61), channel_id=1, source_target_pairs={{1,0},{2,1},{3,2},{4,3},{5,4},{6,5},{7,6},{8,7},{9,8},{10,9},{11,1... | collective-permute-start | bytes 294920 | tf_op jit(solution)/shard_map/ppermute | solution.py:25

commit v3 on v2

--- a/solution.py
+++ b/solution.py
@@ -44,6 +44,18 @@
 def dot_exact(a, b):
     return lax.dot_general(
         a, b, (((1,), (0,)), ((), ())), precision=HIGHEST, preferred_element_type=F32
+    )
+
+
+def dot_exact_nt(a, b):
+    return lax.dot_general(
+        a, b, (((1,), (1,)), ((), ())), precision=HIGHEST, preferred_element_type=F32
+    )
+
+
+def tiled_columns(rows):
+    return lax.dot_general(
+        rows, tile_matrix(), (((0,), (0,)), ((), ())), precision=HIGHEST, preferred_element_type=F32
     )
 
 
@@ -100,40 +112,17 @@
     return pltpu.roll(x, start, 1) if start else x
 
 
-def first_kernel(windows, gap_hbm, coarse_hbm, down, right, blocks, coarse, wide, arrived):
-    width = down.shape[0]
-    copies = [
-        pltpu.make_async_copy(source, target, arrived.at[n])
-        for n, (source, target) in enumerate(
-            (
-                (coarse_hbm, coarse),
-                (gap_hbm.at[pl.ds(0, width)], down),
-                (gap_hbm.at[pl.ds(width, width)], right),
-            )
-        )
-    ]
-    for copy in copies:
-        copy.start()
-    wide[...] = jnp.zeros_like(wide)
-    copies[0].wait()
-    wide[0:3, :] = coarse[...]
-    for i, start in enumerate(windows):
-        blocks[8 * i : 8 * i + 8, :] = wide[:, start : start + blocks.shape[1]]
-    copies[1].wait()
-    copies[2].wait()
-
-
 def prepare_kernel(
-    count_hbm, slots_hbm, mult_hbm, modes_hbm, schur_hbm,
-    place, pick_schur, mode_rows, link_rows, columns,
-    buffer, slots, mult, modes, schur, count, arrived,
+    windows, count_hbm, slots_hbm, mult_hbm, modes_hbm, schur_hbm, coarse_hbm,
+    place, pick_schur, mode_rows, link_rows, columns, blocks,
+    buffer, slots, mult, modes, schur, coarse, wide, count, arrived,
 ):
     copies = [
         pltpu.make_async_copy(source, target, arrived.at[n])
         for n, (source, target) in enumerate(
             (
                 (count_hbm, count), (slots_hbm, slots), (mult_hbm, mult), (modes_hbm, modes),
-                (schur_hbm, schur),
+                (schur_hbm, schur), (coarse_hbm, coarse),
             )
         )
     ]
@@ -142,6 +131,7 @@
     width = slots.shape[1]
     total = 4 * width
     buffer[...] = jnp.zeros_like(buffer)
+    wide[...] = jnp.zeros_like(wide)
     lane = lax.broadcasted_iota(jnp.int32, (1, total), 1)
     copies[0].wait()
     copies[1].wait()
@@ -155,8 +145,7 @@
         sign_row = jnp.where(inside, SIGNS[f], sign_row)
     copies[2].wait()
     weights = 1.0 / mult[...].astype(F32)
-    down = lax.broadcasted_iota(jnp.int32, (total, total), 0).astype(F32)
-    place_value = jnp.where(down == slot_row, sign_row, 0.0).astype(BF16)
+    place_value = placing(slot_row, sign_row)
     place[...] = place_value
     copies[3].wait()
     buffer[...] = jnp.zeros_like(buffer)
@@ -174,8 +163,18 @@
     cols = jnp.transpose(buffer[...])
     columns[...] = cols
     pick_value = picking(cols)
+    copies[5].wait()
+    wide[0:3, :] = coarse[...]
+    for i, start in enumerate(windows):
+        blocks[8 * i : 8 * i + 8, :] = wide[:, start : start + blocks.shape[1]]
     copies[4].wait()
     pick_schur[...] = dot(pick_value, schur[...]).astype(BF16)
+
+
+def placing(slot_row, sign_row):
+    total = slot_row.shape[1]
+    down = lax.broadcasted_iota(jnp.int32, (total, total), 0).astype(F32)
+    return jnp.where(down == slot_row, sign_row, 0.0).astype(BF16)
 
 
 def picking(cols):
@@ -256,14 +255,13 @@
 
 def tables_kernel(
     above, below, left, right, mode_rows, link_rows, saved, images, residual, precond, link_flex_hbm,
-    mode_six, search_six, forms, sums,
+    mode_six, search_rows, base, mode_forms,
     link_flex, arrived,
 ):
     load = pltpu.make_async_copy(link_flex_hbm, link_flex, arrived.at[0])
     load.start()
     total = mode_rows.shape[1]
     width = total // 4
-    tiles = tile_matrix()
     near = lax.broadcasted_iota(jnp.int32, (1, 256), 1) < width
     used = link_rows[1:2, :] != 0.0
     row = lax.broadcasted_iota(jnp.int32, (16, total), 0)
@@ -276,9 +274,8 @@
         theirs = jnp.where(row < 3, theirs, 0.0)
         modes = modes + pltpu.roll(theirs, 3 * (1 + f), 0)
     modes = jnp.where(used, modes, 0.0)
-    mode_six[...] = six_left(
-        lax.dot_general(modes, tiles, (((0,), (0,)), ((), ())), precision=HIGHEST, preferred_element_type=F32)
-    )
+    modes_tiled = tiled_columns(modes)
+    mode_six[...] = six_left(modes_tiled)
     search = jnp.zeros((16, total), F32)
     for f in range(4):
         if f % 2 == 0:
@@ -290,33 +287,34 @@
             piece = lane_window(saved[...], 0 if f == 1 else width, 256)
         search = search + at_lanes(widened(jnp.where(near, piece, 0.0), total), width * f)
     search = jnp.where(used, search, 0.0)
-    search_tiled = lax.dot_general(
-        search, tiles, (((0,), (0,)), ((), ())), precision=HIGHEST, preferred_element_type=F32
-    )
-    search_six[...] = six_left(search_tiled)
+    search_rows[...] = search
     lanes = lax.broadcasted_iota(jnp.int32, (16, total), 1)
     image = widened(images[...], total)
-    image_down = at_lanes(image, width)
-    image_right = at_lanes(image, 2 * width)
-    forms[0:16, :] = jnp.where(
+    image = jnp.where(
         (lanes >= width) & (lanes < 2 * width),
-        image_down,
-        jnp.where(lanes >= 3 * width, image_right, 0.0),
-    )
-    energy = jnp.sum(residual[0:width] * precond[width : 2 * width], axis=0, keepdims=True) + jnp.sum(
-        residual[width:] * precond[3 * width :], axis=0, keepdims=True
+        at_lanes(image, width),
+        jnp.where(lanes >= 3 * width, at_lanes(image, 2 * width), 0.0),
     )
     load.wait()
-    flex_search = select_lanes(search, link_flex[...])
-    forms[16:32, :] = flex_search
-    products = dot_exact(flex_search, search_tiled)
+    flexed = select_lanes(jnp.concatenate([search, modes], axis=0), link_flex[...])
+    forms = jnp.concatenate([image, flexed], axis=0)
+    full = precond[...]
+    base[0:48, :] = dot_exact(forms, full)
+    mode_forms[...] = six_left(dot_exact(forms, modes_tiled))
+    high, mid, _ = split3(full)
+    applied = dot(link_flex[...], jnp.concatenate([high, mid], axis=1))
+    square = jnp.sum(full * (applied[:, :128] + applied[:, 128:]), axis=0, keepdims=True)
+    products = dot_exact(dot_exact_nt(flexed[0:16], search), tile_matrix())
     group = lax.broadcasted_iota(jnp.int32, (16, 128), 1) // 16
     part = lax.broadcasted_iota(jnp.int32, (16, 128), 0)
     products = jnp.where(group == part % 8, products, 0.0)
-    sums[...] = jnp.concatenate(
+    energy = jnp.sum(residual[0:width] * full[width : 2 * width], axis=0, keepdims=True) + jnp.sum(
+        residual[width:] * full[3 * width :], axis=0, keepdims=True
+    )
+    base[48:56, :] = jnp.concatenate(
         [
             energy,
-            jnp.zeros((1, 128), F32),
+            square,
             jnp.sum(products[0:8], axis=0, keepdims=True),
             jnp.sum(products[8:16], axis=0, keepdims=True),
             jnp.zeros((4, 128), F32),
@@ -336,22 +334,14 @@
     return out
 
 
-def project_kernel(
-    chunk, arrived, precond, mode_six, forms, sums, link_flex_hbm, projected, partial,
-    link_flex, copied,
-):
-    load = pltpu.make_async_copy(link_flex_hbm, link_flex, copied.at[0])
-    load.start()
-    links = precond[...] - dot(mode_six[...], six_right(block_sum(arrived, 16)))
-    projected[...] = links
-    linear = dot_exact(forms[...], links)
-    high, mid, _ = split3(links)
-    parts = jnp.concatenate([high, mid], axis=1)
-    load.wait()
-    image = dot(link_flex[...], parts)
-    square = jnp.sum(links * (image[:, :128] + image[:, 128:]), axis=0, keepdims=True)
+def project_kernel(chunk, arrived, base, mode_forms, amplitudes, partial):
+    y = block_sum(arrived, 16)
+    amplitudes[...] = y
+    moved = dot(mode_forms[...], six_right(y))
+    linear = base[0:32] - moved[0:32]
+    square = jnp.sum(y * (moved[32:48] - 2.0 * base[32:48]), axis=0, keepdims=True)
     row = lax.broadcasted_iota(jnp.int32, (8, 128), 0)
-    last = jnp.where(row == 1, square, sums[...])
+    last = base[48:56] + jnp.where(row == 1, square, 0.0)
     padding = jnp.zeros((partial.shape[0] // 2 - 40, 128), F32)
     full = jnp.concatenate([linear, last, padding], axis=0)
     for j in range(partial.shape[0] // chunk):
@@ -359,45 +349,54 @@
         partial[chunk * j : chunk * j + chunk, :] = full[at : at + chunk]
 
 
+def own_rows(x, width):
+    return jnp.concatenate([x[width : 2 * width], x[3 * width :]], axis=0)
+
+
+def lift_kernel(
+    amplitudes, precond, mode_six, search_rows, link_rows,
+    slot_values, slot_six, link_values, link_six,
+):
+    links = precond[...] - dot(mode_six[...], six_right(amplitudes[...]))
+    width = links.shape[0] // 4
+    link_values[...] = own_rows(links, width)
+    search = search_rows[...]
+    link_six[...] = six_left(own_rows(tiled_columns(search), width))
+    place = placing(link_rows[0:1], link_rows[1:2])
+    slot_values[...] = select_rows(place, links)
+    parts = dot_nt(jnp.concatenate(split3(search), axis=0), place)
+    slot_six[...] = six_left(tiled_columns(parts[0:16] + (parts[16:32] + parts[32:48])))
+
+
 def spread_sum_kernel(height, arrived, partial):
     out = block_sum(arrived, height)
     for i in range(partial.shape[0] // height):
         partial[height * i : height * i + height, :] = out
 
 
-def search_kernel(
-    sums, projected, search_six, place, pick_flex_hbm,
-    up_msg, left_msg, own, search_own, step,
-    pick_flex, arrived,
-):
-    load = pltpu.make_async_copy(pick_flex_hbm, pick_flex, arrived.at[0])
-    load.start()
+def search_kernel(sums, slot_values, slot_six, pick_flex, up_msg, left_msg, own):
     width = up_msg.shape[0]
+    lifted = slot_values[...] - dot(slot_six[...], six_right(sums[0:16]))
+    image = dot(pick_flex[...], lifted.astype(BF16))
+    up_msg[...] = image[0:width]
+    left_msg[...] = image[2 * width : 3 * width]
+    own[...] = own_rows(image, width)
+
+
+def multiply_kernel(sums, link_values, link_six, multipliers, step):
     intersect = sums[0:16]
     cross = sums[16:32]
     energy = sums[32:33]
     square = sums[33:34]
-    search = projected[...] - dot(search_six[...], six_right(intersect))
-    lifted = select_rows(place[...], search).astype(BF16)
-    load.wait()
-    image = dot(pick_flex[...], lifted)
-    up_msg[...] = image[0:width]
-    own[0:width, :] = image[width : 2 * width]
-    left_msg[...] = image[2 * width : 3 * width]
-    own[width:, :] = image[3 * width :]
-    search_own[0:width, :] = search[width : 2 * width]
-    search_own[width:, :] = search[3 * width :]
     group = lax.broadcasted_iota(jnp.int32, (16, 128), 1) // 16
     part = lax.broadcasted_iota(jnp.int32, (16, 128), 0)
     packed = jnp.where(part < 8, sums[34:35], sums[35:36])
     packed = jnp.where(group == part % 8, packed, 0.0)
     products = dot_exact(packed, jnp.concatenate([intersect] * 8, axis=0))
     curvature = square + jnp.sum(intersect * (products - 2.0 * cross), axis=0, keepdims=True)
-    step[...] = jnp.broadcast_to(energy / curvature, step.shape)
-
-
-def multiply_kernel(search_own, step, multipliers):
-    multipliers[...] = step[0:1] * search_own[...]
+    size = energy / curvature
+    step[...] = jnp.broadcast_to(size, step.shape)
+    multipliers[...] = size * (link_values[...] - dot(link_six[...], six_right(intersect)))
 
 
 def residual_kernel(before, own, below, right, step, residual):
@@ -466,30 +465,24 @@
     here = lax.axis_index(GX).reshape(1)
     big = (total, total)
     cube = 2 * total**3
-    gap_down, gap_right, blocks = call(
-        functools.partial(first_kernel, windows),
-        (gap, coarse_inverse),
-        (((width, cases), F32), ((width, cases), F32), ((8 * rows, window), F32)),
-        remote=2,
-        scratch=((coarse_inverse.shape, F32), ((8, unknowns), F32)),
-        copies=3,
-        flops=cube // 64,
-    )
+    gap_down = gap[:width]
+    gap_right = gap[width:]
     above = shifted(gap_down, GX, 1)
     left = shifted(gap_right, GY, 1)
-    blocks = lax.all_to_all(blocks, GX, 0, 0, tiled=True)
-    place, pick_schur, mode_rows, link_rows, slot_cols = call(
-        prepare_kernel,
-        (count, slots, multiplicity[0], modes, schur_blocks[0, 0]),
+    place, pick_schur, mode_rows, link_rows, slot_cols, blocks = call(
+        functools.partial(prepare_kernel, windows),
+        (count, slots, multiplicity[0], modes, schur_blocks[0, 0], coarse_inverse),
         (
             (big, BF16), (big, BF16), ((8, total), F32), ((8, total), F32), ((total, 8), F32),
+            ((8 * rows, window), F32),
         ),
-        remote=5,
+        remote=6,
         scratch=(
             ((8, total), F32), (slots.shape, jnp.int32), ((1, total), jnp.int32), (modes.shape, F32),
-            (big, BF16), pltpu.SMEM((1, 4), jnp.int32),
+            (big, BF16), (coarse_inverse.shape, F32), ((8, unknowns), F32),
+            pltpu.SMEM((1, 4), jnp.int32),
         ),
-        copies=5,
+        copies=6,
         flops=cube,
     )
     up_msg, down_msg, left_msg, right_msg, own, residual = call(
@@ -503,6 +496,14 @@
     from_below = shifted(up_msg, GX, -1)
     from_left = shifted(right_msg, GY, 1)
     from_right = shifted(left_msg, GY, -1)
+    blocks = lax.all_to_all(blocks, GX, 0, 0, tiled=True)
+    precond, coarse_in = call(
+        coarse_in_kernel,
+        (own, from_above, from_below, from_left, from_right, mode_rows),
+        (((total, cases), F32), ((8 * rows, cases), F32)),
+        flops=cube // 16,
+    )
+    gathered = lax.all_to_all(coarse_in, GX, 0, 0, tiled=True)
     pick_flex, link_flex, coarse_rows = call(
         functools.partial(flex_kernel, (row_unknowns, (unknowns - window) // 128)),
         (here, link_rows, place, blocks, flex),
@@ -514,39 +515,38 @@
         hbm_out=(0, 1),
         flops=2 * cube,
     )
-    precond, coarse_in = call(
-        coarse_in_kernel,
-        (own, from_above, from_below, from_left, from_right, mode_rows),
-        (((total, cases), F32), ((8 * rows, cases), F32)),
-        flops=cube // 16,
-    )
-    gathered = lax.all_to_all(coarse_in, GX, 0, 0, tiled=True)
-    mode_six, search_six, forms, sums = call(
+    (parts,) = call(
+        coarse_kernel, (coarse_rows, gathered), (((16 * columns, cases), F32),), flops=cube // 8,
+    )
+    parts = lax.all_to_all(parts, GY, 0, 0, tiled=True)
+    mode_six, search_rows, base, mode_forms = call(
         tables_kernel,
         (
             from_above, from_below, from_left, from_right, mode_rows, link_rows, saved, images,
             residual, precond, link_flex,
         ),
-        (((total, 128), BF16), ((total, 128), BF16), ((32, total), F32), ((8, cases), F32)),
+        (((total, 128), BF16), ((16, total), F32), ((56, cases), F32), ((48, 128), BF16)),
         remote=1,
         scratch=((big, BF16),),
         copies=1,
         flops=cube,
     )
-    (parts,) = call(
-        coarse_kernel, (coarse_rows, gathered), (((16 * columns, cases), F32),), flops=cube // 8,
-    )
-    parts = lax.all_to_all(parts, GY, 0, 0, tiled=True)
     pairs = columns // 2
     chunk = -(-(-(-40 // pairs)) // 8) * 8
-    projected, partial = call(
+    amplitudes, partial = call(
         functools.partial(project_kernel, chunk),
-        (parts, precond, mode_six, forms, sums, link_flex),
-        (((total, cases), F32), ((chunk * columns, cases), F32)),
-        remote=1,
-        scratch=((big, BF16),),
-        copies=1,
-        flops=cube // 2,
+        (parts, base, mode_forms),
+        (((16, cases), F32), ((chunk * columns, cases), F32)),
+        flops=cube // 64,
+    )
+    slot_values, slot_six, link_values, link_six = call(
+        lift_kernel,
+        (amplitudes, precond, mode_six, search_rows, link_rows),
+        (
+            ((total, cases), F32), ((total, 128), BF16), ((2 * width, cases), F32),
+            ((2 * width, 128), BF16),
+        ),
+        flops=cube,
     )
     for axis, following in ((GY, rows), (GX, pairs)):
         partial = lax.all_to_all(partial, axis, 0, 0, tiled=True)
@@ -557,22 +557,19 @@
             flops=cube // 64,
         )
     sums = lax.all_to_all(partial, GY[0], 0, 0, tiled=True)
-    up_msg, left_msg, own, search_own, step = call(
+    up_msg, left_msg, own = call(
         search_kernel,
-        (sums, projected, search_six, place, pick_flex),
-        (
-            ((width, cases), F32), ((width, cases), F32), ((2 * width, cases), F32),
-            ((2 * width, cases), F32), ((8, cases), F32),
-        ),
-        remote=1,
-        scratch=((big, BF16),),
-        copies=1,
+        (sums, slot_values, slot_six, pick_flex),
+        (((width, cases), F32), ((width, cases), F32), ((2 * width, cases), F32)),
         flops=cube // 2,
     )
     from_below = shifted(up_msg, GX, -1)
     from_right = shifted(left_msg, GY, -1)
-    (multipliers,) = call(
-        multiply_kernel, (search_own, step), (((2 * width, cases), F32),), flops=cube // 64,
+    multipliers, step = call(
+        multiply_kernel,
+        (sums, link_values, link_six),
+        (((2 * width, cases), F32), ((8, cases), F32)),
+        flops=cube // 64,
     )
     (residual,) = call(
         residual_kernel,

time: 135 us -> 133 us (0.985)
  blocking collectives: 33.2 us -> 23.9 us
  waiting for transfers between devices: 17.7 us -> 23.9 us
  starting transfers between devices: 60.3 us -> 63.8 us
  Pallas kernels: 21.8 us -> 19.8 us
    all_to_all x1 -> x0, blocking collectives: 9.31 us -> none  [step(): sums = lax.all_to_all(partial, GY[0], 0, 0, tiled=True)]
    all_to_all x0 -> x1, waiting for transfers between devices: none -> 4.21 us  [step(): sums = lax.all_to_all(partial, GY[0], 0, 0, tiled=True)]
    all_to_all x0 -> x1, starting transfers between devices: none -> 3.52 us  [step(): sums = lax.all_to_all(partial, GY[0], 0, 0, tiled=True)]
    ppermute x8, waiting for transfers between devices: 6.16 us -> 8.42 us  [shifted(): lax.ppermute(value, axis, [(source, source + steps) for source in range(i...]
    pallas_call x13, Pallas kernels: 21.8 us -> 19.8 us  [call(): pl.pallas_call(kernel, out_shape=outputs, in_specs=[SMEM] * scalars + [VM...]
    ppermute x8, starting transfers between devices: 23 us -> 24.8 us  [shifted(): lax.ppermute(value, axis, [(source, source + steps) for source in range(i...]
    all_to_all x1, starting transfers between devices: 15.1 us -> 13.5 us  [step(): gathered = lax.all_to_all(coarse_in, GX, 0, 0, tiled=True)]
  transfers between devices with their start and end apart: 11 -> 12, of which waited for: 5 -> 7; matrix products, arithmetic and copies ran while one was open for 0% -> 0% of each run, Pallas kernels for 10% -> 10%
where the time goes in v3:
time: 133 us; the launch traced here: 132 us
  starting transfers between devices  63.8 us (48%)
  waiting for transfers between devices  23.9 us (18%)
  blocking collectives  23.9 us (18%)
  Pallas kernels  19.8 us (15%)
    ppermute x8, starting transfers between devices, shifted(): lax.ppermute(value, axis, [(source, source + steps) for source in range(i...  24.8 us
    all_to_all x2, blocking collectives, step(): partial = lax.all_to_all(partial, axis, 0, 0, tiled=True)  23.9 us
    pallas_call x13, Pallas kernels, call(): pl.pallas_call(kernel, out_shape=outputs, in_specs=[SMEM] * scalars + [VM...  19.8 us
    all_to_all x1, starting transfers between devices, step(): blocks = lax.all_to_all(blocks, GX, 0, 0, tiled=True)  13.7 us
    all_to_all x1, starting transfers between devices, step(): gathered = lax.all_to_all(coarse_in, GX, 0, 0, tiled=True)  13.5 us
    ppermute x8, waiting for transfers between devices, shifted(): lax.ppermute(value, axis, [(source, source + steps) for source in range(i...  8.42 us
    all_to_all x1, starting transfers between devices, step(): parts = lax.all_to_all(parts, GY, 0, 0, tiled=True)  8.22 us
    all_to_all x1, waiting for transfers between devices, step(): parts = lax.all_to_all(parts, GY, 0, 0, tiled=True)  6.24 us
  transfers between devices with their start and end apart: 12, of which 7 were waited for; matrix products, arithmetic and copies ran while one was open for 0% of the time, Pallas kernels for 10%

profile of v3, /device:TPU:1, one launch (start us, length us, event | category | flops | bytes accessed | tf_op | source)
XLA Modules:
  0.0 132.4 jit_solution(9938164381202691124)
XLA Ops:
  0.6 0.0 copy-start.3
  0.6 3.1 %shard_map.113 = (bf16[768,768]{1,0:T(8,128)(2,1)S(1)}, bf16[768,768]{1,0:T(8,128)(2,1)S(1)}, f32[8,768]{1,0:T(8,128)S(1)}, f32[8,768]{1,0:T(8,128)S(1)}, f32[768,8]{1,0:T(8,128)S(1)}, /*index=5*/f32[256,384]{1,0:T(8,128)}) custom-call(s32[1,4]{1,0:T(1,128)} %bitcast.46, s32[4,192]{1,0:T(4,128)} %bitcast.44, s32[1,768]{1,0:T(1,128)} %bitcast.45, ...), custom_call_target="tpu_custom_call" | custom-call | flops 905969664 | tf_op jit(solution)/shard_map/pallas_call | solution.py:431
  3.7 0.0 copy-start.1
  3.8 13.7 %all-to-all-start = ((f32[32,8,384]{2,1,0:T(8,128)}), f32[32,8,384]{2,1,0:T(8,128)S(1)}, u32[]{:S(2)}, u32[]{:S(2)}) async-start(f32[32,8,384]{2,1,0:T(8,128)} %bitcast.6), calls=%async_computation | async-start | bytes 786432 | tf_op jit(solution)/shard_map/all_to_all | solution.py:499
  17.5 0.0 copy-done.3
  17.5 4.0 %collective-permute-start.1 = (f32[192,128]{1,0:T(8,128)S(1)}, f32[192,128]{1,0:T(8,128)S(1)}, u32[]{:S(2)}, u32[]{:S(2)}) collective-permute-start(f32[192,128]{1,0:T(8,128)S(1)} %get-tuple-element.66.gap_right), channel_id=1, source_target_pairs={{0,1},{1,2},{2,3},{3,4},{4,5},{5,6},{6,7},{7,8},{8,9},{9,10},{10,1... | collective-permute-start | bytes 294920 | tf_op jit(solution)/shard_map/ppermute | solution.py:25
  21.6 3.4 %collective-permute-start = (f32[192,128]{1,0:T(8,128)S(1)}, f32[192,128]{1,0:T(8,128)S(1)}, u32[]{:S(2)}, u32[]{:S(2)}) collective-permute-start(f32[192,128]{1,0:T(8,128)S(1)} %get-tuple-element.67.gap_down), channel_id=1, source_target_pairs={{0,16},{16,32},{32,48},{48,64},{64,80},{80,96},{96,112},{112,128},... | collective-permute-start | bytes 294920 | tf_op jit(solution)/shard_map/ppermute | solution.py:25
  25.0 0.0 collective-permute-done.1.left
  25.0 2.5 %collective-permute-done.above = f32[192,128]{1,0:T(8,128)S(1)} collective-permute-done((f32[192,128]{1,0:T(8,128)S(1)}, f32[192,128]{1,0:T(8,128)S(1)}, u32[]{:S(2)}, u32[]{:S(2)}) %collective-permute-start) | collective-permute-done | bytes 98336 | tf_op jit(solution)/shard_map/ppermute | solution.py:25
  27.5 0.0 copy-done.1
  27.5 1.7 %shard_map.115 = (f32[208,128]{1,0:T(8,128)S(1)}, f32[240,128]{1,0:T(8,128)S(1)}, f32[208,128]{1,0:T(8,128)S(1)}, f32[240,128]{1,0:T(8,128)S(1)}, f32[768,128]{1,0:T(8,128)S(1)}, /*index=5*/f32[384,128]{1,0:T(8,128)S(1)}) custom-call(f32[192,128]{1,0:T(8,128)S(1)} %get-tuple-element.67.gap_down, f32[192,128]{1,0:T(8,128)S(1)} %get-tuple-element.66.gap_right, ...), custom_call_target="tpu_custom_call" | custom-call | flops 452984832 | tf_op jit(solution)/shard_map/pallas_call | solution.py:431
  29.2 4.5 %collective-permute-start.2 = (f32[240,128]{1,0:T(8,128)S(1)}, f32[240,128]{1,0:T(8,128)S(1)}, u32[]{:S(2)}, u32[]{:S(2)}) collective-permute-start(f32[240,128]{1,0:T(8,128)S(1)} %get-tuple-element.42), channel_id=1, source_target_pairs={{0,16},{16,32},{32,48},{48,64},{64,80},{80,96},{96,112},{112,128},... | collective-permute-start | bytes 368648 | tf_op jit(solution)/shard_map/ppermute | solution.py:25
  33.7 3.8 %collective-permute-start.4 = (f32[240,128]{1,0:T(8,128)S(1)}, f32[240,128]{1,0:T(8,128)S(1)}, u32[]{:S(2)}, u32[]{:S(2)}) collective-permute-start(f32[240,128]{1,0:T(8,128)S(1)} %get-tuple-element.44), channel_id=1, source_target_pairs={{0,1},{1,2},{2,3},{3,4},{4,5},{5,6},{6,7},{7,8},{8,9},{9,10},{10,1... | collective-permute-start | bytes 368648 | tf_op jit(solution)/shard_map/ppermute | solution.py:25
  37.5 1.3 collective-permute-start.3
  38.8 1.9 %collective-permute-start.5 = (f32[208,128]{1,0:T(8,128)S(1)}, f32[208,128]{1,0:T(8,128)S(1)}, u32[]{:S(2)}, u32[]{:S(2)}) collective-permute-start(f32[208,128]{1,0:T(8,128)S(1)} %get-tuple-element.45), channel_id=1, source_target_pairs={{1,0},{2,1},{3,2},{4,3},{5,4},{6,5},{7,6},{8,7},{9,8},{10,9},{11,1... | collective-permute-start | bytes 319496 | tf_op jit(solution)/shard_map/ppermute | solution.py:25
  40.8 2.4 %collective-permute-done.3.below = f32[208,128]{1,0:T(8,128)S(1)} collective-permute-done((f32[208,128]{1,0:T(8,128)S(1)}, f32[208,128]{1,0:T(8,128)S(1)}, u32[]{:S(2)}, u32[]{:S(2)}) %collective-permute-start.3) | collective-permute-done | bytes 106528 | tf_op jit(solution)/shard_map/ppermute | solution.py:25
  43.2 1.7 %collective-permute-done.5.right = f32[208,128]{1,0:T(8,128)S(1)} collective-permute-done((f32[208,128]{1,0:T(8,128)S(1)}, f32[208,128]{1,0:T(8,128)S(1)}, u32[]{:S(2)}, u32[]{:S(2)}) %collective-permute-start.5) | collective-permute-done | bytes 106528 | tf_op jit(solution)/shard_map/ppermute | solution.py:25
  44.9 0.0 collective-permute-done.2.above
  44.9 0.0 collective-permute-done.4.left
  44.9 1.0 shard_map.116
  45.8 0.0 all-to-all-done
  45.8 13.5 %all-to-all-start.1 = ((f32[32,8,128]{2,1,0:T(8,128)}), f32[32,8,128]{2,1,0:T(8,128)S(1)}, u32[]{:S(2)}, u32[]{:S(2)}) async-start(f32[32,8,128]{2,1,0:T(8,128)} %bitcast.12), calls=%async_computation.1 | async-start | bytes 262144 | tf_op jit(solution)/shard_map/all_to_all | solution.py:506
  59.4 0.0 copy-start.2
  59.4 4.8 %shard_map.114 = (bf16[768,768]{1,0:T(8,128)(2,1)}, bf16[768,768]{1,0:T(8,128)(2,1)}, f32[256,256]{1,0:T(8,128)S(1)}) custom-call(s32[1]{0:T(128)} %bitcast.here, f32[8,768]{1,0:T(8,128)S(1)} %get-tuple-element.34.link_rows, bf16[768,768]{1,0:T(8,128)(2,1)S(1)} %get-tuple-element.35.place, f32[256,384]{1,0:T(8,128)S(1)} %bitcast.31, bf16[768,768]{1,0:T(8,128)(2,1)} %bitcast.41), custom_call_target="tpu_custom_call" | custom-call | flops 1811939328 | tf_op jit(solution)/shard_map/pallas_call | solution.py:431
  64.2 5.0 %all-to-all-done.1 = f32[32,8,128]{2,1,0:T(8,128)S(1)} async-done(((f32[32,8,128]{2,1,0:T(8,128)}), f32[32,8,128]{2,1,0:T(8,128)S(1)}, u32[]{:S(2)}, u32[]{:S(2)}) %all-to-all-start.1) | async-done | bytes 131104 | tf_op jit(solution)/shard_map/all_to_all | solution.py:506
  69.3 1.0 shard_map.117
  70.3 8.2 %all-to-all-start.2 = ((f32[16,16,128]{2,1,0:T(8,128)}), f32[16,16,128]{2,1,0:T(8,128)S(1)}, u32[]{:S(2)}, u32[]{:S(2)}) async-start(f32[16,16,128]{2,1,0:T(8,128)} %bitcast.14), calls=%async_computation.2 | async-start | bytes 262144 | tf_op jit(solution)/shard_map/all_to_all | solution.py:521
  78.5 0.0 copy-done.2
  78.6 2.6 %shard_map.118 = (bf16[768,128]{1,0:T(8,128)(2,1)S(1)}, f32[16,768]{1,0:T(8,128)S(1)}, f32[56,128]{1,0:T(8,128)S(1)}, bf16[48,128]{1,0:T(8,128)(2,1)S(1)}) custom-call(f32[240,128]{1,0:T(8,128)S(1)} %collective-permute-done.2.above, f32[208,128]{1,0:T(8,128)S(1)} %collective-permute-done.3.below, f32[240,128]{1,0:T(8,128)S(1)} %collective-permute-done.4.left, ...), custom_call_target="tpu_custom_call" | custom-call | flops 905969664 | tf_op jit(solution)/shard_map/pallas_call | solution.py:431
  81.2 6.2 %all-to-all-done.2 = f32[16,16,128]{2,1,0:T(8,128)S(1)} async-done(((f32[16,16,128]{2,1,0:T(8,128)}), f32[16,16,128]{2,1,0:T(8,128)S(1)}, u32[]{:S(2)}, u32[]{:S(2)}) %all-to-all-start.2) | async-done | bytes 131104 | tf_op jit(solution)/shard_map/all_to_all | solution.py:521
  87.4 0.2 shard_map.119
  87.6 10.4 %all_to_all.66 = f32[16,8,128]{2,1,0:T(8,128)S(1)} all-to-all(f32[16,8,128]{2,1,0:T(8,128)S(1)} %bitcast.35), channel_id=1, replica_groups=mesh['gx_0'=8,'gx_1'=4,'gy_0'=8,'gy_1'=2] {'gy_0','gy_1'}, dimensions={0} | all-to-all | bytes 131072 | tf_op jit(solution)/shard_map/all_to_all | solution.py:552
  98.1 13.5 %all_to_all.67 = f32[32,8,128]{2,1,0:T(8,128)S(1)} all-to-all(f32[32,8,128]{2,1,0:T(8,128)S(1)} %bitcast.29), channel_id=1, replica_groups=mesh['gx_0'=8,'gx_1'=4,'gy_0'=8,'gy_1'=2] {'gx_0','gx_1'}, dimensions={0} | all-to-all | bytes 262144 | tf_op jit(solution)/shard_map/all_to_all | solution.py:552
  111.5 0.6 shard_map.121
  112.2 3.5 %all-to-all-start.5 = ((f32[8,8,128]{2,1,0:T(8,128)}), f32[8,8,128]{2,1,0:T(8,128)S(1)}, u32[]{:S(2)}, u32[]{:S(2)}) async-start(f32[8,8,128]{2,1,0:T(8,128)} %bitcast.21), calls=%async_computation.5 | async-start | bytes 65536 | tf_op jit(solution)/shard_map/all_to_all | solution.py:559
  115.7 0.0 copy-start
  115.7 2.5 %shard_map.122 = (f32[768,128]{1,0:T(8,128)S(1)}, bf16[768,128]{1,0:T(8,128)(2,1)S(1)}, f32[384,128]{1,0:T(8,128)S(1)}, bf16[384,128]{1,0:T(8,128)(2,1)S(1)}) custom-call(f32[16,128]{1,0:T(8,128)S(1)} %get-tuple-element.53.amplitudes, f32[768,128]{1,0:T(8,128)S(1)} %get-tuple-element.48.precond, bf16[768,128]{1,0:T(8,128)(2,1)S(1)} %get-tuple-element.54.mode_six, ...), custom_call_target="tpu_custom_call" | custom-call | flops 905969664 | tf_op jit(solution)/shard_map/pallas_call | solution.py:431
  118.2 4.2 %all-to-all-done.5 = f32[8,8,128]{2,1,0:T(8,128)S(1)} async-done(((f32[8,8,128]{2,1,0:T(8,128)}), f32[8,8,128]{2,1,0:T(8,128)S(1)}, u32[]{:S(2)}, u32[]{:S(2)}) %all-to-all-start.5) | async-done | bytes 32800 | tf_op jit(solution)/shard_map/all_to_all | solution.py:559
  122.4 0.0 copy-done
  122.4 0.7 shard_map.124
  123.1 1.3 collective-permute-start.6
  124.4 4.5 %collective-permute-start.7 = (f32[192,128]{1,0:T(8,128)S(1)}, f32[192,128]{1,0:T(8,128)S(1)}, u32[]{:S(2)}, u32[]{:S(2)}) collective-permute-start(f32[192,128]{1,0:T(8,128)S(1)} %get-tuple-element.64), channel_id=1, source_target_pairs={{1,0},{2,1},{3,2},{4,3},{5,4},{6,5},{7,6},{8,7},{9,8},{10,9},{11,1... | collective-permute-start | bytes 294920 | tf_op jit(solution)/shard_map/ppermute | solution.py:25
  128.9 0.9 shard_map.123
  129.8 0.0 collective-permute-done.6.below
  129.8 1.8 %collective-permute-done.7.right = f32[192,128]{1,0:T(8,128)S(1)} collective-permute-done((f32[192,128]{1,0:T(8,128)S(1)}, f32[192,128]{1,0:T(8,128)S(1)}, u32[]{:S(2)}, u32[]{:S(2)}) %collective-permute-start.7) | collective-permute-done | bytes 98336 | tf_op jit(solution)/shard_map/ppermute | solution.py:25
  131.7 0.7 shard_map.125
  (2 shorter events, 0.0 us)
Async XLA Ops:
  0.6 16.9 %copy-start.3 = (f32[1,1,384,128]{3,2,1,0:T(8,128)S(1)}, f32[1,1,384,128]{3,2,1,0:T(8,128)}, u32[]{:S(2)}) copy-start(f32[1,1,384,128]{3,2,1,0:T(8,128)} %param.10) | copy-start | bytes 589828
  3.7 23.7 %copy-start.1 = (f32[1,1,16,384]{3,2,1,0:T(8,128)S(1)}, f32[1,1,16,384]{3,2,1,0:T(8,128)}, u32[]{:S(2)}) copy-start(f32[1,1,16,384]{3,2,1,0:T(8,128)} %param.15) | copy-start | bytes 73732
  3.8 42.1 %all-to-all-start = ((f32[32,8,384]{2,1,0:T(8,128)}), f32[32,8,384]{2,1,0:T(8,128)S(1)}, u32[]{:S(2)}, u32[]{:S(2)}) async-start(f32[32,8,384]{2,1,0:T(8,128)} %bitcast.6), calls=%async_computation | async-start | bytes 786432 | tf_op jit(solution)/shard_map/all_to_all | solution.py:499
  17.5 7.5 %collective-permute-start.1 = (f32[192,128]{1,0:T(8,128)S(1)}, f32[192,128]{1,0:T(8,128)S(1)}, u32[]{:S(2)}, u32[]{:S(2)}) collective-permute-start(f32[192,128]{1,0:T(8,128)S(1)} %get-tuple-element.66.gap_right), channel_id=1, source_target_pairs={{0,1},{1,2},{2,3},{3,4},{4,5},{5,6},{6,7},{7,8},{8,9},{9,10},{10,1... | collective-permute-start | bytes 294920 | tf_op jit(solution)/shard_map/ppermute | solution.py:25
  21.6 5.9 %collective-permute-start = (f32[192,128]{1,0:T(8,128)S(1)}, f32[192,128]{1,0:T(8,128)S(1)}, u32[]{:S(2)}, u32[]{:S(2)}) collective-permute-start(f32[192,128]{1,0:T(8,128)S(1)} %get-tuple-element.67.gap_down), channel_id=1, source_target_pairs={{0,16},{16,32},{32,48},{48,64},{64,80},{80,96},{96,112},{112,128},... | collective-permute-start | bytes 294920 | tf_op jit(solution)/shard_map/ppermute | solution.py:25
  29.2 15.7 %collective-permute-start.2 = (f32[240,128]{1,0:T(8,128)S(1)}, f32[240,128]{1,0:T(8,128)S(1)}, u32[]{:S(2)}, u32[]{:S(2)}) collective-permute-start(f32[240,128]{1,0:T(8,128)S(1)} %get-tuple-element.42), channel_id=1, source_target_pairs={{0,16},{16,32},{32,48},{48,64},{64,80},{80,96},{96,112},{112,128},... | collective-permute-start | bytes 368648 | tf_op jit(solution)/shard_map/ppermute | solution.py:25
  33.7 11.2 %collective-permute-start.4 = (f32[240,128]{1,0:T(8,128)S(1)}, f32[240,128]{1,0:T(8,128)S(1)}, u32[]{:S(2)}, u32[]{:S(2)}) collective-permute-start(f32[240,128]{1,0:T(8,128)S(1)} %get-tuple-element.44), channel_id=1, source_target_pairs={{0,1},{1,2},{2,3},{3,4},{4,5},{5,6},{6,7},{7,8},{8,9},{9,10},{10,1... | collective-permute-start | bytes 368648 | tf_op jit(solution)/shard_map/ppermute | solution.py:25
  37.5 5.6 %collective-permute-start.3 = (f32[208,128]{1,0:T(8,128)S(1)}, f32[208,128]{1,0:T(8,128)S(1)}, u32[]{:S(2)}, u32[]{:S(2)}) collective-permute-start(f32[208,128]{1,0:T(8,128)S(1)} %get-tuple-element.43), channel_id=1, source_target_pairs={{16,0},{32,16},{48,32},{64,48},{80,64},{96,80},{112,96},{128,112},... | collective-permute-start | bytes 319496 | tf_op jit(solution)/shard_map/ppermute | solution.py:25
  38.8 6.0 %collective-permute-start.5 = (f32[208,128]{1,0:T(8,128)S(1)}, f32[208,128]{1,0:T(8,128)S(1)}, u32[]{:S(2)}, u32[]{:S(2)}) collective-permute-start(f32[208,128]{1,0:T(8,128)S(1)} %get-tuple-element.45), channel_id=1, source_target_pairs={{1,0},{2,1},{3,2},{4,3},{5,4},{6,5},{7,6},{8,7},{9,8},{10,9},{11,1... | collective-permute-start | bytes 319496 | tf_op jit(solution)/shard_map/ppermute | solution.py:25
  45.8 23.5 %all-to-all-start.1 = ((f32[32,8,128]{2,1,0:T(8,128)}), f32[32,8,128]{2,1,0:T(8,128)S(1)}, u32[]{:S(2)}, u32[]{:S(2)}) async-start(f32[32,8,128]{2,1,0:T(8,128)} %bitcast.12), calls=%async_computation.1 | async-start | bytes 262144 | tf_op jit(solution)/shard_map/all_to_all | solution.py:506
  59.4 19.2 %copy-start.2 = (f32[1,1,16,384]{3,2,1,0:T(8,128)S(1)}, f32[1,1,16,384]{3,2,1,0:T(8,128)}, u32[]{:S(2)}) copy-start(f32[1,1,16,384]{3,2,1,0:T(8,128)} %param.16) | copy-start | bytes 73732
  70.3 17.1 %all-to-all-start.2 = ((f32[16,16,128]{2,1,0:T(8,128)}), f32[16,16,128]{2,1,0:T(8,128)S(1)}, u32[]{:S(2)}, u32[]{:S(2)}) async-start(f32[16,16,128]{2,1,0:T(8,128)} %bitcast.14), calls=%async_computation.2 | async-start | bytes 262144 | tf_op jit(solution)/shard_map/all_to_all | solution.py:521
  112.2 10.2 %all-to-all-start.5 = ((f32[8,8,128]{2,1,0:T(8,128)}), f32[8,8,128]{2,1,0:T(8,128)S(1)}, u32[]{:S(2)}, u32[]{:S(2)}) async-start(f32[8,8,128]{2,1,0:T(8,128)} %bitcast.21), calls=%async_computation.5 | async-start | bytes 65536 | tf_op jit(solution)/shard_map/all_to_all | solution.py:559
  115.7 6.7 %copy-start = (bf16[768,768]{1,0:T(8,128)(2,1)S(1)}, bf16[768,768]{1,0:T(8,128)(2,1)}, u32[]{:S(2)}) copy-start(bf16[768,768]{1,0:T(8,128)(2,1)} %get-tuple-element.61.pick_flex) | copy-start | bytes 3538948
  123.1 6.7 %collective-permute-start.6 = (f32[192,128]{1,0:T(8,128)S(1)}, f32[192,128]{1,0:T(8,128)S(1)}, u32[]{:S(2)}, u32[]{:S(2)}) collective-permute-start(f32[192,128]{1,0:T(8,128)S(1)} %get-tuple-element.63), channel_id=1, source_target_pairs={{16,0},{32,16},{48,32},{64,48},{80,64},{96,80},{112,96},{128,112},... | collective-permute-start | bytes 294920 | tf_op jit(solution)/shard_map/ppermute | solution.py:25
  124.4 7.3 %collective-permute-start.7 = (f32[192,128]{1,0:T(8,128)S(1)}, f32[192,128]{1,0:T(8,128)S(1)}, u32[]{:S(2)}, u32[]{:S(2)}) collective-permute-start(f32[192,128]{1,0:T(8,128)S(1)} %get-tuple-element.64), channel_id=1, source_target_pairs={{1,0},{2,1},{3,2},{4,3},{5,4},{6,5},{7,6},{8,7},{9,8},{10,9},{11,1... | collective-permute-start | bytes 294920 | tf_op jit(solution)/shard_map/ppermute | solution.py:25

commit v4 on v3

--- a/solution.py
+++ b/solution.py
@@ -112,17 +112,38 @@
     return pltpu.roll(x, start, 1) if start else x
 
 
+def blocks_kernel(coarse_hbm, blocks, coarse, wide, arrived):
+    load = pltpu.make_async_copy(coarse_hbm, coarse, arrived.at[0])
+    load.start()
+    wide[...] = jnp.zeros_like(wide)
+    load.wait()
+    wide[0:3, :] = coarse[...]
+    unknowns = wide.shape[1]
+    grid_rows = blocks.shape[0] // 8
+    row_unknowns = unknowns // grid_rows
+    for i in range(grid_rows):
+        first = row_unknowns * (i - 1)
+        span = min(unknowns, 384)
+        start = min(max(first // 128, 0) * 128, unknowns - span)
+        piece = wide[:, start : start + span]
+        if first != start:
+            piece = pltpu.roll(piece, (start - first) % span, 1)
+        if span < 256:
+            piece = widened(piece, 256)
+        blocks[8 * i : 8 * i + 8, :] = piece[:, 0:128] + pltpu.roll(piece[:, 128:256], 3, 0)
+
+
 def prepare_kernel(
-    windows, count_hbm, slots_hbm, mult_hbm, modes_hbm, schur_hbm, coarse_hbm,
-    place, pick_schur, mode_rows, link_rows, columns, blocks,
-    buffer, slots, mult, modes, schur, coarse, wide, count, arrived,
+    count_hbm, slots_hbm, mult_hbm, modes_hbm, schur_hbm,
+    place, pick_schur, mode_rows, link_rows,
+    buffer, slots, mult, modes, schur, count, arrived,
 ):
     copies = [
         pltpu.make_async_copy(source, target, arrived.at[n])
         for n, (source, target) in enumerate(
             (
                 (count_hbm, count), (slots_hbm, slots), (mult_hbm, mult), (modes_hbm, modes),
-                (schur_hbm, schur), (coarse_hbm, coarse),
+                (schur_hbm, schur),
             )
         )
     ]
@@ -131,7 +152,6 @@
     width = slots.shape[1]
     total = 4 * width
     buffer[...] = jnp.zeros_like(buffer)
-    wide[...] = jnp.zeros_like(wide)
     lane = lax.broadcasted_iota(jnp.int32, (1, total), 1)
     copies[0].wait()
     copies[1].wait()
@@ -160,13 +180,7 @@
     buffer[2:3, :] = weights
     buffer[3:4, :] = jnp.abs(rows[3:4])
     link_rows[...] = buffer[...]
-    cols = jnp.transpose(buffer[...])
-    columns[...] = cols
-    pick_value = picking(cols)
-    copies[5].wait()
-    wide[0:3, :] = coarse[...]
-    for i, start in enumerate(windows):
-        blocks[8 * i : 8 * i + 8, :] = wide[:, start : start + blocks.shape[1]]
+    pick_value = picking(jnp.transpose(buffer[...]))
     copies[4].wait()
     pick_schur[...] = dot(pick_value, schur[...]).astype(BF16)
 
@@ -184,10 +198,11 @@
 
 
 def precond_kernel(
-    gap_down, gap_right, above, left, place, pick_schur, columns, mode_rows, saved,
+    gap_down, gap_right, above, left, place, pick_schur, link_rows, mode_rows, saved,
     up_msg, down_msg, left_msg, right_msg, own, residual,
 ):
     width = above.shape[0]
+    columns = jnp.transpose(link_rows[...])
     links = jnp.concatenate([above[...], gap_down[...], left[...], gap_right[...]], axis=0)
     spread = select_rows(place[...], links)
     weighted = (columns[:, 2:3] * spread).astype(BF16)
@@ -206,28 +221,34 @@
     residual[width:, :] = jnp.where(columns[3 * width :, 1:2] != 0.0, gap_right[...], 0.0)
 
 
-def flex_kernel(
-    grid, here, link_rows, place, blocks, flex_hbm, pick_flex_hbm, link_flex_hbm, coarse_rows,
-    flex, pick_flex, link_flex, arrived,
-):
-    load = pltpu.make_async_copy(flex_hbm, flex, arrived.at[0])
-    load.start()
-    row_unknowns, last_window = grid
-    count = row_unknowns // 3
-    first = row_unknowns * (here[0] - 1)
-    offset = first - jnp.clip(first >> 7, 0, last_window) * 128
-    row = lax.broadcasted_iota(jnp.int32, (coarse_rows.shape[0], 1), 0)
+def rows_kernel(blocks, coarse_rows):
+    total = coarse_rows.shape[0]
+    count = total // 16
+    row = lax.broadcasted_iota(jnp.int32, (total, 1), 0)
     j = row >> 4
     part = ((row & 15) * 11) >> 5
     mode = (row & 15) - 3 * part
     down = jnp.where(part == 1, -1, jnp.where(part == 2, 1, 0))
     j = j + jnp.where(part == 3, -1, jnp.where(part == 4, 1, 0))
     valid = (part < 5) & (j >= 0) & (j < count)
-    wanted = jnp.where(valid, ((down + 1) * count + j) * 3 + mode + offset, -1)
-    at = lax.broadcasted_iota(jnp.int32, (coarse_rows.shape[0], blocks.shape[1]), 1)
-    chosen = jnp.where(at == wanted, 1.0, 0.0).astype(BF16)
+    wanted = jnp.where(valid, ((down + 1) * count + j) * 3 + mode, -1)
+    at = lax.broadcasted_iota(jnp.int32, (total, 128), 1)
+    chosen = [
+        jnp.where(at + shift == wanted, 1.0, 0.0).astype(BF16) for shift in (0, 128)
+    ]
+    chosen = jnp.concatenate(chosen, axis=0)
     high, mid, low = split3(blocks[...])
-    coarse_rows[...] = dot_nt(chosen, high) + (dot_nt(chosen, mid) + dot_nt(chosen, low))
+    out = dot_nt(chosen, high) + (dot_nt(chosen, mid) + dot_nt(chosen, low))
+    width = coarse_rows.shape[1]
+    coarse_rows[...] = out[:total] + pltpu.roll(out[total:], width - 3, 1)
+
+
+def flex_kernel(
+    link_rows, place, flex_hbm, pick_flex_hbm, link_flex_hbm,
+    flex, pick_flex, link_flex, arrived,
+):
+    load = pltpu.make_async_copy(flex_hbm, flex, arrived.at[0])
+    load.start()
     pick_value = picking(jnp.transpose(link_rows[...]))
     load.wait()
     rows = dot(pick_value, flex[...]).astype(BF16)
@@ -415,7 +436,9 @@
 def call(kernel, inputs, outputs, scalars=0, remote=0, scratch=(), copies=0, hbm_out=(), flops=0):
     out_specs = tuple(HBM if n in hbm_out else VMEM for n in range(len(outputs)))
     outputs = tuple(
-        pltpu.HBM(shape, dtype) if n in hbm_out else jax.ShapeDtypeStruct(shape, dtype)
+        pltpu.HBM(shape, dtype)
+        if n in hbm_out
+        else jax.ShapeDtypeStruct(shape, dtype)
         for n, (shape, dtype) in enumerate(outputs)
     )
     local = len(inputs) - remote
@@ -456,38 +479,39 @@
     total = 4 * width
     cases = gap.shape[1]
     unknowns = coarse_inverse.shape[1]
-    row_unknowns = columns * modes.shape[0]
-    window = min(unknowns, 384)
-    windows = [
-        min(max((row_unknowns * (i - 1)) // 128, 0), (unknowns - window) // 128) * 128
-        for i in range(rows)
-    ]
-    here = lax.axis_index(GX).reshape(1)
     big = (total, total)
     cube = 2 * total**3
     gap_down = gap[:width]
     gap_right = gap[width:]
     above = shifted(gap_down, GX, 1)
     left = shifted(gap_right, GY, 1)
-    place, pick_schur, mode_rows, link_rows, slot_cols, blocks = call(
-        functools.partial(prepare_kernel, windows),
-        (count, slots, multiplicity[0], modes, schur_blocks[0, 0], coarse_inverse),
+    (blocks,) = call(
+        blocks_kernel,
+        (coarse_inverse,),
+        (((8 * rows, 128), F32),),
+        remote=1,
+        scratch=((coarse_inverse.shape, F32), ((8, unknowns), F32)),
+        copies=1,
+        flops=cube // 64,
+    )
+    blocks = lax.all_to_all(blocks, GX, 0, 0, tiled=True)
+    place, pick_schur, mode_rows, link_rows = call(
+        prepare_kernel,
+        (count, slots, multiplicity[0], modes, schur_blocks[0, 0]),
         (
-            (big, BF16), (big, BF16), ((8, total), F32), ((8, total), F32), ((total, 8), F32),
-            ((8 * rows, window), F32),
+            (big, BF16), (big, BF16), ((8, total), F32), ((8, total), F32),
         ),
-        remote=6,
+        remote=5,
         scratch=(
             ((8, total), F32), (slots.shape, jnp.int32), ((1, total), jnp.int32), (modes.shape, F32),
-            (big, BF16), (coarse_inverse.shape, F32), ((8, unknowns), F32),
-            pltpu.SMEM((1, 4), jnp.int32),
+            (big, BF16), pltpu.SMEM((1, 4), jnp.int32),
         ),
-        copies=6,
+        copies=5,
         flops=cube,
     )
     up_msg, down_msg, left_msg, right_msg, own, residual = call(
         precond_kernel,
-        (gap_down, gap_right, above, left, place, pick_schur, slot_cols, mode_rows, saved),
+        (gap_down, gap_right, above, left, place, pick_schur, link_rows, mode_rows, saved),
         tuple(((width + extra, cases), F32) for extra in (16, 48, 16, 48))
         + (((total, cases), F32), ((2 * width, cases), F32)),
         flops=cube // 2,
@@ -496,7 +520,6 @@
     from_below = shifted(up_msg, GX, -1)
     from_left = shifted(right_msg, GY, 1)
     from_right = shifted(left_msg, GY, -1)
-    blocks = lax.all_to_all(blocks, GX, 0, 0, tiled=True)
     precond, coarse_in = call(
         coarse_in_kernel,
         (own, from_above, from_below, from_left, from_right, mode_rows),
@@ -504,16 +527,18 @@
         flops=cube // 16,
     )
     gathered = lax.all_to_all(coarse_in, GX, 0, 0, tiled=True)
-    pick_flex, link_flex, coarse_rows = call(
-        functools.partial(flex_kernel, (row_unknowns, (unknowns - window) // 128)),
-        (here, link_rows, place, blocks, flex),
-        ((big, BF16), (big, BF16), ((16 * columns, 8 * rows), F32)),
-        scalars=1,
+    pick_flex, link_flex = call(
+        flex_kernel,
+        (link_rows, place, flex),
+        ((big, BF16), (big, BF16)),
         remote=1,
         scratch=((big, BF16), (big, BF16), (big, BF16)),
         copies=3,
         hbm_out=(0, 1),
         flops=2 * cube,
+    )
+    (coarse_rows,) = call(
+        rows_kernel, (blocks,), (((16 * columns, 8 * rows), F32),), flops=cube // 16
     )
     (parts,) = call(
         coarse_kernel, (coarse_rows, gathered), (((16 * columns, cases), F32),), flops=cube // 8,

time: 133 us -> 129 us (0.970)
  starting transfers between devices: 63.8 us -> 57.9 us
  waiting for transfers between devices: 23.9 us -> 21.3 us
  blocking collectives: 23.9 us -> 25.9 us
  Pallas kernels: 19.8 us -> 21.5 us
    all_to_all x1, waiting for transfers between devices: 6.24 us -> 1.74 us  [step(): parts = lax.all_to_all(parts, GY, 0, 0, tiled=True)]
    all_to_all x1, waiting for transfers between devices: 5.05 us -> 9.44 us  [step(): gathered = lax.all_to_all(coarse_in, GX, 0, 0, tiled=True)]
    all_to_all x1, starting transfers between devices: 13.5 us -> 11 us  [step(): gathered = lax.all_to_all(coarse_in, GX, 0, 0, tiled=True)]
    ppermute x8, waiting for transfers between devices: 8.42 us -> 5.94 us  [shifted(): lax.ppermute(value, axis, [(source, source + steps) for source in range(i...]
    all_to_all x2, blocking collectives: 23.9 us -> 25.9 us  [step(): partial = lax.all_to_all(partial, axis, 0, 0, tiled=True)]
    ppermute x8, starting transfers between devices: 24.8 us -> 22.9 us  [shifted(): lax.ppermute(value, axis, [(source, source + steps) for source in range(i...]
    pallas_call x13 -> x15, Pallas kernels: 19.8 us -> 21.5 us  [call(): pl.pallas_call(kernel, out_shape=outputs, in_specs=[SMEM] * scalars + [VM...]
  transfers between devices with their start and end apart: 12 -> 12, of which waited for: 7 -> 6; matrix products, arithmetic and copies ran while one was open for 0% -> 0% of each run, Pallas kernels for 10% -> 14%
where the time goes in v4:
time: 129 us; the launch traced here: 128 us
  starting transfers between devices  57.9 us (45%)
  blocking collectives  25.9 us (20%)
  Pallas kernels  21.5 us (17%)
  waiting for transfers between devices  21.3 us (17%)
    all_to_all x2, blocking collectives, step(): partial = lax.all_to_all(partial, axis, 0, 0, tiled=True)  25.9 us
    ppermute x8, starting transfers between devices, shifted(): lax.ppermute(value, axis, [(source, source + steps) for source in range(i...  22.9 us
    pallas_call x15, Pallas kernels, call(): pl.pallas_call(kernel, out_shape=outputs, in_specs=[SMEM] * scalars + [VM...  21.5 us
    all_to_all x1, starting transfers between devices, step(): blocks = lax.all_to_all(blocks, GX, 0, 0, tiled=True)  12.6 us
    all_to_all x1, starting transfers between devices, step(): gathered = lax.all_to_all(coarse_in, GX, 0, 0, tiled=True)  11 us
    all_to_all x1, waiting for transfers between devices, step(): gathered = lax.all_to_all(coarse_in, GX, 0, 0, tiled=True)  9.44 us
    all_to_all x1, starting transfers between devices, step(): parts = lax.all_to_all(parts, GY, 0, 0, tiled=True)  7.93 us
    ppermute x8, waiting for transfers between devices, shifted(): lax.ppermute(value, axis, [(source, source + steps) for source in range(i...  5.94 us
  transfers between devices with their start and end apart: 12, of which 6 were waited for; matrix products, arithmetic and copies ran while one was open for 0% of the time, Pallas kernels for 14%

profile of v4, /device:TPU:1, one launch (start us, length us, event | category | flops | bytes accessed | tf_op | source)
XLA Modules:
  0.0 128.5 jit_solution(5919312865188741433)
XLA Ops:
  0.6 1.0 slice_bitcast_fusion
  1.6 4.6 %collective-permute-start.1 = (f32[192,128]{1,0:T(8,128)S(1)}, f32[192,128]{1,0:T(8,128)S(1)}, u32[]{:S(2)}, u32[]{:S(2)}) collective-permute-start(f32[192,128]{1,0:T(8,128)S(1)} %get-tuple-element.60.gap_right), channel_id=1, source_target_pairs={{0,1},{1,2},{2,3},{3,4},{4,5},{5,6},{6,7},{7,8},{8,9},{9,10},{10,1... | collective-permute-start | bytes 294920 | tf_op jit(solution)/shard_map/ppermute | solution.py:25
  6.2 3.1 %collective-permute-start = (f32[192,128]{1,0:T(8,128)S(1)}, f32[192,128]{1,0:T(8,128)S(1)}, u32[]{:S(2)}, u32[]{:S(2)}) collective-permute-start(f32[192,128]{1,0:T(8,128)S(1)} %get-tuple-element.61.gap_down), channel_id=1, source_target_pairs={{0,16},{16,32},{32,48},{48,64},{64,80},{80,96},{96,112},{112,128},... | collective-permute-start | bytes 294920 | tf_op jit(solution)/shard_map/ppermute | solution.py:25
  9.3 1.6 %shard_map.113 = f32[256,128]{1,0:T(8,128)} custom-call(f32[3,1536]{1,0:T(4,128)} %coarse_hbm.1), custom_call_target="tpu_custom_call" | custom-call | flops 14155776 | tf_op jit(solution)/shard_map/pallas_call | solution.py:454
  10.9 12.6 %all-to-all-start = ((f32[32,8,128]{2,1,0:T(8,128)}), f32[32,8,128]{2,1,0:T(8,128)S(1)}, u32[]{:S(2)}, u32[]{:S(2)}) async-start(f32[32,8,128]{2,1,0:T(8,128)} %bitcast), calls=%async_computation | async-start | bytes 262144 | tf_op jit(solution)/shard_map/all_to_all | solution.py:497
  23.5 0.0 copy-start.1
  23.5 3.1 %shard_map.115 = (bf16[768,768]{1,0:T(8,128)(2,1)S(1)}, bf16[768,768]{1,0:T(8,128)(2,1)S(1)}, f32[8,768]{1,0:T(8,128)S(1)}, f32[8,768]{1,0:T(8,128)S(1)}) custom-call(s32[1,4]{1,0:T(1,128)} %bitcast.45, s32[4,192]{1,0:T(4,128)} %bitcast.43, s32[1,768]{1,0:T(1,128)} %bitcast.44, f32[3,1,768]{2,1,0:T(1,128)} %bitcast.42, bf16[768,768]{1,0:T(8,128)(2,1)} %bitcast.39), custom_call_target="tpu_custom_call" | custom-call | flops 905969664 | tf_op jit(solution)/shard_map/pallas_call | solution.py:454
  26.6 0.0 collective-permute-done.1.left
  26.6 0.0 collective-permute-done.above
  26.6 0.0 copy-done.1
  26.6 1.7 %shard_map.116 = (f32[208,128]{1,0:T(8,128)S(1)}, f32[240,128]{1,0:T(8,128)S(1)}, f32[208,128]{1,0:T(8,128)S(1)}, f32[240,128]{1,0:T(8,128)S(1)}, f32[768,128]{1,0:T(8,128)S(1)}, /*index=5*/f32[384,128]{1,0:T(8,128)S(1)}) custom-call(f32[192,128]{1,0:T(8,128)S(1)} %get-tuple-element.61.gap_down, f32[192,128]{1,0:T(8,128)S(1)} %get-tuple-element.60.gap_right, ...), custom_call_target="tpu_custom_call" | custom-call | flops 452984832 | tf_op jit(solution)/shard_map/pallas_call | solution.py:454
  28.3 3.1 %collective-permute-start.2 = (f32[240,128]{1,0:T(8,128)S(1)}, f32[240,128]{1,0:T(8,128)S(1)}, u32[]{:S(2)}, u32[]{:S(2)}) collective-permute-start(f32[240,128]{1,0:T(8,128)S(1)} %get-tuple-element.36), channel_id=1, source_target_pairs={{0,16},{16,32},{32,48},{48,64},{64,80},{80,96},{96,112},{112,128},... | collective-permute-start | bytes 368648 | tf_op jit(solution)/shard_map/ppermute | solution.py:25
  31.4 3.0 %collective-permute-start.4 = (f32[240,128]{1,0:T(8,128)S(1)}, f32[240,128]{1,0:T(8,128)S(1)}, u32[]{:S(2)}, u32[]{:S(2)}) collective-permute-start(f32[240,128]{1,0:T(8,128)S(1)} %get-tuple-element.38), channel_id=1, source_target_pairs={{0,1},{1,2},{2,3},{3,4},{4,5},{5,6},{6,7},{7,8},{8,9},{9,10},{10,1... | collective-permute-start | bytes 368648 | tf_op jit(solution)/shard_map/ppermute | solution.py:25
  34.5 1.3 %collective-permute-start.3 = (f32[208,128]{1,0:T(8,128)S(1)}, f32[208,128]{1,0:T(8,128)S(1)}, u32[]{:S(2)}, u32[]{:S(2)}) collective-permute-start(f32[208,128]{1,0:T(8,128)S(1)} %get-tuple-element.37), channel_id=1, source_target_pairs={{16,0},{32,16},{48,32},{64,48},{80,64},{96,80},{112,96},{128,112},... | collective-permute-start | bytes 319496 | tf_op jit(solution)/shard_map/ppermute | solution.py:25
  35.8 1.9 %collective-permute-start.5 = (f32[208,128]{1,0:T(8,128)S(1)}, f32[208,128]{1,0:T(8,128)S(1)}, u32[]{:S(2)}, u32[]{:S(2)}) collective-permute-start(f32[208,128]{1,0:T(8,128)S(1)} %get-tuple-element.39), channel_id=1, source_target_pairs={{1,0},{2,1},{3,2},{4,3},{5,4},{6,5},{7,6},{8,7},{9,8},{10,9},{11,1... | collective-permute-start | bytes 319496 | tf_op jit(solution)/shard_map/ppermute | solution.py:25
  37.7 3.3 %collective-permute-done.3.below = f32[208,128]{1,0:T(8,128)S(1)} collective-permute-done((f32[208,128]{1,0:T(8,128)S(1)}, f32[208,128]{1,0:T(8,128)S(1)}, u32[]{:S(2)}, u32[]{:S(2)}) %collective-permute-start.3) | collective-permute-done | bytes 106528 | tf_op jit(solution)/shard_map/ppermute | solution.py:25
  41.1 0.8 collective-permute-done.5.right
  41.8 0.0 collective-permute-done.2.above
  41.8 0.0 collective-permute-done.4.left
  41.8 1.0 shard_map.117
  42.8 0.0 all-to-all-done
  42.8 11.0 %all-to-all-start.1 = ((f32[32,8,128]{2,1,0:T(8,128)}), f32[32,8,128]{2,1,0:T(8,128)S(1)}, u32[]{:S(2)}, u32[]{:S(2)}) async-start(f32[32,8,128]{2,1,0:T(8,128)} %bitcast.10), calls=%async_computation.1 | async-start | bytes 262144 | tf_op jit(solution)/shard_map/all_to_all | solution.py:529
  53.8 0.5 shard_map.114.coarse_rows
  54.3 9.4 %all-to-all-done.1 = f32[32,8,128]{2,1,0:T(8,128)S(1)} async-done(((f32[32,8,128]{2,1,0:T(8,128)}), f32[32,8,128]{2,1,0:T(8,128)S(1)}, u32[]{:S(2)}, u32[]{:S(2)}) %all-to-all-start.1) | async-done | bytes 131104 | tf_op jit(solution)/shard_map/all_to_all | solution.py:529
  63.7 1.0 shard_map.118
  64.8 7.9 %all-to-all-start.2 = ((f32[16,16,128]{2,1,0:T(8,128)}), f32[16,16,128]{2,1,0:T(8,128)S(1)}, u32[]{:S(2)}, u32[]{:S(2)}) async-start(f32[16,16,128]{2,1,0:T(8,128)} %bitcast.12), calls=%async_computation.2 | async-start | bytes 262144 | tf_op jit(solution)/shard_map/all_to_all | solution.py:546
  72.7 0.0 copy-start.2
  72.7 4.5 %shard_map.119 = (bf16[768,768]{1,0:T(8,128)(2,1)}, bf16[768,768]{1,0:T(8,128)(2,1)}) custom-call(f32[8,768]{1,0:T(8,128)S(1)} %get-tuple-element.33.link_rows, bf16[768,768]{1,0:T(8,128)(2,1)S(1)} %get-tuple-element.31.place, bf16[768,768]{1,0:T(8,128)(2,1)} %bitcast.40), custom_call_target="tpu_custom_call" | custom-call | flops 1811939328 | tf_op jit(solution)/shard_map/pallas_call | solution.py:454
  77.2 0.0 copy-done.2
  77.2 2.7 %shard_map.120 = (bf16[768,128]{1,0:T(8,128)(2,1)S(1)}, f32[16,768]{1,0:T(8,128)S(1)}, f32[56,128]{1,0:T(8,128)S(1)}, bf16[48,128]{1,0:T(8,128)(2,1)S(1)}) custom-call(f32[240,128]{1,0:T(8,128)S(1)} %collective-permute-done.2.above, f32[208,128]{1,0:T(8,128)S(1)} %collective-permute-done.3.below, f32[240,128]{1,0:T(8,128)S(1)} %collective-permute-done.4.left, ...), custom_call_target="tpu_custom_call" | custom-call | flops 905969664 | tf_op jit(solution)/shard_map/pallas_call | solution.py:454
  79.8 1.7 %all-to-all-done.2 = f32[16,16,128]{2,1,0:T(8,128)S(1)} async-done(((f32[16,16,128]{2,1,0:T(8,128)}), f32[16,16,128]{2,1,0:T(8,128)S(1)}, u32[]{:S(2)}, u32[]{:S(2)}) %all-to-all-start.2) | async-done | bytes 131104 | tf_op jit(solution)/shard_map/all_to_all | solution.py:546
  81.6 0.2 shard_map.121
  81.7 13.1 %all_to_all.66 = f32[16,8,128]{2,1,0:T(8,128)S(1)} all-to-all(f32[16,8,128]{2,1,0:T(8,128)S(1)} %bitcast.34), channel_id=1, replica_groups=mesh['gx_0'=8,'gx_1'=4,'gy_0'=8,'gy_1'=2] {'gy_0','gy_1'}, dimensions={0} | all-to-all | bytes 131072 | tf_op jit(solution)/shard_map/all_to_all | solution.py:577
  94.8 12.8 %all_to_all.67 = f32[32,8,128]{2,1,0:T(8,128)S(1)} all-to-all(f32[32,8,128]{2,1,0:T(8,128)S(1)} %bitcast.29), channel_id=1, replica_groups=mesh['gx_0'=8,'gx_1'=4,'gy_0'=8,'gy_1'=2] {'gx_0','gx_1'}, dimensions={0} | all-to-all | bytes 262144 | tf_op jit(solution)/shard_map/all_to_all | solution.py:577
  107.6 0.6 shard_map.123
  108.3 3.5 %all-to-all-start.5 = ((f32[8,8,128]{2,1,0:T(8,128)}), f32[8,8,128]{2,1,0:T(8,128)S(1)}, u32[]{:S(2)}, u32[]{:S(2)}) async-start(f32[8,8,128]{2,1,0:T(8,128)} %bitcast.20), calls=%async_computation.5 | async-start | bytes 65536 | tf_op jit(solution)/shard_map/all_to_all | solution.py:584
  111.8 0.0 copy-start
  111.8 2.5 %shard_map.124 = (f32[768,128]{1,0:T(8,128)S(1)}, bf16[768,128]{1,0:T(8,128)(2,1)S(1)}, f32[384,128]{1,0:T(8,128)S(1)}, bf16[384,128]{1,0:T(8,128)(2,1)S(1)}) custom-call(f32[16,128]{1,0:T(8,128)S(1)} %get-tuple-element.47.amplitudes, f32[768,128]{1,0:T(8,128)S(1)} %get-tuple-element.42.precond, bf16[768,128]{1,0:T(8,128)(2,1)S(1)} %get-tuple-element.48.mode_six, ...), custom_call_target="tpu_custom_call" | custom-call | flops 905969664 | tf_op jit(solution)/shard_map/pallas_call | solution.py:454
  114.3 4.2 %all-to-all-done.5 = f32[8,8,128]{2,1,0:T(8,128)S(1)} async-done(((f32[8,8,128]{2,1,0:T(8,128)}), f32[8,8,128]{2,1,0:T(8,128)S(1)}, u32[]{:S(2)}, u32[]{:S(2)}) %all-to-all-start.5) | async-done | bytes 32800 | tf_op jit(solution)/shard_map/all_to_all | solution.py:584
  118.5 0.0 copy-done
  118.5 0.7 shard_map.126
  119.2 1.3 %collective-permute-start.6 = (f32[192,128]{1,0:T(8,128)S(1)}, f32[192,128]{1,0:T(8,128)S(1)}, u32[]{:S(2)}, u32[]{:S(2)}) collective-permute-start(f32[192,128]{1,0:T(8,128)S(1)} %get-tuple-element.57), channel_id=1, source_target_pairs={{16,0},{32,16},{48,32},{64,48},{80,64},{96,80},{112,96},{128,112},... | collective-permute-start | bytes 294920 | tf_op jit(solution)/shard_map/ppermute | solution.py:25
  120.5 4.5 %collective-permute-start.7 = (f32[192,128]{1,0:T(8,128)S(1)}, f32[192,128]{1,0:T(8,128)S(1)}, u32[]{:S(2)}, u32[]{:S(2)}) collective-permute-start(f32[192,128]{1,0:T(8,128)S(1)} %get-tuple-element.58), channel_id=1, source_target_pairs={{1,0},{2,1},{3,2},{4,3},{5,4},{6,5},{7,6},{8,7},{9,8},{10,9},{11,1... | collective-permute-start | bytes 294920 | tf_op jit(solution)/shard_map/ppermute | solution.py:25
  125.0 0.9 shard_map.125
  125.9 0.0 collective-permute-done.6.below
  125.9 1.8 %collective-permute-done.7.right = f32[192,128]{1,0:T(8,128)S(1)} collective-permute-done((f32[192,128]{1,0:T(8,128)S(1)}, f32[192,128]{1,0:T(8,128)S(1)}, u32[]{:S(2)}, u32[]{:S(2)}) %collective-permute-start.7) | collective-permute-done | bytes 98336 | tf_op jit(solution)/shard_map/ppermute | solution.py:25
  127.8 0.7 shard_map.127
  (1 shorter events, 0.0 us)
Async XLA Ops:
  1.6 25.0 %collective-permute-start.1 = (f32[192,128]{1,0:T(8,128)S(1)}, f32[192,128]{1,0:T(8,128)S(1)}, u32[]{:S(2)}, u32[]{:S(2)}) collective-permute-start(f32[192,128]{1,0:T(8,128)S(1)} %get-tuple-element.60.gap_right), channel_id=1, source_target_pairs={{0,1},{1,2},{2,3},{3,4},{4,5},{5,6},{6,7},{7,8},{8,9},{9,10},{10,1... | collective-permute-start | bytes 294920 | tf_op jit(solution)/shard_map/ppermute | solution.py:25
  6.2 20.4 %collective-permute-start = (f32[192,128]{1,0:T(8,128)S(1)}, f32[192,128]{1,0:T(8,128)S(1)}, u32[]{:S(2)}, u32[]{:S(2)}) collective-permute-start(f32[192,128]{1,0:T(8,128)S(1)} %get-tuple-element.61.gap_down), channel_id=1, source_target_pairs={{0,16},{16,32},{32,48},{48,64},{64,80},{80,96},{96,112},{112,128},... | collective-permute-start | bytes 294920 | tf_op jit(solution)/shard_map/ppermute | solution.py:25
  10.9 31.9 %all-to-all-start = ((f32[32,8,128]{2,1,0:T(8,128)}), f32[32,8,128]{2,1,0:T(8,128)S(1)}, u32[]{:S(2)}, u32[]{:S(2)}) async-start(f32[32,8,128]{2,1,0:T(8,128)} %bitcast), calls=%async_computation | async-start | bytes 262144 | tf_op jit(solution)/shard_map/all_to_all | solution.py:497
  23.5 3.1 %copy-start.1 = (f32[1,1,16,384]{3,2,1,0:T(8,128)S(1)}, f32[1,1,16,384]{3,2,1,0:T(8,128)}, u32[]{:S(2)}) copy-start(f32[1,1,16,384]{3,2,1,0:T(8,128)} %param.15) | copy-start | bytes 73732
  28.3 13.5 %collective-permute-start.2 = (f32[240,128]{1,0:T(8,128)S(1)}, f32[240,128]{1,0:T(8,128)S(1)}, u32[]{:S(2)}, u32[]{:S(2)}) collective-permute-start(f32[240,128]{1,0:T(8,128)S(1)} %get-tuple-element.36), channel_id=1, source_target_pairs={{0,16},{16,32},{32,48},{48,64},{64,80},{80,96},{96,112},{112,128},... | collective-permute-start | bytes 368648 | tf_op jit(solution)/shard_map/ppermute | solution.py:25
  31.4 10.4 %collective-permute-start.4 = (f32[240,128]{1,0:T(8,128)S(1)}, f32[240,128]{1,0:T(8,128)S(1)}, u32[]{:S(2)}, u32[]{:S(2)}) collective-permute-start(f32[240,128]{1,0:T(8,128)S(1)} %get-tuple-element.38), channel_id=1, source_target_pairs={{0,1},{1,2},{2,3},{3,4},{4,5},{5,6},{6,7},{7,8},{8,9},{9,10},{10,1... | collective-permute-start | bytes 368648 | tf_op jit(solution)/shard_map/ppermute | solution.py:25
  34.5 6.6 %collective-permute-start.3 = (f32[208,128]{1,0:T(8,128)S(1)}, f32[208,128]{1,0:T(8,128)S(1)}, u32[]{:S(2)}, u32[]{:S(2)}) collective-permute-start(f32[208,128]{1,0:T(8,128)S(1)} %get-tuple-element.37), channel_id=1, source_target_pairs={{16,0},{32,16},{48,32},{64,48},{80,64},{96,80},{112,96},{128,112},... | collective-permute-start | bytes 319496 | tf_op jit(solution)/shard_map/ppermute | solution.py:25
  35.8 6.0 %collective-permute-start.5 = (f32[208,128]{1,0:T(8,128)S(1)}, f32[208,128]{1,0:T(8,128)S(1)}, u32[]{:S(2)}, u32[]{:S(2)}) collective-permute-start(f32[208,128]{1,0:T(8,128)S(1)} %get-tuple-element.39), channel_id=1, source_target_pairs={{1,0},{2,1},{3,2},{4,3},{5,4},{6,5},{7,6},{8,7},{9,8},{10,9},{11,1... | collective-permute-start | bytes 319496 | tf_op jit(solution)/shard_map/ppermute | solution.py:25
  42.8 20.9 %all-to-all-start.1 = ((f32[32,8,128]{2,1,0:T(8,128)}), f32[32,8,128]{2,1,0:T(8,128)S(1)}, u32[]{:S(2)}, u32[]{:S(2)}) async-start(f32[32,8,128]{2,1,0:T(8,128)} %bitcast.10), calls=%async_computation.1 | async-start | bytes 262144 | tf_op jit(solution)/shard_map/all_to_all | solution.py:529
  64.8 16.8 %all-to-all-start.2 = ((f32[16,16,128]{2,1,0:T(8,128)}), f32[16,16,128]{2,1,0:T(8,128)S(1)}, u32[]{:S(2)}, u32[]{:S(2)}) async-start(f32[16,16,128]{2,1,0:T(8,128)} %bitcast.12), calls=%async_computation.2 | async-start | bytes 262144 | tf_op jit(solution)/shard_map/all_to_all | solution.py:546
  72.7 4.5 %copy-start.2 = (f32[1,1,16,384]{3,2,1,0:T(8,128)S(1)}, f32[1,1,16,384]{3,2,1,0:T(8,128)}, u32[]{:S(2)}) copy-start(f32[1,1,16,384]{3,2,1,0:T(8,128)} %param.16) | copy-start | bytes 73732
  108.3 10.2 %all-to-all-start.5 = ((f32[8,8,128]{2,1,0:T(8,128)}), f32[8,8,128]{2,1,0:T(8,128)S(1)}, u32[]{:S(2)}, u32[]{:S(2)}) async-start(f32[8,8,128]{2,1,0:T(8,128)} %bitcast.20), calls=%async_computation.5 | async-start | bytes 65536 | tf_op jit(solution)/shard_map/all_to_all | solution.py:584
  111.8 6.7 %copy-start = (bf16[768,768]{1,0:T(8,128)(2,1)S(1)}, bf16[768,768]{1,0:T(8,128)(2,1)}, u32[]{:S(2)}) copy-start(bf16[768,768]{1,0:T(8,128)(2,1)} %get-tuple-element.55.pick_flex) | copy-start | bytes 3538948
  119.2 6.7 %collective-permute-start.6 = (f32[192,128]{1,0:T(8,128)S(1)}, f32[192,128]{1,0:T(8,128)S(1)}, u32[]{:S(2)}, u32[]{:S(2)}) collective-permute-start(f32[192,128]{1,0:T(8,128)S(1)} %get-tuple-element.57), channel_id=1, source_target_pairs={{16,0},{32,16},{48,32},{64,48},{80,64},{96,80},{112,96},{128,112},... | collective-permute-start | bytes 294920 | tf_op jit(solution)/shard_map/ppermute | solution.py:25
  120.5 7.3 %collective-permute-start.7 = (f32[192,128]{1,0:T(8,128)S(1)}, f32[192,128]{1,0:T(8,128)S(1)}, u32[]{:S(2)}, u32[]{:S(2)}) collective-permute-start(f32[192,128]{1,0:T(8,128)S(1)} %get-tuple-element.58), channel_id=1, source_target_pairs={{1,0},{2,1},{3,2},{4,3},{5,4},{6,5},{7,6},{8,7},{9,8},{10,9},{11,1... | collective-permute-start | bytes 294920 | tf_op jit(solution)/shard_map/ppermute | solution.py:25

commit v5 on v4

--- a/solution.py
+++ b/solution.py
@@ -118,6 +118,8 @@
     wide[...] = jnp.zeros_like(wide)
     load.wait()
     wide[0:3, :] = coarse[...]
+    near = lax.broadcasted_iota(jnp.int32, (8, 128), 1) < 16
+    row = lax.broadcasted_iota(jnp.int32, (8, 128), 0)
     unknowns = wide.shape[1]
     grid_rows = blocks.shape[0] // 8
     row_unknowns = unknowns // grid_rows
@@ -130,7 +132,9 @@
             piece = pltpu.roll(piece, (start - first) % span, 1)
         if span < 256:
             piece = widened(piece, 256)
-        blocks[8 * i : 8 * i + 8, :] = piece[:, 0:128] + pltpu.roll(piece[:, 128:256], 3, 0)
+        others = jnp.where(near, piece[:, 128:256], 0.0)
+        others = others[0:1] + pltpu.roll(others, 16, 1)[1:2] + pltpu.roll(others, 32, 1)[2:3]
+        blocks[8 * i : 8 * i + 8, :] = jnp.where(row == 6, others, pltpu.roll(piece[:, 0:128], 3, 0))
 
 
 def prepare_kernel(
@@ -221,28 +225,6 @@
     residual[width:, :] = jnp.where(columns[3 * width :, 1:2] != 0.0, gap_right[...], 0.0)
 
 
-def rows_kernel(blocks, coarse_rows):
-    total = coarse_rows.shape[0]
-    count = total // 16
-    row = lax.broadcasted_iota(jnp.int32, (total, 1), 0)
-    j = row >> 4
-    part = ((row & 15) * 11) >> 5
-    mode = (row & 15) - 3 * part
-    down = jnp.where(part == 1, -1, jnp.where(part == 2, 1, 0))
-    j = j + jnp.where(part == 3, -1, jnp.where(part == 4, 1, 0))
-    valid = (part < 5) & (j >= 0) & (j < count)
-    wanted = jnp.where(valid, ((down + 1) * count + j) * 3 + mode, -1)
-    at = lax.broadcasted_iota(jnp.int32, (total, 128), 1)
-    chosen = [
-        jnp.where(at + shift == wanted, 1.0, 0.0).astype(BF16) for shift in (0, 128)
-    ]
-    chosen = jnp.concatenate(chosen, axis=0)
-    high, mid, low = split3(blocks[...])
-    out = dot_nt(chosen, high) + (dot_nt(chosen, mid) + dot_nt(chosen, low))
-    width = coarse_rows.shape[1]
-    coarse_rows[...] = out[:total] + pltpu.roll(out[total:], width - 3, 1)
-
-
 def flex_kernel(
     link_rows, place, flex_hbm, pick_flex_hbm, link_flex_hbm,
     flex, pick_flex, link_flex, arrived,
@@ -262,7 +244,7 @@
     store_link.wait()
 
 
-def coarse_in_kernel(own, above, below, left, right, mode_rows, precond, coarse):
+def coarse_in_kernel(own, above, below, left, right, mode_rows, blocks, precond, coarse):
     width = own.shape[0] // 4
     full = own[...] + jnp.concatenate(
         [above[0:width], below[0:width], left[0:width], right[0:width]], axis=0
@@ -271,7 +253,7 @@
     rows = dot_exact(mode_rows[...], full)
     rows = jnp.where(lax.broadcasted_iota(jnp.int32, rows.shape, 0) < 3, rows, 0.0)
     for i in range(coarse.shape[0] // 8):
-        coarse[8 * i : 8 * i + 8, :] = rows
+        coarse[8 * i : 8 * i + 8, :] = rows + blocks[8 * i : 8 * i + 8]
 
 
 def tables_kernel(
@@ -344,8 +326,35 @@
     )
 
 
-def coarse_kernel(coarse_rows, gathered, parts):
-    parts[...] = dot_exact(coarse_rows[...], gathered[...])
+def coarse_kernel(gathered, parts):
+    arrived = gathered[...]
+    height = arrived.shape[0]
+    row = lax.broadcasted_iota(jnp.int32, arrived.shape, 0) % 8
+    lane = lax.broadcasted_iota(jnp.int32, arrived.shape, 1)
+    coarse_in = jnp.where(row < 3, arrived, 0.0)
+    main = jnp.where(row < 3, pltpu.roll(arrived, height - 3, 0), 0.0)
+    others = jnp.zeros_like(arrived)
+    for k in range(3):
+        moved = pltpu.roll(arrived, height - (6 - k), 0)
+        if k:
+            moved = pltpu.roll(moved, 128 - 16 * k, 1)
+        others = others + jnp.where((row == k) & (lane < 16), moved, 0.0)
+    product = lax.dot_general(
+        jnp.concatenate([main, others], axis=1), coarse_in, (((0,), (0,)), ((), ())),
+        precision=HIGHEST, preferred_element_type=F32,
+    )
+    total = parts.shape[0]
+    count = total // 16
+    row = lax.broadcasted_iota(jnp.int32, (total, 1), 0)
+    j = row >> 4
+    part = ((row & 15) * 11) >> 5
+    mode = (row & 15) - 3 * part
+    down = jnp.where(part == 1, -1, jnp.where(part == 2, 1, 0))
+    j = j + jnp.where(part == 3, -1, jnp.where(part == 4, 1, 0))
+    valid = (part < 5) & (j >= 0) & (j < count)
+    wanted = jnp.where(valid, ((down + 1) * count + j) * 3 + mode, -1)
+    at = lax.broadcasted_iota(jnp.int32, (total, 256), 1)
+    parts[...] = select_rows(jnp.where(at == wanted, 1.0, 0.0).astype(BF16), product)
 
 
 def block_sum(ref, height):
@@ -494,7 +503,6 @@
         copies=1,
         flops=cube // 64,
     )
-    blocks = lax.all_to_all(blocks, GX, 0, 0, tiled=True)
     place, pick_schur, mode_rows, link_rows = call(
         prepare_kernel,
         (count, slots, multiplicity[0], modes, schur_blocks[0, 0]),
@@ -522,7 +530,7 @@
     from_right = shifted(left_msg, GY, -1)
     precond, coarse_in = call(
         coarse_in_kernel,
-        (own, from_above, from_below, from_left, from_right, mode_rows),
+        (own, from_above, from_below, from_left, from_right, mode_rows, blocks),
         (((total, cases), F32), ((8 * rows, cases), F32)),
         flops=cube // 16,
     )
@@ -537,12 +545,7 @@
         hbm_out=(0, 1),
         flops=2 * cube,
     )
-    (coarse_rows,) = call(
-        rows_kernel, (blocks,), (((16 * columns, 8 * rows), F32),), flops=cube // 16
-    )
-    (parts,) = call(
-        coarse_kernel, (coarse_rows, gathered), (((16 * columns, cases), F32),), flops=cube // 8,
-    )
+    (parts,) = call(coarse_kernel, (gathered,), (((16 * columns, cases), F32),), flops=cube // 8)
     parts = lax.all_to_all(parts, GY, 0, 0, tiled=True)
     mode_six, search_rows, base, mode_forms = call(
         tables_kernel,

time: 129 us -> 122 us (0.946)
  blocking collectives: 25.9 us -> 54.1 us
  starting transfers between devices: 57.9 us -> 34.5 us
  waiting for transfers between devices: 21.3 us -> 10.3 us
    all_to_all x0 -> x1, blocking collectives: none -> 28.2 us  [step(): gathered = lax.all_to_all(coarse_in, GX, 0, 0, tiled=True)]
    all_to_all x2 -> x0, starting transfers between devices: 23.6 us -> none  [the longest x1 12.6 us: step(): blocks = lax.all_to_all(blocks, GX, 0, 0, tiled=True)]
    all_to_all x2 -> x0, waiting for transfers between devices: 9.44 us -> none  [the longest x1 9.44 us: step(): gathered = lax.all_to_all(coarse_in, GX, 0, 0, tiled=True)]
    ppermute x8, waiting for transfers between devices: 5.94 us -> 4.33 us  [shifted(): lax.ppermute(value, axis, [(source, source + steps) for source in range(i...]
    pallas_call x15 -> x14, Pallas kernels: 21.5 us -> 20.4 us  [call(): pl.pallas_call(kernel, out_shape=outputs, in_specs=[SMEM] * scalars + [VM...]
  transfers between devices with their start and end apart: 12 -> 10, of which waited for: 6 -> 5; matrix products, arithmetic and copies ran while one was open for 0% -> 0% of each run, Pallas kernels for 14% -> 12%
where the time goes in v5:
time: 122 us; the launch traced here: 121 us
  blocking collectives  54.1 us (44%)
  starting transfers between devices  34.5 us (28%)
  Pallas kernels  20.4 us (17%)
  waiting for transfers between devices  10.3 us (8%)
    all_to_all x1, blocking collectives, step(): gathered = lax.all_to_all(coarse_in, GX, 0, 0, tiled=True)  28.2 us
    all_to_all x2, blocking collectives, step(): partial = lax.all_to_all(partial, axis, 0, 0, tiled=True)  25.9 us
    ppermute x8, starting transfers between devices, shifted(): lax.ppermute(value, axis, [(source, source + steps) for source in range(i...  23.1 us
    pallas_call x14, Pallas kernels, call(): pl.pallas_call(kernel, out_shape=outputs, in_specs=[SMEM] * scalars + [VM...  20.4 us
    all_to_all x1, starting transfers between devices, step(): parts = lax.all_to_all(parts, GY, 0, 0, tiled=True)  7.86 us
    ppermute x8, waiting for transfers between devices, shifted(): lax.ppermute(value, axis, [(source, source + steps) for source in range(i...  4.33 us
    all_to_all x1, waiting for transfers between devices, step(): sums = lax.all_to_all(partial, GY[0], 0, 0, tiled=True)  4.19 us
    all_to_all x1, starting transfers between devices, step(): sums = lax.all_to_all(partial, GY[0], 0, 0, tiled=True)  3.52 us
  transfers between devices with their start and end apart: 10, of which 5 were waited for; matrix products, arithmetic and copies ran while one was open for 0% of the time, Pallas kernels for 12%

profile of v5, /device:TPU:1, one launch (start us, length us, event | category | flops | bytes accessed | tf_op | source)
XLA Modules:
  0.0 121.1 jit_solution(10577046122702356261)
XLA Ops:
  0.6 1.0 slice_bitcast_fusion
  1.6 4.6 %collective-permute-start.1 = (f32[192,128]{1,0:T(8,128)S(1)}, f32[192,128]{1,0:T(8,128)S(1)}, u32[]{:S(2)}, u32[]{:S(2)}) collective-permute-start(f32[192,128]{1,0:T(8,128)S(1)} %get-tuple-element.60.gap_right), channel_id=1, source_target_pairs={{0,1},{1,2},{2,3},{3,4},{4,5},{5,6},{6,7},{7,8},{8,9},{9,10},{10,1... | collective-permute-start | bytes 294920 | tf_op jit(solution)/shard_map/ppermute | solution.py:25
  6.2 3.1 %collective-permute-start = (f32[192,128]{1,0:T(8,128)S(1)}, f32[192,128]{1,0:T(8,128)S(1)}, u32[]{:S(2)}, u32[]{:S(2)}) collective-permute-start(f32[192,128]{1,0:T(8,128)S(1)} %get-tuple-element.61.gap_down), channel_id=1, source_target_pairs={{0,16},{16,32},{32,48},{48,64},{64,80},{80,96},{96,112},{112,128},... | collective-permute-start | bytes 294920 | tf_op jit(solution)/shard_map/ppermute | solution.py:25
  9.3 0.0 copy-start.1
  9.3 3.1 %shard_map.113 = (bf16[768,768]{1,0:T(8,128)(2,1)S(1)}, bf16[768,768]{1,0:T(8,128)(2,1)S(1)}, f32[8,768]{1,0:T(8,128)S(1)}, f32[8,768]{1,0:T(8,128)S(1)}) custom-call(s32[1,4]{1,0:T(1,128)} %bitcast.43, s32[4,192]{1,0:T(4,128)} %bitcast.41, s32[1,768]{1,0:T(1,128)} %bitcast.42, f32[3,1,768]{2,1,0:T(1,128)} %bitcast.40, bf16[768,768]{1,0:T(8,128)(2,1)} %bitcast.37), custom_call_target="tpu_custom_call" | custom-call | flops 905969664 | tf_op jit(solution)/shard_map/pallas_call | solution.py:463
  12.4 0.0 collective-permute-done.1.left
  12.4 0.0 collective-permute-done.above
  12.4 0.0 copy-done.1
  12.4 1.7 %shard_map.114 = (f32[208,128]{1,0:T(8,128)S(1)}, f32[240,128]{1,0:T(8,128)S(1)}, f32[208,128]{1,0:T(8,128)S(1)}, f32[240,128]{1,0:T(8,128)S(1)}, f32[768,128]{1,0:T(8,128)S(1)}, /*index=5*/f32[384,128]{1,0:T(8,128)S(1)}) custom-call(f32[192,128]{1,0:T(8,128)S(1)} %get-tuple-element.61.gap_down, f32[192,128]{1,0:T(8,128)S(1)} %get-tuple-element.60.gap_right, ...), custom_call_target="tpu_custom_call" | custom-call | flops 452984832 | tf_op jit(solution)/shard_map/pallas_call | solution.py:463
  14.1 3.1 %collective-permute-start.2 = (f32[240,128]{1,0:T(8,128)S(1)}, f32[240,128]{1,0:T(8,128)S(1)}, u32[]{:S(2)}, u32[]{:S(2)}) collective-permute-start(f32[240,128]{1,0:T(8,128)S(1)} %get-tuple-element.36), channel_id=1, source_target_pairs={{0,16},{16,32},{32,48},{48,64},{64,80},{80,96},{96,112},{112,128},... | collective-permute-start | bytes 368648 | tf_op jit(solution)/shard_map/ppermute | solution.py:25
  17.2 2.8 %collective-permute-start.4 = (f32[240,128]{1,0:T(8,128)S(1)}, f32[240,128]{1,0:T(8,128)S(1)}, u32[]{:S(2)}, u32[]{:S(2)}) collective-permute-start(f32[240,128]{1,0:T(8,128)S(1)} %get-tuple-element.38), channel_id=1, source_target_pairs={{0,1},{1,2},{2,3},{3,4},{4,5},{5,6},{6,7},{7,8},{8,9},{9,10},{10,1... | collective-permute-start | bytes 368648 | tf_op jit(solution)/shard_map/ppermute | solution.py:25
  20.0 1.3 %collective-permute-start.3 = (f32[208,128]{1,0:T(8,128)S(1)}, f32[208,128]{1,0:T(8,128)S(1)}, u32[]{:S(2)}, u32[]{:S(2)}) collective-permute-start(f32[208,128]{1,0:T(8,128)S(1)} %get-tuple-element.37), channel_id=1, source_target_pairs={{16,0},{32,16},{48,32},{64,48},{80,64},{96,80},{112,96},{128,112},... | collective-permute-start | bytes 319496 | tf_op jit(solution)/shard_map/ppermute | solution.py:25
  21.3 2.4 %collective-permute-start.5 = (f32[208,128]{1,0:T(8,128)S(1)}, f32[208,128]{1,0:T(8,128)S(1)}, u32[]{:S(2)}, u32[]{:S(2)}) collective-permute-start(f32[208,128]{1,0:T(8,128)S(1)} %get-tuple-element.39), channel_id=1, source_target_pairs={{1,0},{2,1},{3,2},{4,3},{5,4},{6,5},{7,6},{8,7},{9,8},{10,9},{11,1... | collective-permute-start | bytes 319496 | tf_op jit(solution)/shard_map/ppermute | solution.py:25
  23.8 1.1 shard_map.115.blocks
  24.9 1.1 collective-permute-done.3.below
  26.0 1.4 %collective-permute-done.5.right = f32[208,128]{1,0:T(8,128)S(1)} collective-permute-done((f32[208,128]{1,0:T(8,128)S(1)}, f32[208,128]{1,0:T(8,128)S(1)}, u32[]{:S(2)}, u32[]{:S(2)}) %collective-permute-start.5) | collective-permute-done | bytes 106528 | tf_op jit(solution)/shard_map/ppermute | solution.py:25
  27.4 0.0 collective-permute-done.2.above
  27.4 0.0 collective-permute-done.4.left
  27.4 0.3 shard_map.116
  27.7 28.2 %all_to_all.55 = f32[32,8,128]{2,1,0:T(8,128)S(1)} all-to-all(f32[32,8,128]{2,1,0:T(8,128)S(1)} %bitcast.30), channel_id=1, replica_groups=mesh['gx_0'=8,'gx_1'=4,'gy_0'=8,'gy_1'=2] {'gx_0','gx_1'}, dimensions={0} | all-to-all | bytes 262144 | tf_op jit(solution)/shard_map/all_to_all | solution.py:537
  55.9 1.5 %shard_map.117 = f32[256,128]{1,0:T(8,128)} custom-call(f32[256,128]{1,0:T(8,128)S(1)} %bitcast.31), custom_call_target="tpu_custom_call" | custom-call | flops 113246208 | tf_op jit(solution)/shard_map/pallas_call | solution.py:463
  57.5 7.9 %all-to-all-start.1 = ((f32[16,16,128]{2,1,0:T(8,128)}), f32[16,16,128]{2,1,0:T(8,128)S(1)}, u32[]{:S(2)}, u32[]{:S(2)}) async-start(f32[16,16,128]{2,1,0:T(8,128)} %bitcast.10), calls=%async_computation.1 | async-start | bytes 262144 | tf_op jit(solution)/shard_map/all_to_all | solution.py:549
  65.3 0.0 copy-start.2
  65.3 4.5 %shard_map.118 = (bf16[768,768]{1,0:T(8,128)(2,1)}, bf16[768,768]{1,0:T(8,128)(2,1)}) custom-call(f32[8,768]{1,0:T(8,128)S(1)} %get-tuple-element.33.link_rows, bf16[768,768]{1,0:T(8,128)(2,1)S(1)} %get-tuple-element.31.place, bf16[768,768]{1,0:T(8,128)(2,1)} %bitcast.38), custom_call_target="tpu_custom_call" | custom-call | flops 1811939328 | tf_op jit(solution)/shard_map/pallas_call | solution.py:463
  69.8 0.0 copy-done.2
  69.8 2.7 %shard_map.119 = (bf16[768,128]{1,0:T(8,128)(2,1)S(1)}, f32[16,768]{1,0:T(8,128)S(1)}, f32[56,128]{1,0:T(8,128)S(1)}, bf16[48,128]{1,0:T(8,128)(2,1)S(1)}) custom-call(f32[240,128]{1,0:T(8,128)S(1)} %collective-permute-done.2.above, f32[208,128]{1,0:T(8,128)S(1)} %collective-permute-done.3.below, f32[240,128]{1,0:T(8,128)S(1)} %collective-permute-done.4.left, ...), custom_call_target="tpu_custom_call" | custom-call | flops 905969664 | tf_op jit(solution)/shard_map/pallas_call | solution.py:463
  72.5 1.7 %all-to-all-done.1 = f32[16,16,128]{2,1,0:T(8,128)S(1)} async-done(((f32[16,16,128]{2,1,0:T(8,128)}), f32[16,16,128]{2,1,0:T(8,128)S(1)}, u32[]{:S(2)}, u32[]{:S(2)}) %all-to-all-start.1) | async-done | bytes 131104 | tf_op jit(solution)/shard_map/all_to_all | solution.py:549
  74.2 0.2 shard_map.120
  74.4 13.1 %all_to_all.56 = f32[16,8,128]{2,1,0:T(8,128)S(1)} all-to-all(f32[16,8,128]{2,1,0:T(8,128)S(1)} %bitcast.32), channel_id=1, replica_groups=mesh['gx_0'=8,'gx_1'=4,'gy_0'=8,'gy_1'=2] {'gy_0','gy_1'}, dimensions={0} | all-to-all | bytes 131072 | tf_op jit(solution)/shard_map/all_to_all | solution.py:580
  87.5 12.8 %all_to_all.57 = f32[32,8,128]{2,1,0:T(8,128)S(1)} all-to-all(f32[32,8,128]{2,1,0:T(8,128)S(1)} %bitcast.26), channel_id=1, replica_groups=mesh['gx_0'=8,'gx_1'=4,'gy_0'=8,'gy_1'=2] {'gx_0','gx_1'}, dimensions={0} | all-to-all | bytes 262144 | tf_op jit(solution)/shard_map/all_to_all | solution.py:580
  100.3 0.6 shard_map.122
  100.9 3.5 %all-to-all-start.4 = ((f32[8,8,128]{2,1,0:T(8,128)}), f32[8,8,128]{2,1,0:T(8,128)S(1)}, u32[]{:S(2)}, u32[]{:S(2)}) async-start(f32[8,8,128]{2,1,0:T(8,128)} %bitcast.18), calls=%async_computation.4 | async-start | bytes 65536 | tf_op jit(solution)/shard_map/all_to_all | solution.py:587
  104.5 0.0 copy-start
  104.5 2.5 %shard_map.123 = (f32[768,128]{1,0:T(8,128)S(1)}, bf16[768,128]{1,0:T(8,128)(2,1)S(1)}, f32[384,128]{1,0:T(8,128)S(1)}, bf16[384,128]{1,0:T(8,128)(2,1)S(1)}) custom-call(f32[16,128]{1,0:T(8,128)S(1)} %get-tuple-element.47.amplitudes, f32[768,128]{1,0:T(8,128)S(1)} %get-tuple-element.42.precond, bf16[768,128]{1,0:T(8,128)(2,1)S(1)} %get-tuple-element.48.mode_six, ...), custom_call_target="tpu_custom_call" | custom-call | flops 905969664 | tf_op jit(solution)/shard_map/pallas_call | solution.py:463
  106.9 4.2 %all-to-all-done.4 = f32[8,8,128]{2,1,0:T(8,128)S(1)} async-done(((f32[8,8,128]{2,1,0:T(8,128)}), f32[8,8,128]{2,1,0:T(8,128)S(1)}, u32[]{:S(2)}, u32[]{:S(2)}) %all-to-all-start.4) | async-done | bytes 32800 | tf_op jit(solution)/shard_map/all_to_all | solution.py:587
  111.1 0.0 copy-done
  111.1 0.7 shard_map.125
  111.8 1.3 %collective-permute-start.6 = (f32[192,128]{1,0:T(8,128)S(1)}, f32[192,128]{1,0:T(8,128)S(1)}, u32[]{:S(2)}, u32[]{:S(2)}) collective-permute-start(f32[192,128]{1,0:T(8,128)S(1)} %get-tuple-element.57), channel_id=1, source_target_pairs={{16,0},{32,16},{48,32},{64,48},{80,64},{96,80},{112,96},{128,112},... | collective-permute-start | bytes 294920 | tf_op jit(solution)/shard_map/ppermute | solution.py:25
  113.1 4.5 %collective-permute-start.7 = (f32[192,128]{1,0:T(8,128)S(1)}, f32[192,128]{1,0:T(8,128)S(1)}, u32[]{:S(2)}, u32[]{:S(2)}) collective-permute-start(f32[192,128]{1,0:T(8,128)S(1)} %get-tuple-element.58), channel_id=1, source_target_pairs={{1,0},{2,1},{3,2},{4,3},{5,4},{6,5},{7,6},{8,7},{9,8},{10,9},{11,1... | collective-permute-start | bytes 294920 | tf_op jit(solution)/shard_map/ppermute | solution.py:25
  117.6 0.9 shard_map.124
  118.6 0.0 collective-permute-done.6.below
  118.6 1.8 %collective-permute-done.7.right = f32[192,128]{1,0:T(8,128)S(1)} collective-permute-done((f32[192,128]{1,0:T(8,128)S(1)}, f32[192,128]{1,0:T(8,128)S(1)}, u32[]{:S(2)}, u32[]{:S(2)}) %collective-permute-start.7) | collective-permute-done | bytes 98336 | tf_op jit(solution)/shard_map/ppermute | solution.py:25
  120.4 0.7 shard_map.126
  (1 shorter events, 0.0 us)
Async XLA Ops:
  1.6 10.8 %collective-permute-start.1 = (f32[192,128]{1,0:T(8,128)S(1)}, f32[192,128]{1,0:T(8,128)S(1)}, u32[]{:S(2)}, u32[]{:S(2)}) collective-permute-start(f32[192,128]{1,0:T(8,128)S(1)} %get-tuple-element.60.gap_right), channel_id=1, source_target_pairs={{0,1},{1,2},{2,3},{3,4},{4,5},{5,6},{6,7},{7,8},{8,9},{9,10},{10,1... | collective-permute-start | bytes 294920 | tf_op jit(solution)/shard_map/ppermute | solution.py:25
  6.2 6.2 %collective-permute-start = (f32[192,128]{1,0:T(8,128)S(1)}, f32[192,128]{1,0:T(8,128)S(1)}, u32[]{:S(2)}, u32[]{:S(2)}) collective-permute-start(f32[192,128]{1,0:T(8,128)S(1)} %get-tuple-element.61.gap_down), channel_id=1, source_target_pairs={{0,16},{16,32},{32,48},{48,64},{64,80},{80,96},{96,112},{112,128},... | collective-permute-start | bytes 294920 | tf_op jit(solution)/shard_map/ppermute | solution.py:25
  9.3 3.1 %copy-start.1 = (f32[1,1,16,384]{3,2,1,0:T(8,128)S(1)}, f32[1,1,16,384]{3,2,1,0:T(8,128)}, u32[]{:S(2)}) copy-start(f32[1,1,16,384]{3,2,1,0:T(8,128)} %param.15) | copy-start | bytes 73732
  14.1 13.3 %collective-permute-start.2 = (f32[240,128]{1,0:T(8,128)S(1)}, f32[240,128]{1,0:T(8,128)S(1)}, u32[]{:S(2)}, u32[]{:S(2)}) collective-permute-start(f32[240,128]{1,0:T(8,128)S(1)} %get-tuple-element.36), channel_id=1, source_target_pairs={{0,16},{16,32},{32,48},{48,64},{64,80},{80,96},{96,112},{112,128},... | collective-permute-start | bytes 368648 | tf_op jit(solution)/shard_map/ppermute | solution.py:25
  17.2 10.1 %collective-permute-start.4 = (f32[240,128]{1,0:T(8,128)S(1)}, f32[240,128]{1,0:T(8,128)S(1)}, u32[]{:S(2)}, u32[]{:S(2)}) collective-permute-start(f32[240,128]{1,0:T(8,128)S(1)} %get-tuple-element.38), channel_id=1, source_target_pairs={{0,1},{1,2},{2,3},{3,4},{4,5},{5,6},{6,7},{7,8},{8,9},{9,10},{10,1... | collective-permute-start | bytes 368648 | tf_op jit(solution)/shard_map/ppermute | solution.py:25
  20.0 5.9 %collective-permute-start.3 = (f32[208,128]{1,0:T(8,128)S(1)}, f32[208,128]{1,0:T(8,128)S(1)}, u32[]{:S(2)}, u32[]{:S(2)}) collective-permute-start(f32[208,128]{1,0:T(8,128)S(1)} %get-tuple-element.37), channel_id=1, source_target_pairs={{16,0},{32,16},{48,32},{64,48},{80,64},{96,80},{112,96},{128,112},... | collective-permute-start | bytes 319496 | tf_op jit(solution)/shard_map/ppermute | solution.py:25
  21.3 6.0 %collective-permute-start.5 = (f32[208,128]{1,0:T(8,128)S(1)}, f32[208,128]{1,0:T(8,128)S(1)}, u32[]{:S(2)}, u32[]{:S(2)}) collective-permute-start(f32[208,128]{1,0:T(8,128)S(1)} %get-tuple-element.39), channel_id=1, source_target_pairs={{1,0},{2,1},{3,2},{4,3},{5,4},{6,5},{7,6},{8,7},{9,8},{10,9},{11,1... | collective-permute-start | bytes 319496 | tf_op jit(solution)/shard_map/ppermute | solution.py:25
  57.5 16.7 %all-to-all-start.1 = ((f32[16,16,128]{2,1,0:T(8,128)}), f32[16,16,128]{2,1,0:T(8,128)S(1)}, u32[]{:S(2)}, u32[]{:S(2)}) async-start(f32[16,16,128]{2,1,0:T(8,128)} %bitcast.10), calls=%async_computation.1 | async-start | bytes 262144 | tf_op jit(solution)/shard_map/all_to_all | solution.py:549
  65.3 4.5 %copy-start.2 = (f32[1,1,16,384]{3,2,1,0:T(8,128)S(1)}, f32[1,1,16,384]{3,2,1,0:T(8,128)}, u32[]{:S(2)}) copy-start(f32[1,1,16,384]{3,2,1,0:T(8,128)} %param.16) | copy-start | bytes 73732
  100.9 10.2 %all-to-all-start.4 = ((f32[8,8,128]{2,1,0:T(8,128)}), f32[8,8,128]{2,1,0:T(8,128)S(1)}, u32[]{:S(2)}, u32[]{:S(2)}) async-start(f32[8,8,128]{2,1,0:T(8,128)} %bitcast.18), calls=%async_computation.4 | async-start | bytes 65536 | tf_op jit(solution)/shard_map/all_to_all | solution.py:587
  104.5 6.7 %copy-start = (bf16[768,768]{1,0:T(8,128)(2,1)S(1)}, bf16[768,768]{1,0:T(8,128)(2,1)}, u32[]{:S(2)}) copy-start(bf16[768,768]{1,0:T(8,128)(2,1)} %get-tuple-element.55.pick_flex) | copy-start | bytes 3538948
  111.8 6.7 %collective-permute-start.6 = (f32[192,128]{1,0:T(8,128)S(1)}, f32[192,128]{1,0:T(8,128)S(1)}, u32[]{:S(2)}, u32[]{:S(2)}) collective-permute-start(f32[192,128]{1,0:T(8,128)S(1)} %get-tuple-element.57), channel_id=1, source_target_pairs={{16,0},{32,16},{48,32},{64,48},{80,64},{96,80},{112,96},{128,112},... | collective-permute-start | bytes 294920 | tf_op jit(solution)/shard_map/ppermute | solution.py:25
  113.1 7.3 %collective-permute-start.7 = (f32[192,128]{1,0:T(8,128)S(1)}, f32[192,128]{1,0:T(8,128)S(1)}, u32[]{:S(2)}, u32[]{:S(2)}) collective-permute-start(f32[192,128]{1,0:T(8,128)S(1)} %get-tuple-element.58), channel_id=1, source_target_pairs={{1,0},{2,1},{3,2},{4,3},{5,4},{6,5},{7,6},{8,7},{9,8},{10,9},{11,1... | collective-permute-start | bytes 294920 | tf_op jit(solution)/shard_map/ppermute | solution.py:25

commit v6 on v5

--- a/solution.py
+++ b/solution.py
@@ -23,6 +23,12 @@
     count = lax.axis_size(axis)
     initial, last = (max(0, -steps), min(count, count - steps))
     return lax.ppermute(value, axis, [(source, source + steps) for source in range(initial, last)])
+
+
+def swapped(value, axis, first):
+    count = lax.axis_size(axis)
+    pairs = [(low, low + 1) for low in range(first, count - 1, 2)]
+    return lax.ppermute(value, axis, pairs + [(high, low) for low, high in pairs])
 
 
 def split3(x):
@@ -202,27 +208,42 @@
 
 
 def precond_kernel(
-    gap_down, gap_right, above, left, place, pick_schur, link_rows, mode_rows, saved,
-    up_msg, down_msg, left_msg, right_msg, own, residual,
+    odd_x, odd_y, gap_down, gap_right, above, left, place, pick_schur, link_rows, mode_rows, saved,
+    first_x, second_x, first_y, second_y, own, residual,
 ):
     width = above.shape[0]
+    total = 4 * width
     columns = jnp.transpose(link_rows[...])
     links = jnp.concatenate([above[...], gap_down[...], left[...], gap_right[...]], axis=0)
     spread = select_rows(place[...], links)
     weighted = (columns[:, 2:3] * spread).astype(BF16)
-    picked = columns[:, 3:4] * dot(pick_schur[...], weighted)
-    own[...] = picked
-    for f, msg in enumerate((up_msg, down_msg, left_msg, right_msg)):
-        msg[0:width, :] = picked[width * f : width * f + width]
-        rows = lane_window(mode_rows[...], width * f, 256)
+    own[...] = columns[:, 3:4] * dot(pick_schur[...], weighted)
+    for face, start, msg in (
+        (1 - odd_x[0], 0, first_x),
+        (odd_x[0], 0, second_x),
+        (3 - odd_y[0], width, first_y),
+        (2 + odd_y[0], width, second_y),
+    ):
+        msg[0:width, :] = own[pl.ds(pl.multiple_of(width * face, 8), width), :]
+        rows = pltpu.roll(mode_rows[...], jnp.where(face == 0, 0, total - width * face), 1)
         msg[width : width + 8, :] = rows[:, 0:128]
         msg[width + 8 : width + 16, :] = rows[:, 128:256]
-    for start, msg in ((0, down_msg), (width, right_msg)):
         rows = lane_window(saved[...], start, 256)
         msg[width + 16 : width + 32, :] = rows[:, 0:128]
         msg[width + 32 : width + 48, :] = rows[:, 128:256]
     residual[0:width, :] = jnp.where(columns[width : 2 * width, 1:2] != 0.0, gap_down[...], 0.0)
     residual[width:, :] = jnp.where(columns[3 * width :, 1:2] != 0.0, gap_right[...], 0.0)
+
+
+def four_neighbours(odd_x, odd_y, first_x, second_x, first_y, second_y):
+    even_x = odd_x[0] == 0
+    even_y = odd_y[0] == 0
+    return (
+        jnp.where(even_x, second_x, first_x),
+        jnp.where(even_x, first_x, second_x),
+        jnp.where(even_y, second_y, first_y),
+        jnp.where(even_y, first_y, second_y),
+    )
 
 
 def flex_kernel(
@@ -244,10 +265,15 @@
     store_link.wait()
 
 
-def coarse_in_kernel(own, above, below, left, right, mode_rows, blocks, precond, coarse):
+def coarse_in_kernel(
+    odd_x, odd_y, own, first_x, second_x, first_y, second_y, mode_rows, blocks, precond, coarse
+):
     width = own.shape[0] // 4
     full = own[...] + jnp.concatenate(
-        [above[0:width], below[0:width], left[0:width], right[0:width]], axis=0
+        four_neighbours(
+            odd_x, odd_y, first_x[0:width], second_x[0:width], first_y[0:width], second_y[0:width]
+        ),
+        axis=0,
     )
     precond[...] = full
     rows = dot_exact(mode_rows[...], full)
@@ -257,7 +283,8 @@
 
 
 def tables_kernel(
-    above, below, left, right, mode_rows, link_rows, saved, images, residual, precond, link_flex_hbm,
+    odd_x, odd_y, first_x, second_x, first_y, second_y,
+    mode_rows, link_rows, saved, images, residual, precond, link_flex_hbm,
     mode_six, search_rows, base, mode_forms,
     link_flex, arrived,
 ):
@@ -266,12 +293,15 @@
     total = mode_rows.shape[1]
     width = total // 4
     near = lax.broadcasted_iota(jnp.int32, (1, 256), 1) < width
+    messages = four_neighbours(
+        odd_x, odd_y, first_x[width:], second_x[width:], first_y[width:], second_y[width:]
+    )
     used = link_rows[1:2, :] != 0.0
     row = lax.broadcasted_iota(jnp.int32, (16, total), 0)
     mine = jnp.concatenate([mode_rows[...], jnp.zeros((8, total), F32)], axis=0)
     modes = jnp.where(row < 3, mine, 0.0)
-    for f, msg in enumerate((above, below, left, right)):
-        theirs = jnp.concatenate([msg[width : width + 8], msg[width + 8 : width + 16]], axis=1)
+    for f, msg in enumerate(messages):
+        theirs = jnp.concatenate([msg[0:8], msg[8:16]], axis=1)
         theirs = at_lanes(widened(jnp.where(near, theirs, 0.0), total), width * f)
         theirs = jnp.concatenate([theirs, jnp.zeros((8, total), F32)], axis=0)
         theirs = jnp.where(row < 3, theirs, 0.0)
@@ -282,10 +312,7 @@
     search = jnp.zeros((16, total), F32)
     for f in range(4):
         if f % 2 == 0:
-            msg = above if f == 0 else left
-            piece = jnp.concatenate(
-                [msg[width + 16 : width + 32], msg[width + 32 : width + 48]], axis=1
-            )
+            piece = jnp.concatenate([messages[f][16:32], messages[f][32:48]], axis=1)
         else:
             piece = lane_window(saved[...], 0 if f == 1 else width, 256)
         search = search + at_lanes(widened(jnp.where(near, piece, 0.0), total), width * f)
@@ -494,15 +521,6 @@
     gap_right = gap[width:]
     above = shifted(gap_down, GX, 1)
     left = shifted(gap_right, GY, 1)
-    (blocks,) = call(
-        blocks_kernel,
-        (coarse_inverse,),
-        (((8 * rows, 128), F32),),
-        remote=1,
-        scratch=((coarse_inverse.shape, F32), ((8, unknowns), F32)),
-        copies=1,
-        flops=cube // 64,
-    )
     place, pick_schur, mode_rows, link_rows = call(
         prepare_kernel,
         (count, slots, multiplicity[0], modes, schur_blocks[0, 0]),
@@ -517,21 +535,34 @@
         copies=5,
         flops=cube,
     )
-    up_msg, down_msg, left_msg, right_msg, own, residual = call(
+    odd_x = (lax.axis_index(GX) % 2).reshape(1)
+    odd_y = (lax.axis_index(GY) % 2).reshape(1)
+    first_x, second_x, first_y, second_y, own, residual = call(
         precond_kernel,
-        (gap_down, gap_right, above, left, place, pick_schur, link_rows, mode_rows, saved),
-        tuple(((width + extra, cases), F32) for extra in (16, 48, 16, 48))
-        + (((total, cases), F32), ((2 * width, cases), F32)),
+        (odd_x, odd_y, gap_down, gap_right, above, left, place, pick_schur, link_rows, mode_rows, saved),
+        (((width + 48, cases), F32),) * 4 + (((total, cases), F32), ((2 * width, cases), F32)),
+        scalars=2,
         flops=cube // 2,
     )
-    from_above = shifted(down_msg, GX, 1)
-    from_below = shifted(up_msg, GX, -1)
-    from_left = shifted(right_msg, GY, 1)
-    from_right = shifted(left_msg, GY, -1)
+    first_x = swapped(first_x, GX, 0)
+    second_x = swapped(second_x, GX, 1)
+    first_y = swapped(first_y, GY, 0)
+    second_y = swapped(second_y, GY, 1)
+    messages = (first_x, second_x, first_y, second_y)
+    (blocks,) = call(
+        blocks_kernel,
+        (coarse_inverse,),
+        (((8 * rows, 128), F32),),
+        remote=1,
+        scratch=((coarse_inverse.shape, F32), ((8, unknowns), F32)),
+        copies=1,
+        flops=cube // 64,
+    )
     precond, coarse_in = call(
         coarse_in_kernel,
-        (own, from_above, from_below, from_left, from_right, mode_rows, blocks),
+        (odd_x, odd_y, own, *messages, mode_rows, blocks),
         (((total, cases), F32), ((8 * rows, cases), F32)),
+        scalars=2,
         flops=cube // 16,
     )
     gathered = lax.all_to_all(coarse_in, GX, 0, 0, tiled=True)
@@ -549,11 +580,9 @@
     parts = lax.all_to_all(parts, GY, 0, 0, tiled=True)
     mode_six, search_rows, base, mode_forms = call(
         tables_kernel,
-        (
-            from_above, from_below, from_left, from_right, mode_rows, link_rows, saved, images,
-            residual, precond, link_flex,
-        ),
+        (odd_x, odd_y, *messages, mode_rows, link_rows, saved, images, residual, precond, link_flex),
         (((total, 128), BF16), ((16, total), F32), ((56, cases), F32), ((48, 128), BF16)),
+        scalars=2,
         remote=1,
         scratch=((big, BF16),),
         copies=1,

time: 122 us -> 121 us (level)
  blocking collectives: 54.1 us -> 49.4 us
  starting transfers between devices: 34.5 us -> 37.3 us
    ppermute x8 -> x4, starting transfers between devices: 23.1 us -> 13.5 us  [shifted(): lax.ppermute(value, axis, [(source, source + steps) for source in range(i...]
    ppermute x0 -> x4, starting transfers between devices: none -> 9.59 us  [swapped(): lax.ppermute(value, axis, pairs + [(high, low) for low, high in pairs])]
    all_to_all x1, blocking collectives: 28.2 us -> 23.6 us  [step(): gathered = lax.all_to_all(coarse_in, GX, 0, 0, tiled=True)]
    ppermute x0 -> x4, waiting for transfers between devices: none -> 3.11 us  [swapped(): lax.ppermute(value, axis, pairs + [(high, low) for low, high in pairs])]
    all_to_all x1, starting transfers between devices: 7.86 us -> 10.6 us  [step(): parts = lax.all_to_all(parts, GY, 0, 0, tiled=True)]
    ppermute x8 -> x4, waiting for transfers between devices: 4.33 us -> 1.84 us  [shifted(): lax.ppermute(value, axis, [(source, source + steps) for source in range(i...]
  transfers between devices with their start and end apart: 10 -> 10, of which waited for: 5 -> 4; matrix products, arithmetic and copies ran while one was open for 0% -> 0% of each run, Pallas kernels for 12% -> 12%
where the time goes in v6:
time: 121 us; the launch traced here: 120 us
  blocking collectives  49.4 us (41%)
  starting transfers between devices  37.3 us (31%)
  Pallas kernels  20.5 us (17%)
  waiting for transfers between devices  10.9 us (9%)
    all_to_all x2, blocking collectives, step(): partial = lax.all_to_all(partial, axis, 0, 0, tiled=True)  25.9 us
    all_to_all x1, blocking collectives, step(): gathered = lax.all_to_all(coarse_in, GX, 0, 0, tiled=True)  23.6 us
    pallas_call x14, Pallas kernels, call(): pl.pallas_call(kernel, out_shape=outputs, in_specs=[SMEM] * scalars + [VM...  20.5 us
    ppermute x4, starting transfers between devices, shifted(): lax.ppermute(value, axis, [(source, source + steps) for source in range(i...  13.5 us
    all_to_all x1, starting transfers between devices, step(): parts = lax.all_to_all(parts, GY, 0, 0, tiled=True)  10.6 us
    ppermute x4, starting transfers between devices, swapped(): lax.ppermute(value, axis, pairs + [(high, low) for low, high in pairs])  9.59 us
    all_to_all x1, waiting for transfers between devices, step(): sums = lax.all_to_all(partial, GY[0], 0, 0, tiled=True)  4.21 us
    all_to_all x1, starting transfers between devices, step(): sums = lax.all_to_all(partial, GY[0], 0, 0, tiled=True)  3.52 us
  transfers between devices with their start and end apart: 10, of which 4 were waited for; matrix products, arithmetic and copies ran while one was open for 0% of the time, Pallas kernels for 12%

profile of v6, /device:TPU:1, one launch (start us, length us, event | category | flops | bytes accessed | tf_op | source)
XLA Modules:
  0.0 119.9 jit_solution(11337691441669975536)
XLA Ops:
  0.6 1.0 slice_bitcast_fusion
  1.6 4.6 %collective-permute-start.1 = (f32[192,128]{1,0:T(8,128)S(1)}, f32[192,128]{1,0:T(8,128)S(1)}, u32[]{:S(2)}, u32[]{:S(2)}) collective-permute-start(f32[192,128]{1,0:T(8,128)S(1)} %get-tuple-element.60.gap_right), channel_id=1, source_target_pairs={{0,1},{1,2},{2,3},{3,4},{4,5},{5,6},{6,7},{7,8},{8,9},{9,10},{10,1... | collective-permute-start | bytes 294920 | tf_op jit(solution)/shard_map/ppermute | solution.py:25
  6.2 3.1 %collective-permute-start = (f32[192,128]{1,0:T(8,128)S(1)}, f32[192,128]{1,0:T(8,128)S(1)}, u32[]{:S(2)}, u32[]{:S(2)}) collective-permute-start(f32[192,128]{1,0:T(8,128)S(1)} %get-tuple-element.61.gap_down), channel_id=1, source_target_pairs={{0,16},{16,32},{32,48},{48,64},{64,80},{80,96},{96,112},{112,128},... | collective-permute-start | bytes 294920 | tf_op jit(solution)/shard_map/ppermute | solution.py:25
  9.3 0.0 copy-start.1
  9.3 3.1 %shard_map.113 = (bf16[768,768]{1,0:T(8,128)(2,1)S(1)}, bf16[768,768]{1,0:T(8,128)(2,1)S(1)}, f32[8,768]{1,0:T(8,128)S(1)}, f32[8,768]{1,0:T(8,128)S(1)}) custom-call(s32[1,4]{1,0:T(1,128)} %bitcast.45, s32[4,192]{1,0:T(4,128)} %bitcast.43, s32[1,768]{1,0:T(1,128)} %bitcast.44, f32[3,1,768]{2,1,0:T(1,128)} %bitcast.42, bf16[768,768]{1,0:T(8,128)(2,1)} %bitcast.39), custom_call_target="tpu_custom_call" | custom-call | flops 905969664 | tf_op jit(solution)/shard_map/pallas_call | solution.py:490
  12.4 0.0 collective-permute-done.1.left
  12.4 0.0 collective-permute-done.above
  12.4 0.0 copy-done.1
  12.4 1.7 %shard_map.114 = (f32[240,128]{1,0:T(8,128)S(1)}, f32[240,128]{1,0:T(8,128)S(1)}, f32[240,128]{1,0:T(8,128)S(1)}, f32[240,128]{1,0:T(8,128)S(1)}, f32[768,128]{1,0:T(8,128)S(1)}, /*index=5*/f32[384,128]{1,0:T(8,128)S(1)}) custom-call(s32[1]{0:T(128)} %bitcast.odd_x, s32[1]{0:T(128)} %bitcast.1.odd_y, f32[192,128]{1,0:T(8,128)S(1)} %get-tuple-element.61.gap_down, ...), custom_call_target="tpu_custom_call" | custom-call | flops 452984832 | tf_op jit(solution)/shard_map/pallas_call | solution.py:490
  14.2 3.1 %collective-permute-start.2 = (f32[240,128]{1,0:T(8,128)S(1)}, f32[240,128]{1,0:T(8,128)S(1)}, u32[]{:S(2)}, u32[]{:S(2)}) collective-permute-start(f32[240,128]{1,0:T(8,128)S(1)} %get-tuple-element.36), channel_id=1, source_target_pairs={{0,16},{32,48},{64,80},{96,112},{128,144},{160,176},{192,208},{224... | collective-permute-start | bytes 368648 | tf_op jit(solution)/shard_map/ppermute | solution.py:31
  17.3 0.7 collective-permute-start.3
  18.0 3.9 %collective-permute-start.4 = (f32[240,128]{1,0:T(8,128)S(1)}, f32[240,128]{1,0:T(8,128)S(1)}, u32[]{:S(2)}, u32[]{:S(2)}) collective-permute-start(f32[240,128]{1,0:T(8,128)S(1)} %get-tuple-element.38), channel_id=1, source_target_pairs={{0,1},{2,3},{4,5},{6,7},{8,9},{10,11},{12,13},{14,15},{1,0},{3,2},... | collective-permute-start | bytes 368648 | tf_op jit(solution)/shard_map/ppermute | solution.py:31
  21.9 1.9 %collective-permute-start.5 = (f32[240,128]{1,0:T(8,128)S(1)}, f32[240,128]{1,0:T(8,128)S(1)}, u32[]{:S(2)}, u32[]{:S(2)}) collective-permute-start(f32[240,128]{1,0:T(8,128)S(1)} %get-tuple-element.39), channel_id=1, source_target_pairs={{1,2},{3,4},{5,6},{7,8},{9,10},{11,12},{13,14},{2,1},{4,3},{6,5},{... | collective-permute-start | bytes 368648 | tf_op jit(solution)/shard_map/ppermute | solution.py:31
  23.8 1.1 shard_map.115.blocks
  24.9 0.0 collective-permute-done.2.first_x
  24.9 0.0 collective-permute-done.3.second_x
  24.9 0.0 collective-permute-done.4.first_y
  25.0 3.1 %collective-permute-done.5.second_y = f32[240,128]{1,0:T(8,128)S(1)} collective-permute-done((f32[240,128]{1,0:T(8,128)S(1)}, f32[240,128]{1,0:T(8,128)S(1)}, u32[]{:S(2)}, u32[]{:S(2)}) %collective-permute-start.5) | collective-permute-done | bytes 122912 | tf_op jit(solution)/shard_map/ppermute | solution.py:31
  28.1 0.3 shard_map.116
  28.4 23.6 %all_to_all.55 = f32[32,8,128]{2,1,0:T(8,128)S(1)} all-to-all(f32[32,8,128]{2,1,0:T(8,128)S(1)} %bitcast.32), channel_id=1, replica_groups=mesh['gx_0'=8,'gx_1'=4,'gy_0'=8,'gy_1'=2] {'gx_0','gx_1'}, dimensions={0} | all-to-all | bytes 262144 | tf_op jit(solution)/shard_map/all_to_all | solution.py:568
  51.9 1.5 %shard_map.117 = f32[256,128]{1,0:T(8,128)} custom-call(f32[256,128]{1,0:T(8,128)S(1)} %bitcast.33), custom_call_target="tpu_custom_call" | custom-call | flops 113246208 | tf_op jit(solution)/shard_map/pallas_call | solution.py:490
  53.5 10.6 %all-to-all-start.1 = ((f32[16,16,128]{2,1,0:T(8,128)}), f32[16,16,128]{2,1,0:T(8,128)S(1)}, u32[]{:S(2)}, u32[]{:S(2)}) async-start(f32[16,16,128]{2,1,0:T(8,128)} %bitcast.12), calls=%async_computation.1 | async-start | bytes 262144 | tf_op jit(solution)/shard_map/all_to_all | solution.py:580
  64.1 0.0 copy-start.2
  64.1 4.5 %shard_map.118 = (bf16[768,768]{1,0:T(8,128)(2,1)}, bf16[768,768]{1,0:T(8,128)(2,1)}) custom-call(f32[8,768]{1,0:T(8,128)S(1)} %get-tuple-element.33.link_rows, bf16[768,768]{1,0:T(8,128)(2,1)S(1)} %get-tuple-element.31.place, bf16[768,768]{1,0:T(8,128)(2,1)} %bitcast.40), custom_call_target="tpu_custom_call" | custom-call | flops 1811939328 | tf_op jit(solution)/shard_map/pallas_call | solution.py:490
  68.6 0.0 copy-done.2
  68.6 2.7 %shard_map.119 = (bf16[768,128]{1,0:T(8,128)(2,1)S(1)}, f32[16,768]{1,0:T(8,128)S(1)}, f32[56,128]{1,0:T(8,128)S(1)}, bf16[48,128]{1,0:T(8,128)(2,1)S(1)}) custom-call(s32[1]{0:T(128)} %bitcast.odd_x, s32[1]{0:T(128)} %bitcast.1.odd_y, f32[240,128]{1,0:T(8,128)S(1)} %collective-permute-done.2.first_x, f32[240,128]{1,0:T(8,128)S(1)} %collective-permute-done.3.second_x, ...), custom_call_target="tpu_custom_call" | custom-call | flops 905969664 | tf_op jit(solution)/shard_map/pallas_call | solution.py:490
  71.3 1.7 %all-to-all-done.1 = f32[16,16,128]{2,1,0:T(8,128)S(1)} async-done(((f32[16,16,128]{2,1,0:T(8,128)}), f32[16,16,128]{2,1,0:T(8,128)S(1)}, u32[]{:S(2)}, u32[]{:S(2)}) %all-to-all-start.1) | async-done | bytes 131104 | tf_op jit(solution)/shard_map/all_to_all | solution.py:580
  73.0 0.2 shard_map.120
  73.1 13.1 %all_to_all.56 = f32[16,8,128]{2,1,0:T(8,128)S(1)} all-to-all(f32[16,8,128]{2,1,0:T(8,128)S(1)} %bitcast.34), channel_id=1, replica_groups=mesh['gx_0'=8,'gx_1'=4,'gy_0'=8,'gy_1'=2] {'gy_0','gy_1'}, dimensions={0} | all-to-all | bytes 131072 | tf_op jit(solution)/shard_map/all_to_all | solution.py:609
  86.2 12.8 %all_to_all.57 = f32[32,8,128]{2,1,0:T(8,128)S(1)} all-to-all(f32[32,8,128]{2,1,0:T(8,128)S(1)} %bitcast.28), channel_id=1, replica_groups=mesh['gx_0'=8,'gx_1'=4,'gy_0'=8,'gy_1'=2] {'gx_0','gx_1'}, dimensions={0} | all-to-all | bytes 262144 | tf_op jit(solution)/shard_map/all_to_all | solution.py:609
  99.1 0.6 shard_map.122
  99.7 3.5 %all-to-all-start.4 = ((f32[8,8,128]{2,1,0:T(8,128)}), f32[8,8,128]{2,1,0:T(8,128)S(1)}, u32[]{:S(2)}, u32[]{:S(2)}) async-start(f32[8,8,128]{2,1,0:T(8,128)} %bitcast.20), calls=%async_computation.4 | async-start | bytes 65536 | tf_op jit(solution)/shard_map/all_to_all | solution.py:616
  103.2 0.0 copy-start
  103.2 2.5 %shard_map.123 = (f32[768,128]{1,0:T(8,128)S(1)}, bf16[768,128]{1,0:T(8,128)(2,1)S(1)}, f32[384,128]{1,0:T(8,128)S(1)}, bf16[384,128]{1,0:T(8,128)(2,1)S(1)}) custom-call(f32[16,128]{1,0:T(8,128)S(1)} %get-tuple-element.47.amplitudes, f32[768,128]{1,0:T(8,128)S(1)} %get-tuple-element.42.precond, bf16[768,128]{1,0:T(8,128)(2,1)S(1)} %get-tuple-element.48.mode_six, ...), custom_call_target="tpu_custom_call" | custom-call | flops 905969664 | tf_op jit(solution)/shard_map/pallas_call | solution.py:490
  105.7 4.2 %all-to-all-done.4 = f32[8,8,128]{2,1,0:T(8,128)S(1)} async-done(((f32[8,8,128]{2,1,0:T(8,128)}), f32[8,8,128]{2,1,0:T(8,128)S(1)}, u32[]{:S(2)}, u32[]{:S(2)}) %all-to-all-start.4) | async-done | bytes 32800 | tf_op jit(solution)/shard_map/all_to_all | solution.py:616
  109.9 0.0 copy-done
  109.9 0.7 shard_map.125
  110.6 1.3 %collective-permute-start.6 = (f32[192,128]{1,0:T(8,128)S(1)}, f32[192,128]{1,0:T(8,128)S(1)}, u32[]{:S(2)}, u32[]{:S(2)}) collective-permute-start(f32[192,128]{1,0:T(8,128)S(1)} %get-tuple-element.57), channel_id=1, source_target_pairs={{16,0},{32,16},{48,32},{64,48},{80,64},{96,80},{112,96},{128,112},... | collective-permute-start | bytes 294920 | tf_op jit(solution)/shard_map/ppermute | solution.py:25
  111.9 4.5 %collective-permute-start.7 = (f32[192,128]{1,0:T(8,128)S(1)}, f32[192,128]{1,0:T(8,128)S(1)}, u32[]{:S(2)}, u32[]{:S(2)}) collective-permute-start(f32[192,128]{1,0:T(8,128)S(1)} %get-tuple-element.58), channel_id=1, source_target_pairs={{1,0},{2,1},{3,2},{4,3},{5,4},{6,5},{7,6},{8,7},{9,8},{10,9},{11,1... | collective-permute-start | bytes 294920 | tf_op jit(solution)/shard_map/ppermute | solution.py:25
  116.4 0.9 shard_map.124
  117.4 0.0 collective-permute-done.6.below
  117.4 1.8 %collective-permute-done.7.right = f32[192,128]{1,0:T(8,128)S(1)} collective-permute-done((f32[192,128]{1,0:T(8,128)S(1)}, f32[192,128]{1,0:T(8,128)S(1)}, u32[]{:S(2)}, u32[]{:S(2)}) %collective-permute-start.7) | collective-permute-done | bytes 98336 | tf_op jit(solution)/shard_map/ppermute | solution.py:25
  119.2 0.7 shard_map.126
  (1 shorter events, 0.0 us)
Async XLA Ops:
  1.6 10.8 %collective-permute-start.1 = (f32[192,128]{1,0:T(8,128)S(1)}, f32[192,128]{1,0:T(8,128)S(1)}, u32[]{:S(2)}, u32[]{:S(2)}) collective-permute-start(f32[192,128]{1,0:T(8,128)S(1)} %get-tuple-element.60.gap_right), channel_id=1, source_target_pairs={{0,1},{1,2},{2,3},{3,4},{4,5},{5,6},{6,7},{7,8},{8,9},{9,10},{10,1... | collective-permute-start | bytes 294920 | tf_op jit(solution)/shard_map/ppermute | solution.py:25
  6.2 6.2 %collective-permute-start = (f32[192,128]{1,0:T(8,128)S(1)}, f32[192,128]{1,0:T(8,128)S(1)}, u32[]{:S(2)}, u32[]{:S(2)}) collective-permute-start(f32[192,128]{1,0:T(8,128)S(1)} %get-tuple-element.61.gap_down), channel_id=1, source_target_pairs={{0,16},{16,32},{32,48},{48,64},{64,80},{80,96},{96,112},{112,128},... | collective-permute-start | bytes 294920 | tf_op jit(solution)/shard_map/ppermute | solution.py:25
  9.3 3.1 %copy-start.1 = (f32[1,1,16,384]{3,2,1,0:T(8,128)S(1)}, f32[1,1,16,384]{3,2,1,0:T(8,128)}, u32[]{:S(2)}) copy-start(f32[1,1,16,384]{3,2,1,0:T(8,128)} %param.15) | copy-start | bytes 73732
  14.2 10.8 %collective-permute-start.2 = (f32[240,128]{1,0:T(8,128)S(1)}, f32[240,128]{1,0:T(8,128)S(1)}, u32[]{:S(2)}, u32[]{:S(2)}) collective-permute-start(f32[240,128]{1,0:T(8,128)S(1)} %get-tuple-element.36), channel_id=1, source_target_pairs={{0,16},{32,48},{64,80},{96,112},{128,144},{160,176},{192,208},{224... | collective-permute-start | bytes 368648 | tf_op jit(solution)/shard_map/ppermute | solution.py:31
  17.3 7.6 %collective-permute-start.3 = (f32[240,128]{1,0:T(8,128)S(1)}, f32[240,128]{1,0:T(8,128)S(1)}, u32[]{:S(2)}, u32[]{:S(2)}) collective-permute-start(f32[240,128]{1,0:T(8,128)S(1)} %get-tuple-element.37), channel_id=1, source_target_pairs={{16,32},{48,64},{80,96},{112,128},{144,160},{176,192},{208,224},{2... | collective-permute-start | bytes 368648 | tf_op jit(solution)/shard_map/ppermute | solution.py:31
  18.0 7.0 %collective-permute-start.4 = (f32[240,128]{1,0:T(8,128)S(1)}, f32[240,128]{1,0:T(8,128)S(1)}, u32[]{:S(2)}, u32[]{:S(2)}) collective-permute-start(f32[240,128]{1,0:T(8,128)S(1)} %get-tuple-element.38), channel_id=1, source_target_pairs={{0,1},{2,3},{4,5},{6,7},{8,9},{10,11},{12,13},{14,15},{1,0},{3,2},... | collective-permute-start | bytes 368648 | tf_op jit(solution)/shard_map/ppermute | solution.py:31
  21.9 6.2 %collective-permute-start.5 = (f32[240,128]{1,0:T(8,128)S(1)}, f32[240,128]{1,0:T(8,128)S(1)}, u32[]{:S(2)}, u32[]{:S(2)}) collective-permute-start(f32[240,128]{1,0:T(8,128)S(1)} %get-tuple-element.39), channel_id=1, source_target_pairs={{1,2},{3,4},{5,6},{7,8},{9,10},{11,12},{13,14},{2,1},{4,3},{6,5},{... | collective-permute-start | bytes 368648 | tf_op jit(solution)/shard_map/ppermute | solution.py:31
  53.5 19.5 %all-to-all-start.1 = ((f32[16,16,128]{2,1,0:T(8,128)}), f32[16,16,128]{2,1,0:T(8,128)S(1)}, u32[]{:S(2)}, u32[]{:S(2)}) async-start(f32[16,16,128]{2,1,0:T(8,128)} %bitcast.12), calls=%async_computation.1 | async-start | bytes 262144 | tf_op jit(solution)/shard_map/all_to_all | solution.py:580
  64.1 4.5 %copy-start.2 = (f32[1,1,16,384]{3,2,1,0:T(8,128)S(1)}, f32[1,1,16,384]{3,2,1,0:T(8,128)}, u32[]{:S(2)}) copy-start(f32[1,1,16,384]{3,2,1,0:T(8,128)} %param.16) | copy-start | bytes 73732
  99.7 10.2 %all-to-all-start.4 = ((f32[8,8,128]{2,1,0:T(8,128)}), f32[8,8,128]{2,1,0:T(8,128)S(1)}, u32[]{:S(2)}, u32[]{:S(2)}) async-start(f32[8,8,128]{2,1,0:T(8,128)} %bitcast.20), calls=%async_computation.4 | async-start | bytes 65536 | tf_op jit(solution)/shard_map/all_to_all | solution.py:616
  103.2 6.7 %copy-start = (bf16[768,768]{1,0:T(8,128)(2,1)S(1)}, bf16[768,768]{1,0:T(8,128)(2,1)}, u32[]{:S(2)}) copy-start(bf16[768,768]{1,0:T(8,128)(2,1)} %get-tuple-element.55.pick_flex) | copy-start | bytes 3538948
  110.6 6.7 %collective-permute-start.6 = (f32[192,128]{1,0:T(8,128)S(1)}, f32[192,128]{1,0:T(8,128)S(1)}, u32[]{:S(2)}, u32[]{:S(2)}) collective-permute-start(f32[192,128]{1,0:T(8,128)S(1)} %get-tuple-element.57), channel_id=1, source_target_pairs={{16,0},{32,16},{48,32},{64,48},{80,64},{96,80},{112,96},{128,112},... | collective-permute-start | bytes 294920 | tf_op jit(solution)/shard_map/ppermute | solution.py:25
  111.9 7.3 %collective-permute-start.7 = (f32[192,128]{1,0:T(8,128)S(1)}, f32[192,128]{1,0:T(8,128)S(1)}, u32[]{:S(2)}, u32[]{:S(2)}) collective-permute-start(f32[192,128]{1,0:T(8,128)S(1)} %get-tuple-element.58), channel_id=1, source_target_pairs={{1,0},{2,1},{3,2},{4,3},{5,4},{6,5},{7,6},{8,7},{9,8},{10,9},{11,1... | collective-permute-start | bytes 294920 | tf_op jit(solution)/shard_map/ppermute | solution.py:25

commit v7 on v6

--- a/solution.py
+++ b/solution.py
@@ -175,6 +175,10 @@
         sign_row = jnp.where(inside, SIGNS[f], sign_row)
     copies[2].wait()
     weights = 1.0 / mult[...].astype(F32)
+    buffer[...] = jnp.zeros_like(buffer)
+    buffer[0:1, :] = slot_row
+    buffer[1:2, :] = sign_row
+    pick_value = picking(jnp.transpose(buffer[...]))
     place_value = placing(slot_row, sign_row)
     place[...] = place_value
     copies[3].wait()
@@ -190,7 +194,6 @@
     buffer[2:3, :] = weights
     buffer[3:4, :] = jnp.abs(rows[3:4])
     link_rows[...] = buffer[...]
-    pick_value = picking(jnp.transpose(buffer[...]))
     copies[4].wait()
     pick_schur[...] = dot(pick_value, schur[...]).astype(BF16)
 
@@ -246,23 +249,15 @@
     )
 
 
-def flex_kernel(
-    link_rows, place, flex_hbm, pick_flex_hbm, link_flex_hbm,
-    flex, pick_flex, link_flex, arrived,
-):
+def flex_kernel(link_rows, flex_hbm, pick_flex_hbm, flex, pick_flex, arrived):
     load = pltpu.make_async_copy(flex_hbm, flex, arrived.at[0])
     load.start()
     pick_value = picking(jnp.transpose(link_rows[...]))
     load.wait()
-    rows = dot(pick_value, flex[...]).astype(BF16)
-    pick_flex[...] = rows
+    pick_flex[...] = dot(pick_value, flex[...]).astype(BF16)
     store = pltpu.make_async_copy(pick_flex, pick_flex_hbm, arrived.at[1])
     store.start()
-    link_flex[...] = dot(rows, place[...]).astype(BF16)
-    store_link = pltpu.make_async_copy(link_flex, link_flex_hbm, arrived.at[2])
-    store_link.start()
     store.wait()
-    store_link.wait()
 
 
 def coarse_in_kernel(
@@ -284,11 +279,11 @@
 
 def tables_kernel(
     odd_x, odd_y, first_x, second_x, first_y, second_y,
-    mode_rows, link_rows, saved, images, residual, precond, link_flex_hbm,
+    mode_rows, link_rows, place, saved, images, residual, precond, pick_flex_hbm,
     mode_six, search_rows, base, mode_forms,
-    link_flex, arrived,
+    pick_flex, arrived,
 ):
-    load = pltpu.make_async_copy(link_flex_hbm, link_flex, arrived.at[0])
+    load = pltpu.make_async_copy(pick_flex_hbm, pick_flex, arrived.at[0])
     load.start()
     total = mode_rows.shape[1]
     width = total // 4
@@ -326,13 +321,16 @@
         jnp.where(lanes >= 3 * width, at_lanes(image, 2 * width), 0.0),
     )
     load.wait()
-    flexed = select_lanes(jnp.concatenate([search, modes], axis=0), link_flex[...])
+    flexed = select_lanes(jnp.concatenate([search, modes], axis=0), pick_flex[...])
+    flexed = select_lanes(flexed, place[...])
     forms = jnp.concatenate([image, flexed], axis=0)
     full = precond[...]
     base[0:48, :] = dot_exact(forms, full)
     mode_forms[...] = six_left(dot_exact(forms, modes_tiled))
     high, mid, _ = split3(full)
-    applied = dot(link_flex[...], jnp.concatenate([high, mid], axis=1))
+    slots = dot(place[...], jnp.concatenate([high, mid], axis=1))
+    high, mid, _ = split3(slots[:, :128] + slots[:, 128:])
+    applied = dot(pick_flex[...], jnp.concatenate([high, mid], axis=1))
     square = jnp.sum(full * (applied[:, :128] + applied[:, 128:]), axis=0, keepdims=True)
     products = dot_exact(dot_exact_nt(flexed[0:16], search), tile_matrix())
     group = lax.broadcasted_iota(jnp.int32, (16, 128), 1) // 16
@@ -566,21 +564,24 @@
         flops=cube // 16,
     )
     gathered = lax.all_to_all(coarse_in, GX, 0, 0, tiled=True)
-    pick_flex, link_flex = call(
+    (pick_flex,) = call(
         flex_kernel,
-        (link_rows, place, flex),
-        ((big, BF16), (big, BF16)),
+        (link_rows, flex),
+        ((big, BF16),),
         remote=1,
-        scratch=((big, BF16), (big, BF16), (big, BF16)),
-        copies=3,
-        hbm_out=(0, 1),
-        flops=2 * cube,
+        scratch=((big, BF16), (big, BF16)),
+        copies=2,
+        hbm_out=(0,),
+        flops=cube,
     )
     (parts,) = call(coarse_kernel, (gathered,), (((16 * columns, cases), F32),), flops=cube // 8)
     parts = lax.all_to_all(parts, GY, 0, 0, tiled=True)
     mode_six, search_rows, base, mode_forms = call(
         tables_kernel,
-        (odd_x, odd_y, *messages, mode_rows, link_rows, saved, images, residual, precond, link_flex),
+        (
+            odd_x, odd_y, *messages, mode_rows, link_rows, place, saved, images, residual, precond,
+            pick_flex,
+        ),
         (((total, 128), BF16), ((16, total), F32), ((56, cases), F32), ((48, 128), BF16)),
         scalars=2,
         remote=1,

time: 121 us -> 120 us (level)
  waiting for transfers between devices: 10.9 us -> 9.65 us
    ppermute x4, waiting for transfers between devices: 3.11 us -> 1.84 us  [swapped(): lax.ppermute(value, axis, pairs + [(high, low) for low, high in pairs])]
where the time goes in v7:
time: 120 us; the launch traced here: 119 us
  blocking collectives  49.6 us (41%)
  starting transfers between devices  37.8 us (31%)
  Pallas kernels  20.4 us (17%)
  waiting for transfers between devices  9.65 us (8%)
    all_to_all x2, blocking collectives, step(): partial = lax.all_to_all(partial, axis, 0, 0, tiled=True)  25.9 us
    all_to_all x1, blocking collectives, step(): gathered = lax.all_to_all(coarse_in, GX, 0, 0, tiled=True)  23.7 us
    pallas_call x14, Pallas kernels, call(): pl.pallas_call(kernel, out_shape=outputs, in_specs=[SMEM] * scalars + [VM...  20.4 us
    ppermute x4, starting transfers between devices, shifted(): lax.ppermute(value, axis, [(source, source + steps) for source in range(i...  13.8 us
    all_to_all x1, starting transfers between devices, step(): parts = lax.all_to_all(parts, GY, 0, 0, tiled=True)  11.2 us
    ppermute x4, starting transfers between devices, swapped(): lax.ppermute(value, axis, pairs + [(high, low) for low, high in pairs])  9.3 us
    all_to_all x1, waiting for transfers between devices, step(): sums = lax.all_to_all(partial, GY[0], 0, 0, tiled=True)  4.21 us
    all_to_all x1, starting transfers between devices, step(): sums = lax.all_to_all(partial, GY[0], 0, 0, tiled=True)  3.52 us
  transfers between devices with their start and end apart: 10, of which 4 were waited for; matrix products, arithmetic and copies ran while one was open for 0% of the time, Pallas kernels for 12%

profile of v7, /device:TPU:1, one launch (start us, length us, event | category | flops | bytes accessed | tf_op | source)
XLA Modules:
  0.0 119.4 jit_solution(2612988081412478410)
XLA Ops:
  0.6 1.0 slice_bitcast_fusion
  1.6 3.9 %collective-permute-start = (f32[192,128]{1,0:T(8,128)S(1)}, f32[192,128]{1,0:T(8,128)S(1)}, u32[]{:S(2)}, u32[]{:S(2)}) collective-permute-start(f32[192,128]{1,0:T(8,128)S(1)} %get-tuple-element.57.gap_down), channel_id=1, source_target_pairs={{0,16},{16,32},{32,48},{48,64},{64,80},{80,96},{96,112},{112,128},... | collective-permute-start | bytes 294920 | tf_op jit(solution)/shard_map/ppermute | solution.py:25
  5.5 4.0 %collective-permute-start.1 = (f32[192,128]{1,0:T(8,128)S(1)}, f32[192,128]{1,0:T(8,128)S(1)}, u32[]{:S(2)}, u32[]{:S(2)}) collective-permute-start(f32[192,128]{1,0:T(8,128)S(1)} %get-tuple-element.56.gap_right), channel_id=1, source_target_pairs={{0,1},{1,2},{2,3},{3,4},{4,5},{5,6},{6,7},{7,8},{8,9},{9,10},{10,1... | collective-permute-start | bytes 294920 | tf_op jit(solution)/shard_map/ppermute | solution.py:25
  9.6 0.0 copy-start.1
  9.6 3.0 %shard_map.113 = (bf16[768,768]{1,0:T(8,128)(2,1)S(1)}, bf16[768,768]{1,0:T(8,128)(2,1)S(1)}, f32[8,768]{1,0:T(8,128)S(1)}, f32[8,768]{1,0:T(8,128)S(1)}) custom-call(s32[1,4]{1,0:T(1,128)} %bitcast.45, s32[4,192]{1,0:T(4,128)} %bitcast.43, s32[1,768]{1,0:T(1,128)} %bitcast.44, f32[3,1,768]{2,1,0:T(1,128)} %bitcast.42, bf16[768,768]{1,0:T(8,128)(2,1)} %bitcast.39), custom_call_target="tpu_custom_call" | custom-call | flops 905969664 | tf_op jit(solution)/shard_map/pallas_call | solution.py:488
  12.7 0.0 collective-permute-done.above
  12.7 0.0 collective-permute-done.1.left
  12.7 0.0 copy-done.1
  12.7 1.7 %shard_map.114 = (f32[240,128]{1,0:T(8,128)S(1)}, f32[240,128]{1,0:T(8,128)S(1)}, f32[240,128]{1,0:T(8,128)S(1)}, f32[240,128]{1,0:T(8,128)S(1)}, f32[768,128]{1,0:T(8,128)S(1)}, /*index=5*/f32[384,128]{1,0:T(8,128)S(1)}) custom-call(s32[1]{0:T(128)} %bitcast.odd_x, s32[1]{0:T(128)} %bitcast.1.odd_y, f32[192,128]{1,0:T(8,128)S(1)} %get-tuple-element.57.gap_down, ...), custom_call_target="tpu_custom_call" | custom-call | flops 452984832 | tf_op jit(solution)/shard_map/pallas_call | solution.py:488
  14.4 3.1 %collective-permute-start.2 = (f32[240,128]{1,0:T(8,128)S(1)}, f32[240,128]{1,0:T(8,128)S(1)}, u32[]{:S(2)}, u32[]{:S(2)}) collective-permute-start(f32[240,128]{1,0:T(8,128)S(1)} %get-tuple-element.34), channel_id=1, source_target_pairs={{0,16},{32,48},{64,80},{96,112},{128,144},{160,176},{192,208},{224... | collective-permute-start | bytes 368648 | tf_op jit(solution)/shard_map/ppermute | solution.py:31
  17.5 0.7 collective-permute-start.3
  18.2 2.3 %collective-permute-start.4 = (f32[240,128]{1,0:T(8,128)S(1)}, f32[240,128]{1,0:T(8,128)S(1)}, u32[]{:S(2)}, u32[]{:S(2)}) collective-permute-start(f32[240,128]{1,0:T(8,128)S(1)} %get-tuple-element.36), channel_id=1, source_target_pairs={{0,1},{2,3},{4,5},{6,7},{8,9},{10,11},{12,13},{14,15},{1,0},{3,2},... | collective-permute-start | bytes 368648 | tf_op jit(solution)/shard_map/ppermute | solution.py:31
  20.6 3.2 %collective-permute-start.5 = (f32[240,128]{1,0:T(8,128)S(1)}, f32[240,128]{1,0:T(8,128)S(1)}, u32[]{:S(2)}, u32[]{:S(2)}) collective-permute-start(f32[240,128]{1,0:T(8,128)S(1)} %get-tuple-element.37), channel_id=1, source_target_pairs={{1,2},{3,4},{5,6},{7,8},{9,10},{11,12},{13,14},{2,1},{4,3},{6,5},{... | collective-permute-start | bytes 368648 | tf_op jit(solution)/shard_map/ppermute | solution.py:31
  23.7 1.1 shard_map.115.blocks
  24.9 0.0 collective-permute-done.2.first_x
  24.9 0.0 collective-permute-done.3.second_x
  24.9 0.0 collective-permute-done.4.first_y
  24.9 1.8 %collective-permute-done.5.second_y = f32[240,128]{1,0:T(8,128)S(1)} collective-permute-done((f32[240,128]{1,0:T(8,128)S(1)}, f32[240,128]{1,0:T(8,128)S(1)}, u32[]{:S(2)}, u32[]{:S(2)}) %collective-permute-start.5) | collective-permute-done | bytes 122912 | tf_op jit(solution)/shard_map/ppermute | solution.py:31
  26.8 0.3 shard_map.116
  27.1 23.7 %all_to_all.55 = f32[32,8,128]{2,1,0:T(8,128)S(1)} all-to-all(f32[32,8,128]{2,1,0:T(8,128)S(1)} %bitcast.32), channel_id=1, replica_groups=mesh['gx_0'=8,'gx_1'=4,'gy_0'=8,'gy_1'=2] {'gx_0','gx_1'}, dimensions={0} | all-to-all | bytes 262144 | tf_op jit(solution)/shard_map/all_to_all | solution.py:566
  50.8 1.5 %shard_map.117 = f32[256,128]{1,0:T(8,128)} custom-call(f32[256,128]{1,0:T(8,128)S(1)} %bitcast.33), custom_call_target="tpu_custom_call" | custom-call | flops 113246208 | tf_op jit(solution)/shard_map/pallas_call | solution.py:488
  52.3 11.2 %all-to-all-start.1 = ((f32[16,16,128]{2,1,0:T(8,128)}), f32[16,16,128]{2,1,0:T(8,128)S(1)}, u32[]{:S(2)}, u32[]{:S(2)}) async-start(f32[16,16,128]{2,1,0:T(8,128)} %bitcast.12), calls=%async_computation.1 | async-start | bytes 262144 | tf_op jit(solution)/shard_map/all_to_all | solution.py:578
  63.6 0.0 copy-start.2
  63.6 3.4 %shard_map.118.pick_flex_hbm.pick_flex = bf16[768,768]{1,0:T(8,128)(2,1)} custom-call(f32[8,768]{1,0:T(8,128)S(1)} %get-tuple-element.31.link_rows, bf16[768,768]{1,0:T(8,128)(2,1)} %bitcast.40), custom_call_target="tpu_custom_call" | custom-call | flops 905969664 | tf_op jit(solution)/shard_map/pallas_call | solution.py:488
  67.0 0.0 copy-done.2
  67.0 3.7 %shard_map.119 = (bf16[768,128]{1,0:T(8,128)(2,1)S(1)}, f32[16,768]{1,0:T(8,128)S(1)}, f32[56,128]{1,0:T(8,128)S(1)}, bf16[48,128]{1,0:T(8,128)(2,1)S(1)}) custom-call(s32[1]{0:T(128)} %bitcast.odd_x, s32[1]{0:T(128)} %bitcast.1.odd_y, f32[240,128]{1,0:T(8,128)S(1)} %collective-permute-done.2.first_x, f32[240,128]{1,0:T(8,128)S(1)} %collective-permute-done.3.second_x, ...), custom_call_target="tpu_custom_call" | custom-call | flops 905969664 | tf_op jit(solution)/shard_map/pallas_call | solution.py:488
  70.7 1.7 %all-to-all-done.1 = f32[16,16,128]{2,1,0:T(8,128)S(1)} async-done(((f32[16,16,128]{2,1,0:T(8,128)}), f32[16,16,128]{2,1,0:T(8,128)S(1)}, u32[]{:S(2)}, u32[]{:S(2)}) %all-to-all-start.1) | async-done | bytes 131104 | tf_op jit(solution)/shard_map/all_to_all | solution.py:578
  72.5 0.2 shard_map.120
  72.6 13.1 %all_to_all.56 = f32[16,8,128]{2,1,0:T(8,128)S(1)} all-to-all(f32[16,8,128]{2,1,0:T(8,128)S(1)} %bitcast.36), channel_id=1, replica_groups=mesh['gx_0'=8,'gx_1'=4,'gy_0'=8,'gy_1'=2] {'gy_0','gy_1'}, dimensions={0} | all-to-all | bytes 131072 | tf_op jit(solution)/shard_map/all_to_all | solution.py:610
  85.7 12.8 %all_to_all.57 = f32[32,8,128]{2,1,0:T(8,128)S(1)} all-to-all(f32[32,8,128]{2,1,0:T(8,128)S(1)} %bitcast.28), channel_id=1, replica_groups=mesh['gx_0'=8,'gx_1'=4,'gy_0'=8,'gy_1'=2] {'gx_0','gx_1'}, dimensions={0} | all-to-all | bytes 262144 | tf_op jit(solution)/shard_map/all_to_all | solution.py:610
  98.5 0.6 shard_map.122
  99.2 3.5 %all-to-all-start.4 = ((f32[8,8,128]{2,1,0:T(8,128)}), f32[8,8,128]{2,1,0:T(8,128)S(1)}, u32[]{:S(2)}, u32[]{:S(2)}) async-start(f32[8,8,128]{2,1,0:T(8,128)} %bitcast.20), calls=%async_computation.4 | async-start | bytes 65536 | tf_op jit(solution)/shard_map/all_to_all | solution.py:617
  102.7 0.0 copy-start
  102.7 2.5 %shard_map.123 = (f32[768,128]{1,0:T(8,128)S(1)}, bf16[768,128]{1,0:T(8,128)(2,1)S(1)}, f32[384,128]{1,0:T(8,128)S(1)}, bf16[384,128]{1,0:T(8,128)(2,1)S(1)}) custom-call(f32[16,128]{1,0:T(8,128)S(1)} %get-tuple-element.44.amplitudes, f32[768,128]{1,0:T(8,128)S(1)} %get-tuple-element.40.precond, bf16[768,128]{1,0:T(8,128)(2,1)S(1)} %get-tuple-element.45.mode_six, ...), custom_call_target="tpu_custom_call" | custom-call | flops 905969664 | tf_op jit(solution)/shard_map/pallas_call | solution.py:488
  105.2 4.2 %all-to-all-done.4 = f32[8,8,128]{2,1,0:T(8,128)S(1)} async-done(((f32[8,8,128]{2,1,0:T(8,128)}), f32[8,8,128]{2,1,0:T(8,128)S(1)}, u32[]{:S(2)}, u32[]{:S(2)}) %all-to-all-start.4) | async-done | bytes 32800 | tf_op jit(solution)/shard_map/all_to_all | solution.py:617
  109.4 0.0 copy-done
  109.4 0.7 shard_map.125
  110.1 1.3 %collective-permute-start.6 = (f32[192,128]{1,0:T(8,128)S(1)}, f32[192,128]{1,0:T(8,128)S(1)}, u32[]{:S(2)}, u32[]{:S(2)}) collective-permute-start(f32[192,128]{1,0:T(8,128)S(1)} %get-tuple-element.53), channel_id=1, source_target_pairs={{16,0},{32,16},{48,32},{64,48},{80,64},{96,80},{112,96},{128,112},... | collective-permute-start | bytes 294920 | tf_op jit(solution)/shard_map/ppermute | solution.py:25
  111.4 4.5 %collective-permute-start.7 = (f32[192,128]{1,0:T(8,128)S(1)}, f32[192,128]{1,0:T(8,128)S(1)}, u32[]{:S(2)}, u32[]{:S(2)}) collective-permute-start(f32[192,128]{1,0:T(8,128)S(1)} %get-tuple-element.54), channel_id=1, source_target_pairs={{1,0},{2,1},{3,2},{4,3},{5,4},{6,5},{7,6},{8,7},{9,8},{10,9},{11,1... | collective-permute-start | bytes 294920 | tf_op jit(solution)/shard_map/ppermute | solution.py:25
  115.9 0.9 shard_map.124
  116.8 0.0 collective-permute-done.6.below
  116.8 1.8 %collective-permute-done.7.right = f32[192,128]{1,0:T(8,128)S(1)} collective-permute-done((f32[192,128]{1,0:T(8,128)S(1)}, f32[192,128]{1,0:T(8,128)S(1)}, u32[]{:S(2)}, u32[]{:S(2)}) %collective-permute-start.7) | collective-permute-done | bytes 98336 | tf_op jit(solution)/shard_map/ppermute | solution.py:25
  118.7 0.7 shard_map.126
  (1 shorter events, 0.0 us)
Async XLA Ops:
  1.6 11.1 %collective-permute-start = (f32[192,128]{1,0:T(8,128)S(1)}, f32[192,128]{1,0:T(8,128)S(1)}, u32[]{:S(2)}, u32[]{:S(2)}) collective-permute-start(f32[192,128]{1,0:T(8,128)S(1)} %get-tuple-element.57.gap_down), channel_id=1, source_target_pairs={{0,16},{16,32},{32,48},{48,64},{64,80},{80,96},{96,112},{112,128},... | collective-permute-start | bytes 294920 | tf_op jit(solution)/shard_map/ppermute | solution.py:25
  5.5 7.1 %collective-permute-start.1 = (f32[192,128]{1,0:T(8,128)S(1)}, f32[192,128]{1,0:T(8,128)S(1)}, u32[]{:S(2)}, u32[]{:S(2)}) collective-permute-start(f32[192,128]{1,0:T(8,128)S(1)} %get-tuple-element.56.gap_right), channel_id=1, source_target_pairs={{0,1},{1,2},{2,3},{3,4},{4,5},{5,6},{6,7},{7,8},{8,9},{9,10},{10,1... | collective-permute-start | bytes 294920 | tf_op jit(solution)/shard_map/ppermute | solution.py:25
  9.6 3.1 %copy-start.1 = (f32[1,1,16,384]{3,2,1,0:T(8,128)S(1)}, f32[1,1,16,384]{3,2,1,0:T(8,128)}, u32[]{:S(2)}) copy-start(f32[1,1,16,384]{3,2,1,0:T(8,128)} %param.15) | copy-start | bytes 73732
  14.4 10.5 %collective-permute-start.2 = (f32[240,128]{1,0:T(8,128)S(1)}, f32[240,128]{1,0:T(8,128)S(1)}, u32[]{:S(2)}, u32[]{:S(2)}) collective-permute-start(f32[240,128]{1,0:T(8,128)S(1)} %get-tuple-element.34), channel_id=1, source_target_pairs={{0,16},{32,48},{64,80},{96,112},{128,144},{160,176},{192,208},{224... | collective-permute-start | bytes 368648 | tf_op jit(solution)/shard_map/ppermute | solution.py:31
  17.5 7.4 %collective-permute-start.3 = (f32[240,128]{1,0:T(8,128)S(1)}, f32[240,128]{1,0:T(8,128)S(1)}, u32[]{:S(2)}, u32[]{:S(2)}) collective-permute-start(f32[240,128]{1,0:T(8,128)S(1)} %get-tuple-element.35), channel_id=1, source_target_pairs={{16,32},{48,64},{80,96},{112,128},{144,160},{176,192},{208,224},{2... | collective-permute-start | bytes 368648 | tf_op jit(solution)/shard_map/ppermute | solution.py:31
  18.2 6.7 %collective-permute-start.4 = (f32[240,128]{1,0:T(8,128)S(1)}, f32[240,128]{1,0:T(8,128)S(1)}, u32[]{:S(2)}, u32[]{:S(2)}) collective-permute-start(f32[240,128]{1,0:T(8,128)S(1)} %get-tuple-element.36), channel_id=1, source_target_pairs={{0,1},{2,3},{4,5},{6,7},{8,9},{10,11},{12,13},{14,15},{1,0},{3,2},... | collective-permute-start | bytes 368648 | tf_op jit(solution)/shard_map/ppermute | solution.py:31
  20.6 6.2 %collective-permute-start.5 = (f32[240,128]{1,0:T(8,128)S(1)}, f32[240,128]{1,0:T(8,128)S(1)}, u32[]{:S(2)}, u32[]{:S(2)}) collective-permute-start(f32[240,128]{1,0:T(8,128)S(1)} %get-tuple-element.37), channel_id=1, source_target_pairs={{1,2},{3,4},{5,6},{7,8},{9,10},{11,12},{13,14},{2,1},{4,3},{6,5},{... | collective-permute-start | bytes 368648 | tf_op jit(solution)/shard_map/ppermute | solution.py:31
  52.3 20.1 %all-to-all-start.1 = ((f32[16,16,128]{2,1,0:T(8,128)}), f32[16,16,128]{2,1,0:T(8,128)S(1)}, u32[]{:S(2)}, u32[]{:S(2)}) async-start(f32[16,16,128]{2,1,0:T(8,128)} %bitcast.12), calls=%async_computation.1 | async-start | bytes 262144 | tf_op jit(solution)/shard_map/all_to_all | solution.py:578
  63.6 3.4 %copy-start.2 = (f32[1,1,16,384]{3,2,1,0:T(8,128)S(1)}, f32[1,1,16,384]{3,2,1,0:T(8,128)}, u32[]{:S(2)}) copy-start(f32[1,1,16,384]{3,2,1,0:T(8,128)} %param.16) | copy-start | bytes 73732
  99.2 10.2 %all-to-all-start.4 = ((f32[8,8,128]{2,1,0:T(8,128)}), f32[8,8,128]{2,1,0:T(8,128)S(1)}, u32[]{:S(2)}, u32[]{:S(2)}) async-start(f32[8,8,128]{2,1,0:T(8,128)} %bitcast.20), calls=%async_computation.4 | async-start | bytes 65536 | tf_op jit(solution)/shard_map/all_to_all | solution.py:617
  102.7 6.7 %copy-start = (bf16[768,768]{1,0:T(8,128)(2,1)S(1)}, bf16[768,768]{1,0:T(8,128)(2,1)}, u32[]{:S(2)}) copy-start(bf16[768,768]{1,0:T(8,128)(2,1)} %shard_map.118.pick_flex_hbm.pick_flex) | copy-start | bytes 3538948
  110.1 6.7 %collective-permute-start.6 = (f32[192,128]{1,0:T(8,128)S(1)}, f32[192,128]{1,0:T(8,128)S(1)}, u32[]{:S(2)}, u32[]{:S(2)}) collective-permute-start(f32[192,128]{1,0:T(8,128)S(1)} %get-tuple-element.53), channel_id=1, source_target_pairs={{16,0},{32,16},{48,32},{64,48},{80,64},{96,80},{112,96},{128,112},... | collective-permute-start | bytes 294920 | tf_op jit(solution)/shard_map/ppermute | solution.py:25
  111.4 7.3 %collective-permute-start.7 = (f32[192,128]{1,0:T(8,128)S(1)}, f32[192,128]{1,0:T(8,128)S(1)}, u32[]{:S(2)}, u32[]{:S(2)}) collective-permute-start(f32[192,128]{1,0:T(8,128)S(1)} %get-tuple-element.54), channel_id=1, source_target_pairs={{1,0},{2,1},{3,2},{4,3},{5,4},{6,5},{7,6},{8,7},{9,8},{10,9},{11,1... | collective-permute-start | bytes 294920 | tf_op jit(solution)/shard_map/ppermute | solution.py:25
